TPU v7x, 1024 devices: a whole 8x8x8 slice. The times are simulated.
1024 devices in a mesh: gx: 8 (over y_lo, core), gy: 16 (over y_hi, x), gz: 8 (over z).
Axes of the slice: x: 8, y: 8 (y_hi: 2, y_lo: 4; y = y_hi * 4 + y_lo), z: 8, core: 2. Of those that a mesh axis runs over, the one named last changes fastest.
Arguments:
- sources: float32 [1, 128, 256, 1024], P(None, 'gx', 'gy', 'gz'), may hold values from -6 to 6
- stiffness: float32 [128, 256, 1024], P('gx', 'gy', 'gz'), may hold values from 0.5 to 2
- coarse_inverse: float32 [8192, 8192], P(('gx', 'gy', 'gz')), may hold values from -1.25 to 1.25
Outputs:
- pressure: float32 [1, 128, 256, 1024], P(None, 'gx', 'gy', 'gz')
All inputs are finite; a program needn't handle non-finite values.
Results may differ from a plain program's by a relative error of at most 0.0001.
Values sent between devices are 32-bit elements; how exact they have to be, the bound alone decides.
A program may use at most 32 MiB of HBM per device.

v0:
```python
import jax
import jax.numpy as jnp
from jax import lax
from jax.sharding import PartitionSpec as P

damping = 0.8


def extended(cells, sides, width):
    for axis, dim in sides:
        count = lax.axis_size(axis)
        ends = count - 1
        head = lax.slice_in_dim(cells, 0, width, axis=dim)
        tail = lax.slice_in_dim(cells, cells.shape[dim] - width, cells.shape[dim], axis=dim)
        cells = jnp.concatenate(
            [
                lax.ppermute(tail, axis, [(i, (i + 1) % count) for i in range(ends)]),
                cells,
                lax.ppermute(head, axis, [((i + 1) % count, i) for i in range(ends)]),
            ],
            axis=dim,
        )
    return cells


def with_halo(value, sides, width):
    edges = {}
    for axis, dim in sides:
        devices, length = (lax.axis_size(axis), value.shape[dim])
        up = [(i, (i + 1) % devices) for i in range(devices - 1)]
        last = lax.slice_in_dim(value, length - width, length, axis=dim)
        leading = lax.slice_in_dim(value, 0, width, axis=dim)
        edges[dim] = (
            lax.ppermute(last, axis, up),
            lax.ppermute(leading, axis, [(b, a) for a, b in up]),
        )
    done = []
    for _, dim in sides:
        low, high = edges[dim]
        around = [(width, width) if d in done else (0, 0) for d in range(value.ndim)]
        value = jnp.concatenate([jnp.pad(low, around), value, jnp.pad(high, around)], axis=dim)
        done.append(dim)
    return value


def loop_sum(padded):
    total = padded[:, 2:, 1:-1, 1:-1] + padded[:, :-2, 1:-1, 1:-1]
    total = total + padded[:, 1:-1, 2:, 1:-1] + padded[:, 1:-1, :-2, 1:-1]
    total = total + padded[:, 1:-1, 1:-1, 2:] + padded[:, 1:-1, 1:-1, :-2]
    return total


def inner_part(values):
    return values[:, 1:-1, 1:-1, 1:-1]


def pre_smooth(source, weights):
    count = source.shape[0]
    stacked = jnp.concatenate([source, weights], axis=0)
    wide = extended(stacked, (("gx", 1), ("gy", 2), ("gz", 3)), 2)
    wide_source = wide[:count]
    wide_weights = wide[count:]
    safe_weights = jnp.where(wide_weights > 0.0, wide_weights, 1.0)
    first = damping * wide_source / (6.0 * safe_weights * safe_weights)
    first_scaled = wide_weights * first
    mid_weights = inner_part(wide_weights)
    mid_safe = inner_part(safe_weights)
    applied = mid_weights * (6.0 * inner_part(first_scaled) - loop_sum(first_scaled))
    second = inner_part(first) + damping * (inner_part(wide_source) - applied) / (
        6.0 * mid_safe * mid_safe
    )
    second_scaled = mid_weights * second
    answer = inner_part(second)
    resid = source - weights * (6.0 * inner_part(second_scaled) - loop_sum(second_scaled))
    return (answer, resid)


def post_smooth(answer, source, weights):
    scaled = weights * answer
    wide = with_halo(scaled, (("gx", 1), ("gy", 2), ("gz", 3)), 1)
    applied = weights * (6.0 * scaled - loop_sum(wide))
    return answer + damping * (source - applied) / (6.0 * weights * weights)


def coarsen(values):
    leading = values.shape[0]
    size_x, size_y, size_z = (values.shape[1], values.shape[2], values.shape[3])
    blocks = values.reshape((leading, size_x // 2, 2, size_y // 2, 2, size_z // 2, 2))
    return jnp.mean(blocks, axis=(2, 4, 6))


def refine(values):
    return jnp.repeat(jnp.repeat(jnp.repeat(values, 2, axis=1), 2, axis=2), 2, axis=3)


def per_device(sources, stiffness, coarse_inverse):
    weight_list = [stiffness[None]]
    for level in range(3):
        weight_list.append(0.5 * coarsen(weight_list[-1]))
    source_list = []
    answer_list = []
    current = sources
    for level in range(4):
        source_list.append(current)
        answer, resid = pre_smooth(current, weight_list[level])
        answer_list.append(answer)
        current = coarsen(resid)
    count = current.shape[0]
    flat_source = current.reshape((count, -1))
    solved = lax.dot_general(
        lax.all_gather(flat_source, ("gx", "gy", "gz"), axis=1, tiled=True),
        coarse_inverse,
        (((1,), (1,)), ((), ())),
        precision=lax.Precision.HIGHEST,
        preferred_element_type=jnp.float32,
    )
    correction = solved.reshape(current.shape)
    for level in range(3, -1, -1):
        correction = post_smooth(
            answer_list[level] + refine(correction), source_list[level], weight_list[level]
        )
    return correction


def solution(mesh):
    in_specs = (P(None, "gx", "gy", "gz"), P("gx", "gy", "gz"), P(("gx", "gy", "gz"), None))
    out_specs = P(None, "gx", "gy", "gz")
    return jax.shard_map(
        per_device, mesh=mesh, in_specs=in_specs, out_specs=out_specs, check_vma=False
    )
```

profile of v0, /device:TPU:14, one launch (start us, length us, event | category | flops | bytes accessed | tf_op | source)
XLA Modules:
  0.0 397.5 jit_solution(8532078544136235170)
XLA Ops:
  3.9 3.3 collective-permute-done.1
  8.2 7.1 %collective-permute-start.2 = (f32[2,20,2,128]{3,2,1,0:T(2,128)S(1)}, f32[2,20,2,128]{3,2,1,0:T(2,128)S(1)}, u32[]{:S(2)}, u32[]{:S(2)}) collective-permute-start(f32[2,20,2,128]{3,2,1,0:T(2,128)S(1)} %get-tuple-element.27), channel_id=1, source_target_pairs={{0,8},{8,16},{16,24},{24,32},{32,40},{40,48},{48,56},{56,64},{64,7... | collective-permute-start | bytes 122888 | tf_op jit(solution)/shard_map/ppermute | solution.py:17
  15.3 10.5 %reshape_broadcast_in_dim.3 = f32[8,2,8,2,64,2]{5,4,3,2,1,0:T(8,128)} reshape(f32[16,16,128]{2,1,0:T(8,128)} %param.4) | data formatting | bytes 262144 | tf_op jit(solution)/shard_map/reshape;broadcast_in_dim | solution.py:88
  25.8 4.0 %reduce_sum.71 = f32[8,8,64]{2,1,0:T(8,128)S(1)} reduce(f32[8,2,8,2,64,2]{5,4,3,2,1,0:T(8,128)} %reshape_broadcast_in_dim.3, f32[]{:T(128)} %constant.15.clone.1), dimensions={1,3,5}, to_apply=%region_1.0 | reduce | flops 28672 | bytes 147460 | tf_op jit(solution)/shard_map/reduce_sum | solution.py:89
  32.2 10.1 %collective-permute-done.3 = f32[2,20,2,128]{3,2,1,0:T(2,128)S(1)} collective-permute-done((f32[2,20,2,128]{3,2,1,0:T(2,128)S(1)}, f32[2,20,2,128]{3,2,1,0:T(2,128)S(1)}, u32[]{:S(2)}, u32[]{:S(2)}) %collective-permute-start.3) | collective-permute-done | bytes 40992 | tf_op jit(solution)/shard_map/ppermute | solution.py:19
  42.8 5.2 %collective-permute-start.4 = (f32[2,20,20,2]{3,0,2,1:T(2,128)S(1)}, f32[2,20,20,2]{3,0,2,1:T(2,128)S(1)}, u32[]{:S(2)}, u32[]{:S(2)}) collective-permute-start(f32[2,20,20,2]{3,0,2,1:T(2,128)S(1)} %get-tuple-element.24), channel_id=1, source_target_pairs={{0,1},{1,2},{2,3},{3,4},{4,5},{5,6},{6,7},{8,9},{9,10},{10,11},{11... | collective-permute-start | bytes 19208 | tf_op jit(solution)/shard_map/ppermute | solution.py:17
  49.3 8.3 %collective-permute-done.4 = f32[2,20,20,2]{3,0,2,1:T(2,128)S(1)} collective-permute-done((f32[2,20,20,2]{3,0,2,1:T(2,128)S(1)}, f32[2,20,20,2]{3,0,2,1:T(2,128)S(1)}, u32[]{:S(2)}, u32[]{:S(2)}) %collective-permute-start.4) | collective-permute-done | bytes 6432 | tf_op jit(solution)/shard_map/ppermute | solution.py:17
  57.6 5.7 %collective-permute-done.5 = f32[2,20,20,2]{3,0,2,1:T(2,128)S(1)} collective-permute-done((f32[2,20,20,2]{3,0,2,1:T(2,128)S(1)}, f32[2,20,20,2]{3,0,2,1:T(2,128)S(1)}, u32[]{:S(2)}, u32[]{:S(2)}) %collective-permute-start.5) | collective-permute-done | bytes 6432 | tf_op jit(solution)/shard_map/ppermute | solution.py:19
  68.2 9.8 %reshape.211 = f32[8,2,8,2,64,2]{5,4,3,2,1,0:T(8,128)} reshape(f32[1,16,16,128]{3,2,1,0:T(8,128)S(1)} %fusion.22) | data formatting | bytes 262144 | tf_op jit(solution)/shard_map/reshape | solution.py:88
  78.0 4.0 %reduce_sum.70 = f32[8,8,64]{2,1,0:T(8,128)S(1)} reduce(f32[8,2,8,2,64,2]{5,4,3,2,1,0:T(8,128)} %reshape.211, f32[]{:T(128)} %constant.15.clone.1), dimensions={1,3,5}, to_apply=%region_0.0 | reduce | flops 28672 | bytes 147460 | tf_op jit(solution)/shard_map/reduce_sum | solution.py:89
  91.0 3.9 collective-permute-start.9
  95.1 7.7 %collective-permute-done.9 = f32[2,12,2,64]{3,2,1,0:T(2,128)S(1)} collective-permute-done((f32[2,12,2,64]{3,2,1,0:T(2,128)S(1)}, f32[2,12,2,64]{3,2,1,0:T(2,128)S(1)}, u32[]{:S(2)}, u32[]{:S(2)}) %collective-permute-start.9) | collective-permute-done | bytes 12320 | tf_op jit(solution)/shard_map/ppermute | solution.py:19
  103.0 5.2 %collective-permute-start.10 = (f32[2,12,12,2]{3,0,2,1:T(2,128)S(1)}, f32[2,12,12,2]{3,0,2,1:T(2,128)S(1)}, u32[]{:S(2)}, u32[]{:S(2)}) collective-permute-start(f32[2,12,12,2]{3,0,2,1:T(2,128)S(1)} %get-tuple-element.36), channel_id=1, source_target_pairs={{0,1},{1,2},{2,3},{3,4},{4,5},{5,6},{6,7},{8,9},{9,10},{10,11},{11... | collective-permute-start | bytes 6920 | tf_op jit(solution)/shard_map/ppermute | solution.py:17
  112.1 6.9 %collective-permute-done.11 = f32[2,12,12,2]{3,0,2,1:T(2,128)S(1)} collective-permute-done((f32[2,12,12,2]{3,0,2,1:T(2,128)S(1)}, f32[2,12,12,2]{3,0,2,1:T(2,128)S(1)}, u32[]{:S(2)}, u32[]{:S(2)}) %collective-permute-start.11) | collective-permute-done | bytes 2336 | tf_op jit(solution)/shard_map/ppermute | solution.py:19
  124.8 3.3 collective-permute-done.13
  130.1 3.9 collective-permute-start.15
  134.0 7.7 %collective-permute-done.15 = f32[2,8,2,32]{3,2,1,0:T(2,128)S(1)} collective-permute-done((f32[2,8,2,32]{3,2,1,0:T(2,128)S(1)}, f32[2,8,2,32]{3,2,1,0:T(2,128)S(1)}, u32[]{:S(2)}, u32[]{:S(2)}) %collective-permute-start.15) | collective-permute-done | bytes 4128 | tf_op jit(solution)/shard_map/ppermute | solution.py:19
  141.9 4.8 %collective-permute-start.16 = (f32[2,8,8,2]{3,2,1,0:T(8,128)S(1)}, f32[2,8,8,2]{3,2,1,0:T(8,128)S(1)}, u32[]{:S(2)}, u32[]{:S(2)}) collective-permute-start(f32[2,8,8,2]{3,2,1,0:T(8,128)S(1)} %get-tuple-element.48), channel_id=1, source_target_pairs={{0,1},{1,2},{2,3},{3,4},{4,5},{5,6},{6,7},{8,9},{9,10},{10,11},{11... | collective-permute-start | bytes 3080 | tf_op jit(solution)/shard_map/ppermute | solution.py:17
  148.9 4.6 %collective-permute-done.17 = f32[2,8,8,2]{3,2,1,0:T(8,128)S(1)} collective-permute-done((f32[2,8,8,2]{3,2,1,0:T(8,128)S(1)}, f32[2,8,8,2]{3,2,1,0:T(8,128)S(1)}, u32[]{:S(2)}, u32[]{:S(2)}) %collective-permute-start.17) | collective-permute-done | bytes 1056 | tf_op jit(solution)/shard_map/ppermute | solution.py:19
  162.4 3.9 collective-permute-start.21
  166.3 7.7 %collective-permute-done.21 = f32[2,6,2,16]{3,2,1,0:T(2,128)S(1)} collective-permute-done((f32[2,6,2,16]{3,2,1,0:T(2,128)S(1)}, f32[2,6,2,16]{3,2,1,0:T(2,128)S(1)}, u32[]{:S(2)}, u32[]{:S(2)}) %collective-permute-start.21) | collective-permute-done | bytes 1568 | tf_op jit(solution)/shard_map/ppermute | solution.py:19
  174.1 4.7 %collective-permute-start.22 = (f32[2,6,6,2]{3,2,1,0:T(8,128)S(1)}, f32[2,6,6,2]{3,2,1,0:T(8,128)S(1)}, u32[]{:S(2)}, u32[]{:S(2)}) collective-permute-start(f32[2,6,6,2]{3,2,1,0:T(8,128)S(1)} %get-tuple-element.53), channel_id=1, source_target_pairs={{0,1},{1,2},{2,3},{3,4},{4,5},{5,6},{6,7},{8,9},{9,10},{10,11},{11... | collective-permute-start | bytes 1736 | tf_op jit(solution)/shard_map/ppermute | solution.py:17
  180.6 4.4 %collective-permute-done.23 = f32[2,6,6,2]{3,2,1,0:T(8,128)S(1)} collective-permute-done((f32[2,6,6,2]{3,2,1,0:T(8,128)S(1)}, f32[2,6,6,2]{3,2,1,0:T(8,128)S(1)}, u32[]{:S(2)}, u32[]{:S(2)}) %collective-permute-start.23) | collective-permute-done | bytes 608 | tf_op jit(solution)/shard_map/ppermute | solution.py:19
  185.7 112.0 %all-reduce.16 = f32[8192]{0:T(1024)S(1)} all-reduce(f32[8192]{0:T(1024)S(1)} %multiply_dynamic-update-slice_fusion), channel_id=2, replica_groups=mesh['gx'=8,'gy'=16,'gz'=8] {'gx','gy','gz'}, use_global_device_ids=true, to_apply=%add.16 | all-reduce | flops 8192 | bytes 65536
  300.0 4.5 %collective-permute-start.29 = (f32[1,2,2,1]{3,2,1,0:T(2,128)S(1)}, f32[1,2,2,1]{3,2,1,0:T(2,128)S(1)}, u32[]{:S(2)}, u32[]{:S(2)}) collective-permute-start(f32[1,2,2,1]{3,2,1,0:T(2,128)S(1)} %get-tuple-element.76), channel_id=1, source_target_pairs={{0,1},{1,2},{2,3},{3,4},{4,5},{5,6},{6,7},{8,9},{9,10},{10,11},{11... | collective-permute-start | bytes 56 | tf_op jit(solution)/shard_map/ppermute | solution.py:34
  306.8 9.6 %collective-permute-start.27 = (f32[1,2,1,16]{3,2,1,0:T(1,128)S(1)}, f32[1,2,1,16]{3,2,1,0:T(1,128)S(1)}, u32[]{:S(2)}, u32[]{:S(2)}) collective-permute-start(f32[1,2,1,16]{3,2,1,0:T(1,128)S(1)} %get-tuple-element.77), channel_id=1, source_target_pairs={{0,8},{8,16},{16,24},{24,32},{32,40},{40,48},{48,56},{56,64},{64,7... | collective-permute-start | bytes 392 | tf_op jit(solution)/shard_map/ppermute | solution.py:34
  324.0 9.9 %collective-permute-start.33 = (f32[1,4,1,32]{3,2,1,0:T(1,128)S(1)}, f32[1,4,1,32]{3,2,1,0:T(1,128)S(1)}, u32[]{:S(2)}, u32[]{:S(2)}) collective-permute-start(f32[1,4,1,32]{3,2,1,0:T(1,128)S(1)} %get-tuple-element.69), channel_id=1, source_target_pairs={{0,8},{8,16},{16,24},{24,32},{32,40},{40,48},{48,56},{56,64},{64,7... | collective-permute-start | bytes 1544 | tf_op jit(solution)/shard_map/ppermute | solution.py:34
  339.6 4.5 %collective-permute-start.35 = (f32[1,4,4,1]{3,2,1,0:T(4,128)S(1)}, f32[1,4,4,1]{3,2,1,0:T(4,128)S(1)}, u32[]{:S(2)}, u32[]{:S(2)}) collective-permute-start(f32[1,4,4,1]{3,2,1,0:T(4,128)S(1)} %get-tuple-element.68), channel_id=1, source_target_pairs={{0,1},{1,2},{2,3},{3,4},{4,5},{5,6},{6,7},{8,9},{9,10},{10,11},{11... | collective-permute-start | bytes 200 | tf_op jit(solution)/shard_map/ppermute | solution.py:34
  348.0 9.9 %collective-permute-start.39 = (f32[1,8,1,64]{3,2,1,0:T(1,128)S(1)}, f32[1,8,1,64]{3,2,1,0:T(1,128)S(1)}, u32[]{:S(2)}, u32[]{:S(2)}) collective-permute-start(f32[1,8,1,64]{3,2,1,0:T(1,128)S(1)} %get-tuple-element.57), channel_id=1, source_target_pairs={{0,8},{8,16},{16,24},{24,32},{32,40},{40,48},{48,56},{56,64},{64,7... | collective-permute-start | bytes 6152 | tf_op jit(solution)/shard_map/ppermute | solution.py:34
  363.7 4.8 %collective-permute-start.41 = (f32[1,8,8,1]{3,2,1,0:T(8,128)S(1)}, f32[1,8,8,1]{3,2,1,0:T(8,128)S(1)}, u32[]{:S(2)}, u32[]{:S(2)}) collective-permute-start(f32[1,8,8,1]{3,2,1,0:T(8,128)S(1)} %get-tuple-element.56), channel_id=1, source_target_pairs={{0,1},{1,2},{2,3},{3,4},{4,5},{5,6},{6,7},{8,9},{9,10},{10,11},{11... | collective-permute-start | bytes 776 | tf_op jit(solution)/shard_map/ppermute | solution.py:34
  373.2 9.9 %collective-permute-start.45 = (f32[1,16,1,128]{3,1,2,0:T(8,128)S(1)}, f32[1,16,1,128]{3,1,2,0:T(8,128)S(1)}, u32[]{:S(2)}, u32[]{:S(2)}) collective-permute-start(f32[1,16,1,128]{3,1,2,0:T(8,128)S(1)} %bitcast.106), channel_id=1, source_target_pairs={{0,8},{8,16},{16,24},{24,32},{32,40},{40,48},{48,56},{56,64},{64,7... | collective-permute-start | bytes 24584 | tf_op jit(solution)/shard_map/ppermute | solution.py:34
  388.9 4.9 %collective-permute-start.47 = (f32[1,16,16,1]{3,2,1,0:T(8,128)S(1)}, f32[1,16,16,1]{3,2,1,0:T(8,128)S(1)}, u32[]{:S(2)}, u32[]{:S(2)}) collective-permute-start(f32[1,16,16,1]{3,2,1,0:T(8,128)S(1)} %get-tuple-element.39), channel_id=1, source_target_pairs={{0,1},{1,2},{2,3},{3,4},{4,5},{5,6},{6,7},{8,9},{9,10},{10,11},{11... | collective-permute-start | bytes 3080 | tf_op jit(solution)/shard_map/ppermute | solution.py:34
  (183 shorter events, 89.4 us)
Async XLA Ops:
  8.2 23.7 %collective-permute-start.2 = (f32[2,20,2,128]{3,2,1,0:T(2,128)S(1)}, f32[2,20,2,128]{3,2,1,0:T(2,128)S(1)}, u32[]{:S(2)}, u32[]{:S(2)}) collective-permute-start(f32[2,20,2,128]{3,2,1,0:T(2,128)S(1)} %get-tuple-element.27), channel_id=1, source_target_pairs={{0,8},{8,16},{16,24},{24,32},{32,40},{40,48},{48,56},{56,64},{64,7... | collective-permute-start | bytes 122888 | tf_op jit(solution)/shard_map/ppermute | solution.py:17
  29.8 12.4 %collective-permute-start.3 = (f32[2,20,2,128]{3,2,1,0:T(2,128)S(1)}, f32[2,20,2,128]{3,2,1,0:T(2,128)S(1)}, u32[]{:S(2)}, u32[]{:S(2)}) collective-permute-start(f32[2,20,2,128]{3,2,1,0:T(2,128)S(1)} %get-tuple-element.26), channel_id=1, source_target_pairs={{8,0},{16,8},{24,16},{32,24},{40,32},{48,40},{56,48},{64,56},{72,6... | collective-permute-start | bytes 122888 | tf_op jit(solution)/shard_map/ppermute | solution.py:19
  42.8 14.9 %collective-permute-start.4 = (f32[2,20,20,2]{3,0,2,1:T(2,128)S(1)}, f32[2,20,20,2]{3,0,2,1:T(2,128)S(1)}, u32[]{:S(2)}, u32[]{:S(2)}) collective-permute-start(f32[2,20,20,2]{3,0,2,1:T(2,128)S(1)} %get-tuple-element.24), channel_id=1, source_target_pairs={{0,1},{1,2},{2,3},{3,4},{4,5},{5,6},{6,7},{8,9},{9,10},{10,11},{11... | collective-permute-start | bytes 19208 | tf_op jit(solution)/shard_map/ppermute | solution.py:17
  48.0 15.3 %collective-permute-start.5 = (f32[2,20,20,2]{3,0,2,1:T(2,128)S(1)}, f32[2,20,20,2]{3,0,2,1:T(2,128)S(1)}, u32[]{:S(2)}, u32[]{:S(2)}) collective-permute-start(f32[2,20,20,2]{3,0,2,1:T(2,128)S(1)} %get-tuple-element.25), channel_id=1, source_target_pairs={{1,0},{2,1},{3,2},{4,3},{5,4},{6,5},{7,6},{9,8},{10,9},{11,10},{12... | collective-permute-start | bytes 19208 | tf_op jit(solution)/shard_map/ppermute | solution.py:19
  87.9 7.1 %collective-permute-start.8 = (f32[2,12,2,64]{3,2,1,0:T(2,128)S(1)}, f32[2,12,2,64]{3,2,1,0:T(2,128)S(1)}, u32[]{:S(2)}, u32[]{:S(2)}) collective-permute-start(f32[2,12,2,64]{3,2,1,0:T(2,128)S(1)} %get-tuple-element.45), channel_id=1, source_target_pairs={{0,8},{8,16},{16,24},{24,32},{32,40},{40,48},{48,56},{56,64},{64,7... | collective-permute-start | bytes 36872 | tf_op jit(solution)/shard_map/ppermute | solution.py:17
  91.0 11.7 %collective-permute-start.9 = (f32[2,12,2,64]{3,2,1,0:T(2,128)S(1)}, f32[2,12,2,64]{3,2,1,0:T(2,128)S(1)}, u32[]{:S(2)}, u32[]{:S(2)}) collective-permute-start(f32[2,12,2,64]{3,2,1,0:T(2,128)S(1)} %get-tuple-element.44), channel_id=1, source_target_pairs={{8,0},{16,8},{24,16},{32,24},{40,32},{48,40},{56,48},{64,56},{72,6... | collective-permute-start | bytes 36872 | tf_op jit(solution)/shard_map/ppermute | solution.py:19
  103.0 9.1 %collective-permute-start.10 = (f32[2,12,12,2]{3,0,2,1:T(2,128)S(1)}, f32[2,12,12,2]{3,0,2,1:T(2,128)S(1)}, u32[]{:S(2)}, u32[]{:S(2)}) collective-permute-start(f32[2,12,12,2]{3,0,2,1:T(2,128)S(1)} %get-tuple-element.36), channel_id=1, source_target_pairs={{0,1},{1,2},{2,3},{3,4},{4,5},{5,6},{6,7},{8,9},{9,10},{10,11},{11... | collective-permute-start | bytes 6920 | tf_op jit(solution)/shard_map/ppermute | solution.py:17
  108.2 10.7 %collective-permute-start.11 = (f32[2,12,12,2]{3,0,2,1:T(2,128)S(1)}, f32[2,12,12,2]{3,0,2,1:T(2,128)S(1)}, u32[]{:S(2)}, u32[]{:S(2)}) collective-permute-start(f32[2,12,12,2]{3,0,2,1:T(2,128)S(1)} %get-tuple-element.37), channel_id=1, source_target_pairs={{1,0},{2,1},{3,2},{4,3},{5,4},{6,5},{7,6},{9,8},{10,9},{11,10},{12... | collective-permute-start | bytes 6920 | tf_op jit(solution)/shard_map/ppermute | solution.py:19
  130.1 11.6 %collective-permute-start.15 = (f32[2,8,2,32]{3,2,1,0:T(2,128)S(1)}, f32[2,8,2,32]{3,2,1,0:T(2,128)S(1)}, u32[]{:S(2)}, u32[]{:S(2)}) collective-permute-start(f32[2,8,2,32]{3,2,1,0:T(2,128)S(1)} %get-tuple-element.62), channel_id=1, source_target_pairs={{8,0},{16,8},{24,16},{32,24},{40,32},{48,40},{56,48},{64,56},{72,6... | collective-permute-start | bytes 12296 | tf_op jit(solution)/shard_map/ppermute | solution.py:19
  141.9 7.0 %collective-permute-start.16 = (f32[2,8,8,2]{3,2,1,0:T(8,128)S(1)}, f32[2,8,8,2]{3,2,1,0:T(8,128)S(1)}, u32[]{:S(2)}, u32[]{:S(2)}) collective-permute-start(f32[2,8,8,2]{3,2,1,0:T(8,128)S(1)} %get-tuple-element.48), channel_id=1, source_target_pairs={{0,1},{1,2},{2,3},{3,4},{4,5},{5,6},{6,7},{8,9},{9,10},{10,11},{11... | collective-permute-start | bytes 3080 | tf_op jit(solution)/shard_map/ppermute | solution.py:17
  146.7 6.8 %collective-permute-start.17 = (f32[2,8,8,2]{3,2,1,0:T(8,128)S(1)}, f32[2,8,8,2]{3,2,1,0:T(8,128)S(1)}, u32[]{:S(2)}, u32[]{:S(2)}) collective-permute-start(f32[2,8,8,2]{3,2,1,0:T(8,128)S(1)} %get-tuple-element.49), channel_id=1, source_target_pairs={{1,0},{2,1},{3,2},{4,3},{5,4},{6,5},{7,6},{9,8},{10,9},{11,10},{12... | collective-permute-start | bytes 3080 | tf_op jit(solution)/shard_map/ppermute | solution.py:19
  162.4 11.6 %collective-permute-start.21 = (f32[2,6,2,16]{3,2,1,0:T(2,128)S(1)}, f32[2,6,2,16]{3,2,1,0:T(2,128)S(1)}, u32[]{:S(2)}, u32[]{:S(2)}) collective-permute-start(f32[2,6,2,16]{3,2,1,0:T(2,128)S(1)} %pad_maximum_fusion.45), channel_id=1, source_target_pairs={{8,0},{16,8},{24,16},{32,24},{40,32},{48,40},{56,48},{64,56},{72,6... | collective-permute-start | bytes 4616 | tf_op jit(solution)/shard_map/ppermute | solution.py:19
  174.1 6.5 %collective-permute-start.22 = (f32[2,6,6,2]{3,2,1,0:T(8,128)S(1)}, f32[2,6,6,2]{3,2,1,0:T(8,128)S(1)}, u32[]{:S(2)}, u32[]{:S(2)}) collective-permute-start(f32[2,6,6,2]{3,2,1,0:T(8,128)S(1)} %get-tuple-element.53), channel_id=1, source_target_pairs={{0,1},{1,2},{2,3},{3,4},{4,5},{5,6},{6,7},{8,9},{9,10},{10,11},{11... | collective-permute-start | bytes 1736 | tf_op jit(solution)/shard_map/ppermute | solution.py:17
  298.7 22.1 %collective-permute-start.28 = (f32[1,2,2,1]{3,2,1,0:T(2,128)S(1)}, f32[1,2,2,1]{3,2,1,0:T(2,128)S(1)}, u32[]{:S(2)}, u32[]{:S(2)}) collective-permute-start(f32[1,2,2,1]{3,2,1,0:T(2,128)S(1)} %get-tuple-element.75), channel_id=1, source_target_pairs={{1,0},{2,1},{3,2},{4,3},{5,4},{6,5},{7,6},{9,8},{10,9},{11,10},{12... | collective-permute-start | bytes 56 | tf_op jit(solution)/shard_map/ppermute | solution.py:35
  300.0 20.8 %collective-permute-start.29 = (f32[1,2,2,1]{3,2,1,0:T(2,128)S(1)}, f32[1,2,2,1]{3,2,1,0:T(2,128)S(1)}, u32[]{:S(2)}, u32[]{:S(2)}) collective-permute-start(f32[1,2,2,1]{3,2,1,0:T(2,128)S(1)} %get-tuple-element.76), channel_id=1, source_target_pairs={{0,1},{1,2},{2,3},{3,4},{4,5},{5,6},{6,7},{8,9},{9,10},{10,11},{11... | collective-permute-start | bytes 56 | tf_op jit(solution)/shard_map/ppermute | solution.py:34
  304.6 13.2 %collective-permute-start.26 = (f32[1,2,1,16]{3,2,1,0:T(1,128)S(1)}, f32[1,2,1,16]{3,2,1,0:T(1,128)S(1)}, u32[]{:S(2)}, u32[]{:S(2)}) collective-permute-start(f32[1,2,1,16]{3,2,1,0:T(1,128)S(1)} %get-tuple-element.78), channel_id=1, source_target_pairs={{8,0},{16,8},{24,16},{32,24},{40,32},{48,40},{56,48},{64,56},{72,6... | collective-permute-start | bytes 392 | tf_op jit(solution)/shard_map/ppermute | solution.py:35
  306.8 14.0 %collective-permute-start.27 = (f32[1,2,1,16]{3,2,1,0:T(1,128)S(1)}, f32[1,2,1,16]{3,2,1,0:T(1,128)S(1)}, u32[]{:S(2)}, u32[]{:S(2)}) collective-permute-start(f32[1,2,1,16]{3,2,1,0:T(1,128)S(1)} %get-tuple-element.77), channel_id=1, source_target_pairs={{0,8},{8,16},{16,24},{24,32},{32,40},{40,48},{48,56},{56,64},{64,7... | collective-permute-start | bytes 392 | tf_op jit(solution)/shard_map/ppermute | solution.py:34
  322.1 17.5 %collective-permute-start.32 = (f32[1,4,1,32]{3,2,1,0:T(1,128)S(1)}, f32[1,4,1,32]{3,2,1,0:T(1,128)S(1)}, u32[]{:S(2)}, u32[]{:S(2)}) collective-permute-start(f32[1,4,1,32]{3,2,1,0:T(1,128)S(1)} %get-tuple-element.70), channel_id=1, source_target_pairs={{8,0},{16,8},{24,16},{32,24},{40,32},{48,40},{56,48},{64,56},{72,6... | collective-permute-start | bytes 1544 | tf_op jit(solution)/shard_map/ppermute | solution.py:35
  324.0 20.2 %collective-permute-start.33 = (f32[1,4,1,32]{3,2,1,0:T(1,128)S(1)}, f32[1,4,1,32]{3,2,1,0:T(1,128)S(1)}, u32[]{:S(2)}, u32[]{:S(2)}) collective-permute-start(f32[1,4,1,32]{3,2,1,0:T(1,128)S(1)} %get-tuple-element.69), channel_id=1, source_target_pairs={{0,8},{8,16},{16,24},{24,32},{32,40},{40,48},{48,56},{56,64},{64,7... | collective-permute-start | bytes 1544 | tf_op jit(solution)/shard_map/ppermute | solution.py:34
  334.0 11.6 %collective-permute-start.30 = (f32[1,1,4,32]{3,2,1,0:T(4,128)S(1)}, f32[1,1,4,32]{3,2,1,0:T(4,128)S(1)}, u32[]{:S(2)}, u32[]{:S(2)}) collective-permute-start(f32[1,1,4,32]{3,2,1,0:T(4,128)S(1)} %get-tuple-element.72), channel_id=1, source_target_pairs={{128,0},{256,128},{384,256},{512,384},{640,512},{768,640},{896,768... | collective-permute-start | bytes 1544 | tf_op jit(solution)/shard_map/ppermute | solution.py:35
  335.3 10.3 %collective-permute-start.31 = (f32[1,1,4,32]{3,2,1,0:T(4,128)S(1)}, f32[1,1,4,32]{3,2,1,0:T(4,128)S(1)}, u32[]{:S(2)}, u32[]{:S(2)}) collective-permute-start(f32[1,1,4,32]{3,2,1,0:T(4,128)S(1)} %get-tuple-element.71), channel_id=1, source_target_pairs={{0,128},{128,256},{256,384},{384,512},{512,640},{640,768},{768,896... | collective-permute-start | bytes 1544 | tf_op jit(solution)/shard_map/ppermute | solution.py:34
  346.1 17.6 %collective-permute-start.38 = (f32[1,8,1,64]{3,2,1,0:T(1,128)S(1)}, f32[1,8,1,64]{3,2,1,0:T(1,128)S(1)}, u32[]{:S(2)}, u32[]{:S(2)}) collective-permute-start(f32[1,8,1,64]{3,2,1,0:T(1,128)S(1)} %get-tuple-element.58), channel_id=1, source_target_pairs={{8,0},{16,8},{24,16},{32,24},{40,32},{48,40},{56,48},{64,56},{72,6... | collective-permute-start | bytes 6152 | tf_op jit(solution)/shard_map/ppermute | solution.py:35
  348.0 20.5 %collective-permute-start.39 = (f32[1,8,1,64]{3,2,1,0:T(1,128)S(1)}, f32[1,8,1,64]{3,2,1,0:T(1,128)S(1)}, u32[]{:S(2)}, u32[]{:S(2)}) collective-permute-start(f32[1,8,1,64]{3,2,1,0:T(1,128)S(1)} %get-tuple-element.57), channel_id=1, source_target_pairs={{0,8},{8,16},{16,24},{24,32},{32,40},{40,48},{48,56},{56,64},{64,7... | collective-permute-start | bytes 6152 | tf_op jit(solution)/shard_map/ppermute | solution.py:34
  358.0 12.1 %collective-permute-start.36 = (f32[1,1,8,64]{3,2,1,0:T(8,128)S(1)}, f32[1,1,8,64]{3,2,1,0:T(8,128)S(1)}, u32[]{:S(2)}, u32[]{:S(2)}) collective-permute-start(f32[1,1,8,64]{3,2,1,0:T(8,128)S(1)} %get-tuple-element.60), channel_id=1, source_target_pairs={{128,0},{256,128},{384,256},{512,384},{640,512},{768,640},{896,768... | collective-permute-start | bytes 6152 | tf_op jit(solution)/shard_map/ppermute | solution.py:35
  359.3 10.8 %collective-permute-start.37 = (f32[1,1,8,64]{3,2,1,0:T(8,128)S(1)}, f32[1,1,8,64]{3,2,1,0:T(8,128)S(1)}, u32[]{:S(2)}, u32[]{:S(2)}) collective-permute-start(f32[1,1,8,64]{3,2,1,0:T(8,128)S(1)} %get-tuple-element.59), channel_id=1, source_target_pairs={{0,128},{128,256},{256,384},{384,512},{512,640},{640,768},{768,896... | collective-permute-start | bytes 6152 | tf_op jit(solution)/shard_map/ppermute | solution.py:34
  363.7 6.4 %collective-permute-start.41 = (f32[1,8,8,1]{3,2,1,0:T(8,128)S(1)}, f32[1,8,8,1]{3,2,1,0:T(8,128)S(1)}, u32[]{:S(2)}, u32[]{:S(2)}) collective-permute-start(f32[1,8,8,1]{3,2,1,0:T(8,128)S(1)} %get-tuple-element.56), channel_id=1, source_target_pairs={{0,1},{1,2},{2,3},{3,4},{4,5},{5,6},{6,7},{8,9},{9,10},{10,11},{11... | collective-permute-start | bytes 776 | tf_op jit(solution)/shard_map/ppermute | solution.py:34
  371.2 17.6 %collective-permute-start.44 = (f32[1,16,1,128]{3,1,2,0:T(8,128)S(1)}, f32[1,16,1,128]{3,1,2,0:T(8,128)S(1)}, u32[]{:S(2)}, u32[]{:S(2)}) collective-permute-start(f32[1,16,1,128]{3,1,2,0:T(8,128)S(1)} %bitcast.107), channel_id=1, source_target_pairs={{8,0},{16,8},{24,16},{32,24},{40,32},{48,40},{56,48},{64,56},{72,6... | collective-permute-start | bytes 24584 | tf_op jit(solution)/shard_map/ppermute | solution.py:35
  373.2 20.6 %collective-permute-start.45 = (f32[1,16,1,128]{3,1,2,0:T(8,128)S(1)}, f32[1,16,1,128]{3,1,2,0:T(8,128)S(1)}, u32[]{:S(2)}, u32[]{:S(2)}) collective-permute-start(f32[1,16,1,128]{3,1,2,0:T(8,128)S(1)} %bitcast.106), channel_id=1, source_target_pairs={{0,8},{8,16},{16,24},{24,32},{32,40},{40,48},{48,56},{56,64},{64,7... | collective-permute-start | bytes 24584 | tf_op jit(solution)/shard_map/ppermute | solution.py:34
  383.1 13.4 %collective-permute-start.42 = (f32[1,1,16,128]{3,2,1,0:T(8,128)S(1)}, f32[1,1,16,128]{3,2,1,0:T(8,128)S(1)}, u32[]{:S(2)}, u32[]{:S(2)}) collective-permute-start(f32[1,1,16,128]{3,2,1,0:T(8,128)S(1)} %get-tuple-element.41), channel_id=1, source_target_pairs={{128,0},{256,128},{384,256},{512,384},{640,512},{768,640},{896,768... | collective-permute-start | bytes 24584 | tf_op jit(solution)/shard_map/ppermute | solution.py:35
  384.4 12.1 %collective-permute-start.43 = (f32[1,1,16,128]{3,2,1,0:T(8,128)S(1)}, f32[1,1,16,128]{3,2,1,0:T(8,128)S(1)}, u32[]{:S(2)}, u32[]{:S(2)}) collective-permute-start(f32[1,1,16,128]{3,2,1,0:T(8,128)S(1)} %get-tuple-element.40), channel_id=1, source_target_pairs={{0,128},{128,256},{256,384},{384,512},{512,640},{640,768},{768,896... | collective-permute-start | bytes 24584 | tf_op jit(solution)/shard_map/ppermute | solution.py:34
  387.5 7.2 %collective-permute-start.46 = (f32[1,16,16,1]{3,2,1,0:T(8,128)S(1)}, f32[1,16,16,1]{3,2,1,0:T(8,128)S(1)}, u32[]{:S(2)}, u32[]{:S(2)}) collective-permute-start(f32[1,16,16,1]{3,2,1,0:T(8,128)S(1)} %get-tuple-element.38), channel_id=1, source_target_pairs={{1,0},{2,1},{3,2},{4,3},{5,4},{6,5},{7,6},{9,8},{10,9},{11,10},{12... | collective-permute-start | bytes 3080 | tf_op jit(solution)/shard_map/ppermute | solution.py:35
  388.9 7.7 %collective-permute-start.47 = (f32[1,16,16,1]{3,2,1,0:T(8,128)S(1)}, f32[1,16,16,1]{3,2,1,0:T(8,128)S(1)}, u32[]{:S(2)}, u32[]{:S(2)}) collective-permute-start(f32[1,16,16,1]{3,2,1,0:T(8,128)S(1)} %get-tuple-element.39), channel_id=1, source_target_pairs={{0,1},{1,2},{2,3},{3,4},{4,5},{5,6},{6,7},{8,9},{9,10},{10,11},{11... | collective-permute-start | bytes 3080 | tf_op jit(solution)/shard_map/ppermute | solution.py:34
  (19 other events, 448.5 us)
where the time goes:
time: 401 us; the launch traced here: 397 us
  starting transfers between devices  153 us (38%)
  blocking collectives  112 us (28%)
  waiting for transfers between devices  85.2 us (21%)
  local copies, waits for them, and re-layouts  28.5 us (7%)
  other arithmetic  16.6 us (4%)
    unnamed x1, blocking collectives  112 us
    ppermute x12, starting transfers between devices, with_halo(): lax.ppermute(last, axis, up)  70.3 us
    ppermute x12, waiting for transfers between devices, extended(): lax.ppermute(head, axis, [((i + 1) % count, i) for i in range(ends)])  66.8 us
    ppermute x12, starting transfers between devices, extended(): lax.ppermute(tail, axis, [(i, (i + 1) % count) for i in range(ends)])  40.4 us
    ppermute x12, starting transfers between devices, extended(): lax.ppermute(head, axis, [((i + 1) % count, i) for i in range(ends)])  24.3 us
    ppermute x12, starting transfers between devices, with_halo(): lax.ppermute(leading, axis, [(b, a) for a, b in up])  18.3 us
    ppermute x12, waiting for transfers between devices, extended(): lax.ppermute(tail, axis, [(i, (i + 1) % count) for i in range(ends)])  11.9 us
    reshape x3, local copies, waits for them, and re-layouts, coarsen(): values.reshape((leading, size_x // 2, 2, size_y // 2, 2, size_z // 2, 2))  11 us
  transfers between devices with their start and end apart: 48, of which 21 were waited for; matrix products, arithmetic and copies ran while one was open for 4% of the time, Pallas kernels for 0%

commit v1 on v0

v1 whole, which is shorter than its diff:
```python
import functools
import itertools

import jax
import jax.numpy as jnp
from jax import lax
from jax.experimental import pallas as pl
from jax.experimental.pallas import tpu as pltpu
from jax.sharding import PartitionSpec as P

MESH = pl.DeviceIdType.MESH
F32 = jnp.float32
S = 0.8 / 6.0
OFFS = [o for o in itertools.product((-1, 0, 1), repeat=3) if o != (0, 0, 0)]
SLOT = {o: i for i, o in enumerate(OFFS)}
ZOFFS = [o for o in OFFS if o[2] != 0]
ZSLOT = {o: i for i, o in enumerate(ZOFFS)}
XY = [(-1, -1), (-1, 1), (1, -1), (1, 1)]
XZ = [(0, -1), (0, 1)] + XY


def neg(o):
    return tuple(-v for v in o)


def roll(v, shift):
    shift = shift % 128
    return v if shift == 0 else pltpu.roll(v, shift, v.ndim - 1)


def split2(v):
    hi = v.astype(jnp.bfloat16)
    lo = (v - hi.astype(F32)).astype(jnp.bfloat16)
    return jnp.concatenate([hi, lo], axis=1)


def select_dot(v, sel):
    return jnp.dot(split2(v), sel, preferred_element_type=F32)


def kernel(dims, refs):
    nx, ny, nz = dims
    xn = ny // 2
    n_y = nx * 2
    r = refs
    ix, iy, iz = lax.axis_index("gx"), lax.axis_index("gy"), lax.axis_index("gz")
    ih, ixx = iy // xn, iy % xn

    def dev(dx, dy, dz):
        return {
            "gx": lax.rem(ix + dx + nx, nx),
            "gy": lax.rem(iy + dy + ny, ny),
            "gz": lax.rem(iz + dz + nz, nz),
        }

    def copy(src, dst, key, device):
        c = pltpu.make_async_remote_copy(
            src_ref=src,
            dst_ref=dst,
            send_sem=r["ssem"].at[key],
            recv_sem=r["rsem"].at[key],
            device_id=device,
            device_id_type=MESH,
        )
        return c

    def send(src, dst, key, device):
        copy(src, dst, key, device).start()

    me = {"gx": ix, "gy": iy, "gz": iz}
    right = {"gx": lax.rem(ix + 1, nx), "gy": iy, "gz": iz}

    group_y = []
    for k in range(1, n_y):
        t = lax.rem(ih * nx + ix + k, n_y)
        group_y.append({"gx": t % nx, "gy": (t // nx) * xn + ixx, "gz": iz})
    group_x = [{"gx": ix, "gy": ih * xn + lax.rem(ixx + k, xn), "gz": iz} for k in range(1, xn)]
    group_z = [{"gx": ix, "gy": iy, "gz": lax.rem(iz + k, nz)} for k in range(1, nz)]

    barrier = pltpu.get_barrier_semaphore()
    partners = [dev(*o) for o in OFFS] + group_y + group_x + group_z
    for d in partners:
        pl.semaphore_signal(barrier, inc=1, device_id=d, device_id_type=MESH)

    lane = lax.broadcasted_iota(jnp.int32, (8, 128), 1)
    row = lax.broadcasted_iota(jnp.int32, (8, 128), 0)
    zero = jnp.zeros((8, 128), F32)

    def flag(c):
        return jnp.where(c, jnp.float32(1), jnp.float32(0))

    mx = {-1: flag(ix > 0), 0: jnp.float32(1), 1: flag(ix < nx - 1)}
    my = {-1: flag(iy > 0), 0: jnp.float32(1), 1: flag(iy < ny - 1)}
    mz = {-1: flag(iz > 0), 0: jnp.float32(1), 1: flag(iz < nz - 1)}
    zmask = jnp.where(lane < 32, mz[-1], jnp.where(lane >= 96, mz[1], 1.0))

    b_ref, w_ref, c_ref, out_ref = r["b"], r["w"], r["c"], r["out"]
    for name in ("G0", "W0", "V0"):
        a = r[name]
        a[:, 0:8, :] = jnp.zeros((20, 8, 128), F32)
        a[:, 24:32, :] = jnp.zeros((20, 8, 128), F32)
    for name in ("GQ", "WQ", "VQ", "UQ", "G1", "W1", "V1", "U1", "G2", "W2", "V2", "U2", "P2", "Q2", "G3", "W3", "V3", "U3", "P3", "T4"):
        r[name][...] = jnp.zeros(r[name].shape, F32)

    G0, W0, V0 = r["G0"], r["W0"], r["V0"]
    w0 = w_ref[...]
    g0 = b_ref[0] / w0
    W0[2:18, 8:24, :] = w0
    G0[2:18, 8:24, :] = g0

    r["YS"][0] = G0[2:18, 8:10, :]
    r["YS"][1] = G0[2:18, 22:24, :]

    def pack_q(src, dst):
        for h in range(2):
            acc = zero
            for x in range(16):
                m = src[x + 2, 8 + 8 * h : 16 + 8 * h, :]
                base = 6 * (x + 2)
                acc = jnp.where((lane >= base) & (lane < base + 3), roll(m, base - 126), acc)
                acc = jnp.where((lane >= base + 3) & (lane < base + 6), roll(m, base + 3 - 127), acc)
            dst[8 * h : 8 * h + 8, :] = acc

    pack_q(G0, r["QS"])
    r["QE"][0] = r["QS"][0:1, :]
    r["QE"][1] = r["QS"][15:16, :]

    pl.semaphore_wait(barrier, len(partners))

    gsl = pl.ds(8, 16)
    send(G0.at[pl.ds(2, 2), gsl], G0.at[pl.ds(18, 2), gsl], 0, dev(-1, 0, 0))
    send(G0.at[pl.ds(16, 2), gsl], G0.at[pl.ds(0, 2), gsl], 1, dev(1, 0, 0))
    for i, d in enumerate((-1, 1)):
        send(r["YS"].at[i], r["RY"].at[1 - i], 2 + i, dev(0, d, 0))
    for dx, dy in XY:
        src = r["YS"].at[(dy + 1) // 2, 0 if dx < 0 else 15]
        send(src, r["RXY"].at[XY.index((-dx, -dy))], 4, dev(dx, dy, 0))
    for dx, dz in XZ:
        send(r["QS"], r["RQ"].at[XZ.index((-dx, -dz))], 5, dev(dx, 0, dz))
    for dy, dz in XY:
        send(r["QE"].at[(dy + 1) // 2], r["RQE"].at[XY.index((-dy, -dz))], 6, dev(0, dy, dz))

    zr = lax.broadcasted_iota(jnp.int32, (256, 128), 0) % 128
    zc = lax.broadcasted_iota(jnp.int32, (256, 128), 1)
    down = jnp.where(zc == 32 + zr // 2, jnp.float32(1), jnp.float32(0)).astype(jnp.bfloat16)
    up = jnp.where(zr == 32 + zc // 2, jnp.float32(1), jnp.float32(0)).astype(jnp.bfloat16)

    C0 = r["C0"]

    def coarsen0(values, scale):
        C0[...] = jnp.sum(values.reshape(8, 2, 16, 128), axis=1)
        t = C0[:, pl.ds(0, 8, stride=2), :] + C0[:, pl.ds(1, 8, stride=2), :]
        return (select_dot(t.reshape(64, 128), down) * scale).reshape(8, 8, 128)

    def pair_z(t, dil):
        ln = lax.broadcasted_iota(jnp.int32, t.shape, t.ndim - 1)
        return t + jnp.where((ln // dil) % 2 == 0, roll(t, -dil), roll(t, dil))

    C1, C2 = r["C1"], r["C2"]

    def coarsen1(values, scale):
        n = values.shape[0] // 2
        C1[...] = jnp.sum(values.reshape(n, 2, 8, 128), axis=1)
        t = C1[:, pl.ds(0, 4, stride=2), :] + C1[:, pl.ds(1, 4, stride=2), :]
        return pair_z(t, 1) * scale

    S1 = r["S1"]
    w1 = coarsen0(w0, 0.0625)
    own1 = (lane >= 32) & (lane < 96)
    w2 = coarsen1(w1, 0.0625)
    C2[0:4, 0:4, :] = w2
    t = C2[0:4, pl.ds(0, 2, stride=2), :] + C2[0:4, pl.ds(1, 2, stride=2), :]
    w3 = pair_z(jnp.sum(t.reshape(2, 2, 2, 128), axis=1), 2) * 0.0625

    lane4 = lane[0:4]

    def pack2(v):
        halves = []
        for h in range(2):
            a = jnp.where(lane4 % 2 == 0, v[2 * h], v[2 * h + 1])
            halves.append(roll(a, -32 if h == 0 else 32))
        return jnp.where(lane4 < 64, halves[0], halves[1])

    def pack3(v):
        return jnp.where(lane[0:2] < 64, roll(v[0], -32), roll(v[1], 32))

    SW = r["SW"]
    SW[0:4, :] = pack2(w2)
    SW[4:6, :] = pack3(w3)
    SW[6:8, :] = jnp.zeros((2, 128), F32)

    def send_all(src, dst, key):
        for o in OFFS:
            send(src, dst.at[SLOT[neg(o)]], key, dev(*o))

    def wait_recv(dst, key):
        copy(dst, dst, key, right).wait_recv()

    def wait_send(like, key):
        copy(like, like, key, right).wait_send()

    send_all(SW, r["RW"], 7)

    def send1(own, n, key):
        s1, ys, zs = r["S1" + n], r["YS1" + n], r["ZS1" + n]
        s1[...] = own
        ys[0] = s1[:, 0:4, :]
        ys[1] = s1[:, 4:8, :]
        acc = zero
        for x in range(8):
            acc = jnp.where((lane >= 16 * x) & (lane < 16 * x + 4), roll(own[x], 16 * x - 32), acc)
            acc = jnp.where((lane >= 16 * x + 4) & (lane < 16 * x + 8), roll(own[x], 16 * x + 4 - 92), acc)
        zs[...] = acc
        send(s1.at[pl.ds(0, 3)], r["RX1" + n].at[1], key, dev(-1, 0, 0))
        send(s1.at[pl.ds(5, 3)], r["RX1" + n].at[0], key, dev(1, 0, 0))
        send(ys.at[0], r["RY1" + n].at[1], key + 1, dev(0, -1, 0))
        send(ys.at[1], r["RY1" + n].at[0], key + 1, dev(0, 1, 0))
        for dx, dy in XY:
            src = ys.at[(dy + 1) // 2, pl.ds(0 if dx < 0 else 5, 3)]
            send(src, r["RXY1" + n].at[XY.index((-dx, -dy))], key + 2, dev(dx, dy, 0))
        for o in ZOFFS:
            send(zs, r["RZ1" + n].at[ZSLOT[neg(o)]], key + 3, dev(*o))

    def recv1(own, n, key, dst):
        for i, name in enumerate(("RX1", "RY1", "RXY1", "RZ1")):
            wait_recv(r[name + n], key + i)
        for x in range(14):
            dx = -1 if x < 3 else (1 if x > 10 else 0)
            for dy in (-1, 0, 1):
                if dx == 0 and dy == 0:
                    base = own[x - 3]
                elif dy == 0:
                    base = r["RX1" + n][(dx + 1) // 2, x if dx < 0 else x - 11]
                elif dx == 0:
                    base = r["RY1" + n][(dy + 1) // 2, x - 3]
                else:
                    base = r["RXY1" + n][XY.index((dx, dy)), x if dx < 0 else x - 11]
                sx = x - 3 if dx == 0 else (x + 5 if dx < 0 else x - 11)
                rows = slice(0, 8) if dy == 0 else (slice(4, 8) if dy < 0 else slice(0, 4))
                lo = r["RZ1" + n][ZSLOT[(dx, dy, -1)], rows, :]
                hi = r["RZ1" + n][ZSLOT[(dx, dy, 1)], rows, :]
                ln = lane[0:8] if dy == 0 else lane4
                v = jnp.where((ln >= 28) & (ln < 32), roll(lo, 28 - 16 * x0(sx) - 4) * mz[-1], base)
                v = jnp.where((ln >= 96) & (ln < 100), roll(hi, 96 - 16 * x0(sx)) * mz[1], v)
                if dx != 0 or dy != 0:
                    v = v * (mx[dx] * my[dy])
                at = 8 if dy == 0 else (4 if dy < 0 else 16)
                dst[x, at : at + (8 if dy == 0 else 4), :] = v

    def x0(v):
        return v

    send1(w1, "w", 8)

    r["YW"][0] = W0[2:18, 8:9, :]
    r["YW"][1] = W0[2:18, 23:24, :]
    pack_q(W0, r["QW"])
    send(W0.at[pl.ds(2, 1), gsl], W0.at[pl.ds(18, 1), gsl], 12, dev(-1, 0, 0))
    send(W0.at[pl.ds(17, 1), gsl], W0.at[pl.ds(1, 1), gsl], 13, dev(1, 0, 0))
    for i, d in enumerate((-1, 1)):
        send(r["YW"].at[i], r["RYW"].at[1 - i], 14, dev(0, d, 0))
        send(r["QW"], r["RQW"].at[1 - i], 15, dev(0, 0, d))

    wi1 = 1.0 / jnp.where(own1, w1, 1.0)
    wi2 = 1.0 / jnp.where(own1[0:4], w2, 1.0)
    wi3 = 1.0 / jnp.where(own1[0:2], w3, 1.0)

    cp = r["CP"]

    @pl.loop(0, nx)
    def _(x):
        for z in range(nz):
            acc = zero
            for p in range(ny // 2):
                tile = c_ref[:, pl.ds(pl.multiple_of((x * (ny // 2) + p) * 128, 128), 128)]
                for q in range(2):
                    y = 2 * p + q
                    at = 8 * y
                    acc = jnp.where((lane >= at) & (lane < at + 8), roll(tile, at - 64 * q - 8 * z), acc)
            cp[x * nz + z] = acc

    GQ, VQ = r["GQ"], r["VQ"]
    for key, dst in ((0, G0.at[pl.ds(18, 2), gsl]), (1, G0.at[pl.ds(0, 2), gsl]), (2, r["RY"].at[1]), (3, r["RY"].at[0])):
        wait_recv(dst, key)
    wait_recv(r["RXY"], 4)
    wait_recv(r["RQ"], 5)
    wait_recv(r["RQE"], 6)
    G0[0:2, 8:24, :] = G0[0:2, 8:24, :] * mx[-1]
    G0[18:20, 8:24, :] = G0[18:20, 8:24, :] * mx[1]
    G0[2:18, 6:8, :] = r["RY"][0] * my[-1]
    G0[2:18, 24:26, :] = r["RY"][1] * my[1]
    for dx, dy in XY:
        v = r["RXY"][XY.index((dx, dy))] * (mx[dx] * my[dy])
        G0[1 if dx < 0 else 18, 7 if dy < 0 else 24, :] = v[1 if dy < 0 else 0, :]

    def qj(ln):
        return ln % 6

    for h in range(2):
        sl = slice(8 * h, 8 * h + 8)
        own = r["QS"][sl, :]
        j = qj(lane)
        v = jnp.where(j < 2, r["RQ"][0, sl, :] * mz[-1], jnp.where(j > 3, r["RQ"][1, sl, :] * mz[1], own))
        lo = jnp.where(j < 2, r["RQ"][2, sl, :] * mz[-1], jnp.where(j > 3, r["RQ"][3, sl, :] * mz[1], 0.0)) * mx[-1]
        hi = jnp.where(j < 2, r["RQ"][4, sl, :] * mz[-1], jnp.where(j > 3, r["RQ"][5, sl, :] * mz[1], 0.0)) * mx[1]
        v = jnp.where((lane >= 6) & (lane < 12), roll(lo, 6 - 102), jnp.where((lane >= 108) & (lane < 114), roll(hi, 108 - 12), v))
        GQ[8 + 8 * h : 16 + 8 * h, :] = jnp.where((lane >= 6) & (lane < 114), v, 0.0)
    for dy, at in ((-1, 7), (1, 24)):
        j = qj(lane[0:1])
        lo = r["RQE"][XY.index((dy, -1))] * (my[dy] * mz[-1])
        hi = r["RQE"][XY.index((dy, 1))] * (my[dy] * mz[1])
        v = jnp.where(j < 2, lo, jnp.where(j > 3, hi, 0.0))
        GQ[at : at + 1, :] = jnp.where((lane[0:1] >= 12) & (lane[0:1] < 108), v, 0.0)

    INJ = r["INJ"]

    def inject(q, xs, tiles):
        for at in tiles:
            m = q[at : at + 8, :]
            for xp in xs:
                a = roll(m, -(6 * xp + 1))
                c = roll(m, 127 - (6 * xp + 4))
                INJ[xp, at : at + 8, :] = jnp.where(lane == 0, a, jnp.where(lane == 127, c, 0.0))

    def sum0(a, x, n, at):
        c = a[x : x + n, at : at + 8, :]
        t = a[x - 1 : x + n - 1, at : at + 8, :] + a[x + 1 : x + n + 1, at : at + 8, :]
        t = t + (a[x : x + n, at - 1 : at + 7, :] + a[x : x + n, at + 1 : at + 9, :])
        z = jnp.where(lane == 0, 0.0, roll(c, 1)) + jnp.where(lane == 127, 0.0, roll(c, -1))
        return c, t + (z + INJ[x : x + n, at : at + 8, :])

    inject(GQ, range(1, 19), (7, 15, 17))
    for at in (7, 15, 17):
        c, t = sum0(G0, 1, 18, at)
        v = S * (1.2 * c + S * t)
        if at == 7:
            v = v * jnp.where(row == 0, my[-1], 1.0)
        if at == 17:
            v = v * jnp.where(row == 7, my[1], 1.0)
        V0[1:19, at : at + 8, :] = v
    V0[1:2, 7:25, :] = V0[1:2, 7:25, :] * mx[-1]
    V0[18:19, 7:25, :] = V0[18:19, 7:25, :] * mx[1]

    for at in (8, 16):
        c = GQ[at : at + 8, :]
        t = roll(c, 1) + roll(c, -1) + roll(c, 6) + roll(c, -6)
        t = t + GQ[at - 1 : at + 7, :] + GQ[at + 1 : at + 9, :]
        j = qj(lane)
        keep = jnp.where(j == 1, mz[-1], jnp.where(j == 4, mz[1], 0.0))
        keep = jnp.where((lane >= 12) & (lane < 108), keep, 0.0)
        VQ[at : at + 8, :] = S * (1.2 * c + S * t) * keep

    inject(VQ, range(2, 18), (8, 16))
    halves = []
    for at in (8, 16):
        c, t = sum0(V0, 2, 16, at)
        halves.append(W0[2:18, at : at + 8, :] * (G0[2:18, at : at + 8, :] - 6.0 * c + t))
    r0 = jnp.concatenate(halves, axis=1)
    g1 = jnp.where(own1, coarsen0(r0, 0.125) * wi1, 0.0)
    send1(g1, "g", 16)

    G1, W1, V1, U1 = r["G1"], r["W1"], r["V1"], r["U1"]
    G2, W2, V2, U2, P2, Q2 = r["G2"], r["W2"], r["V2"], r["U2"], r["P2"], r["Q2"]
    G3, W3, V3, U3, P3 = r["G3"], r["W3"], r["V3"], r["U3"], r["P3"]
    wait_recv(r["RW"], 7)

    def spread(m0, lo, hi, l, m):
        c = jnp.where((l // 32) % 2 == 1, lo * mz[-1], hi * mz[1]) * m
        return m0 * m, c

    def place(m0, c, l, h):
        a = roll(m0, 32 if h == 0 else 96)
        e = roll(c, 96 if h == 0 else 32)
        return jnp.where((l >= 32) & (l < 96), a, e)

    def piece(buf, own, rows, o):
        return own[rows, :] if o == (0, 0, 0) else buf[SLOT[o], rows, :]

    def unpack2(buf, own, dst):
        rows = slice(0, 4)
        for dx in (-1, 0, 1):
            for dy in (-1, 0, 1):
                m0, c = spread(*[piece(buf, own, rows, (dx, dy, dz)) for dz in (0, -1, 1)], lane4, mx[dx] * my[dy])
                for p in range(2):
                    take = lane4 % 2 == p
                    a = jnp.where(take, m0, roll(m0, 1 if p == 0 else -1))
                    e = jnp.where(take, c, roll(c, 1 if p == 0 else -1))
                    for h in range(2):
                        dst[4 + 4 * dx + 2 * h + p, 8 + 4 * dy : 12 + 4 * dy, :] = place(a, e, lane4, h)

    def unpack3(buf, own, rows, dst):
        l = lane[0:2]
        for dx in (-1, 0, 1):
            for dy in (-1, 0, 1):
                m0, c = spread(*[piece(buf, own, rows, (dx, dy, dz)) for dz in (0, -1, 1)], l, mx[dx] * my[dy])
                for h in range(2):
                    dst[4 + 2 * dx + h, 11 + 2 * dy : 13 + 2 * dy, :] = place(m0, c, l, h)

    unpack2(r["RW"], SW, W2)
    unpack3(r["RW"], SW, slice(4, 6), W3)
    r["SX"][0] = W3[6, 8:16, :]
    r["SX"][1] = W3[3, 8:16, :]
    for i in range(8):
        r["SY"][0, i : i + 1, :] = W3[i + 1, 13:14, :]
        r["SY"][1, i : i + 1, :] = W3[i + 1, 10:11, :]
    for i, d in enumerate((-1, 1)):
        send(r["SX"].at[i], r["RSX"].at[1 - i], 20, dev(d, 0, 0))
        send(r["SY"].at[i], r["RSY"].at[1 - i], 21, dev(0, d, 0))

    recv1(w1, "w", 8, W1)
    wait_recv(W0.at[pl.ds(18, 1), gsl], 12)
    wait_recv(W0.at[pl.ds(1, 1), gsl], 13)
    wait_recv(r["RYW"], 14)
    wait_recv(r["RQW"], 15)
    W0[1:2, 8:24, :] = W0[1:2, 8:24, :] * mx[-1]
    W0[18:19, 8:24, :] = W0[18:19, 8:24, :] * mx[1]
    W0[2:18, 7:8, :] = r["RYW"][0] * my[-1]
    W0[2:18, 24:25, :] = r["RYW"][1] * my[1]
    for h in range(2):
        sl = slice(8 * h, 8 * h + 8)
        j = qj(lane)
        v = jnp.where(j == 1, r["RQW"][0, sl, :] * mz[-1], jnp.where(j == 4, r["RQW"][1, sl, :] * mz[1], 0.0))
        r["WQ"][8 + 8 * h : 16 + 8 * h, :] = v

    wait_recv(r["RSX"], 20)
    wait_recv(r["RSY"], 21)
    W3[1, 8:16, :] = r["RSX"][0] * mx[-1]
    W3[8, 8:16, :] = r["RSX"][1] * mx[1]
    for i in range(1, 7):
        W3[i + 1, 8:9, :] = r["RSY"][0, i : i + 1, :] * my[-1]
        W3[i + 1, 15:16, :] = r["RSY"][1, i : i + 1, :] * my[1]

    def inverse(w):
        return jnp.where(w > 0.0, 1.0 / jnp.where(w > 0.0, w, 1.0), 0.0)

    recv1(g1, "g", 16, G1)

    def nsum(a, x, n, at, rows, dil):
        c = a[x : x + n, at : at + rows, :]
        t = a[x - 1 : x + n - 1, at : at + rows, :] + a[x + 1 : x + n + 1, at : at + rows, :]
        t = t + (a[x : x + n, at - 1 : at + rows - 1, :] + a[x : x + n, at + 1 : at + rows + 1, :])
        return c, t + (roll(c, dil) + roll(c, -dil))

    def rowmask(at, rows, low, high):
        y = lax.broadcasted_iota(jnp.int32, (rows, 128), 0) + at
        l = lax.broadcasted_iota(jnp.int32, (rows, 128), 1)
        m = jnp.where(y < low, my[-1], jnp.where(y >= high, my[1], 1.0))
        return m * jnp.where(l < 32, mz[-1], jnp.where(l >= 96, mz[1], 1.0))

    def xmask(a, low, high, x, n, at, rows):
        if low > x:
            a[x:low, at : at + rows, :] = a[x:low, at : at + rows, :] * mx[-1]
        if x + n > high:
            a[high : x + n, at : at + rows, :] = a[high : x + n, at : at + rows, :] * mx[1]

    for at in (4, 12):
        c, t = nsum(G1, 1, 12, at, 8, 1)
        V1[1:13, at : at + 8, :] = S * (1.2 * c + S * t) * rowmask(at, 8, 8, 16)
    xmask(V1, 3, 11, 1, 12, 4, 16)
    c, t = nsum(V1, 3, 8, 8, 8, 1)
    r1 = W1[3:11, 8:16, :] * (G1[3:11, 8:16, :] - 6.0 * c + t)
    g2 = jnp.where(own1[0:4], coarsen1(r1, 0.125) * wi2, 0.0)
    SC = r["SC"]
    SC[...] = pack2(g2)
    send_all(SC, r["RC"], 22)

    P2[4:8, 8:12, :] = g2
    c, t = nsum(P2, 2, 8, 6, 8, 2)
    Q2[2:10, 6:14, :] = S * (1.2 * c + S * t) * rowmask(6, 8, 8, 12)
    xmask(Q2, 4, 8, 2, 8, 6, 8)
    c, t = nsum(Q2, 2, 8, 6, 8, 2)
    res = W2[2:10, 6:14, :] * (P2[2:10, 6:14, :] - 6.0 * c + t)
    C2[...] = jnp.sum(res.reshape(4, 2, 8, 128), axis=1)
    t = C2[:, pl.ds(0, 4, stride=2), :] + C2[:, pl.ds(1, 4, stride=2), :]
    b3 = pair_z(t, 2) * 0.125
    P3[3:7, 10:14, :] = b3 * inverse(W3[3:7, 10:14, :])
    c, t = nsum(P3, 1, 8, 8, 8, 4)
    V3[1:9, 8:16, :] = S * (1.2 * c + S * t) * rowmask(8, 8, 11, 13)
    xmask(V3, 4, 6, 1, 8, 8, 8)
    c, t = nsum(V3, 1, 8, 8, 8, 4)
    res = W3[1:9, 8:16, :] * (P3[1:9, 8:16, :] - 6.0 * c + t)
    T4 = r["T4"]
    T4[0, 8:16, :] = res[0]
    for i in range(3):
        T4[1 + i, 8:16, :] = res[1 + 2 * i] + res[2 + 2 * i]
    T4[4, 8:16, :] = res[7]
    t = T4[:, pl.ds(7, 8, stride=2), :] + T4[:, pl.ds(8, 8, stride=2), :]
    patch = pair_z(t, 4) * 0.125

    msg = zero
    for dx in range(5):
        v = patch[dx]
        main = zero
        for q in range(4):
            lo = 32 + 16 * q + 7
            main = jnp.where((lane >= 2 * q) & (lane < 2 * q + 2), roll(v, 2 * q - lo), main)
        edge = jnp.where(lane < 2, roll(v, 0 - 23), jnp.where(lane < 4, roll(v, 2 - 103), 0.0))
        line = pltpu.roll(main, 0, 1, stride=8, stride_axis=0) + pltpu.roll(edge, 40, 1, stride=4, stride_axis=0)
        line = jnp.sum(line, axis=0, keepdims=True)
        msg = jnp.where(row == ix + (dx - 2), line, msg)
    msg = jnp.where(ih == 1, roll(msg, 64), msg)
    GA, GB, GC = r["GA"], r["GB"], r["GC"]
    SA, SB, SZ = r["SA"], r["SB"], r["SZ"]
    SA[...] = msg
    ga_at = ih * nx + ix
    for d in group_y:
        send(SA, GA.at[ga_at], 23, d)

    wait_recv(GA.at[pl.ds(0, n_y - 1)], 23)
    GA[ga_at] = msg
    SB[...] = jnp.sum(GA[...], axis=0)
    for d in group_x:
        send(SB, GB.at[ixx], 24, d)

    wait_recv(r["RC"], 22)
    unpack2(r["RC"], SC, G2)
    c, t = nsum(G2, 2, 8, 6, 8, 2)
    V2[2:10, 6:14, :] = S * (1.2 * c + S * t) * rowmask(6, 8, 8, 12)
    xmask(V2, 4, 8, 2, 8, 6, 8)
    c, t = nsum(V2, 4, 4, 8, 4, 2)
    res = W2[4:8, 8:12, :] * (G2[4:8, 8:12, :] - 6.0 * c + t)
    C2[0:2, 0:4, :] = jnp.sum(res.reshape(2, 2, 4, 128), axis=1)
    t = C2[0:2, pl.ds(0, 2, stride=2), :] + C2[0:2, pl.ds(1, 2, stride=2), :]
    g3 = jnp.where(own1[0:2], pair_z(t, 2) * 0.125 * wi3, 0.0)
    SD = r["SD"]
    SD[...] = pack3(g3)
    send_all(SD, r["RD"], 25)

    wait_recv(GB.at[pl.ds(0, xn - 1)], 24)
    GB[ixx] = SB[...]
    main = zero
    edges = [zero] * 5
    for k in range(xn):
        v = GB[k]
        for h in range(2):
            if xn == 8 and h == 1:
                continue
            shift = 8 * k - 16 + h * (8 * xn - 64)
            m = roll(v, shift)
            src = (lane - shift + 256) % 128
            if xn != 8:
                m = jnp.where(src // 64 == h, m, 0.0)
            main = main + jnp.where(src % 64 < 40, m, 0.0)
            for dy in range(5):
                a = 40 + 4 * dy
                edges[dy] = edges[dy] + jnp.where((src % 64 >= a) & (src % 64 < a + 4), m, 0.0)
    edge = zero
    for dy in range(5):
        edge = edge + roll(edges[dy], 4 * dy - 40)
    SZ[0] = main
    SZ[1] = edge
    for d in group_z:
        send(SZ, GC.at[iz], 26, d)

    wait_recv(r["RD"], 25)
    unpack3(r["RD"], SD, slice(0, 2), G3)
    c, t = nsum(G3, 4, 2, 11, 2, 4)
    v3 = jnp.where(own1[0:2], S * (1.2 * c + S * t), 0.0)
    SE = r["SE"]
    SE[2:4, :] = pack3(v3)
    SE[1:2, :] = jnp.zeros((1, 128), F32)

    wait_recv(GC.at[pl.ds(0, nz - 1)], 26)
    GC[iz, 0] = SZ[0]
    GC[iz, 1] = SZ[1]
    acc = [zero] * 4
    for z in range(nz):
        v = GC[z, 0]
        if z + 1 < nz:
            v = v + jnp.where(lane % 8 >= 6, roll(GC[z + 1, 1], 6), 0.0)
        if z > 0:
            v = v + jnp.where(lane % 8 < 2, roll(GC[z - 1, 1], -2), 0.0)
        for x in range(nx):
            acc[x % 4] = acc[x % 4] + cp[x * nz + z] * v[x : x + 1, :]
    acc = (acc[0] + acc[1]) + (acc[2] + acc[3])
    tot = jnp.sum(acc, axis=1, keepdims=True)
    e4 = jnp.sum(jnp.where((lane >= 32 + 8 * row) & (lane < 40 + 8 * row), tot, 0.0), axis=0, keepdims=True)
    SE[0:1, :] = e4
    send_all(SE, r["RE"], 27)
    RE = r["RE"]
    wait_recv(RE, 27)

    unpack3(RE, SE, slice(2, 4), V3)
    for x in (1, 8):
        V3[x, 8:16, :] = zero
    for x in range(2, 8):
        V3[x, 8:9, :] = zero[0:1]
        V3[x, 15:16, :] = zero[0:1]
    l1 = lane[0:1]
    par = []
    for dx in (-1, 0, 1):
        v = zero
        for dy in (-1, 0, 1):
            o = (dx, dy, 0)
            own = SE[0:1, :] if o == (0, 0, 0) else RE[SLOT[o], 0:1, :]
            lo, hi = RE[SLOT[(dx, dy, -1)], 0:1, :], RE[SLOT[(dx, dy, 1)], 0:1, :]
            e = jnp.where((l1 >= 32) & (l1 < 96), own, roll(jnp.where(l1 < 64, hi, lo), 64))
            y = 3 + 2 * dy
            v = jnp.where((row == y) | (row == y + 1), e, v)
        par.append(v)
    for i in range(6):
        U3[2 + i, 8:16, :] = V3[2 + i, 8:16, :] + W3[2 + i, 8:16, :] * par[i // 2]
    c, t = nsum(U3, 3, 4, 8, 8, 4)
    E3 = r["E3"]
    E3[...] = (0.2 * c + S * (G3[3:7, 8:16, :] + t)) * inverse(W3[3:7, 8:16, :])
    F2 = r["F2"]
    F2[:, pl.ds(0, 4, stride=2), :] = E3[:, 2:6, :]
    F2[:, pl.ds(1, 4, stride=2), :] = E3[:, 2:6, :]
    for i in range(8):
        U2[2 + i, 6:14, :] = V2[2 + i, 6:14, :] + W2[2 + i, 6:14, :] * F2[i // 2]
    c, t = nsum(U2, 3, 6, 6, 8, 2)
    E2 = r["E2"]
    E2[...] = (0.2 * c + S * (G2[3:9, 6:14, :] + t)) * inverse(W2[3:9, 6:14, :])
    F1 = r["F1"]
    F1[:, pl.ds(2, 6, stride=2), :] = E2[:, 1:7, :]
    F1[:, pl.ds(3, 6, stride=2), :] = E2[:, 1:7, :]
    for i in range(12):
        U1[1 + i, 6:18, :] = V1[1 + i, 6:18, :] + W1[1 + i, 6:18, :] * F1[i // 2, 2:14, :]
    E1 = r["E1"]
    for at in (7, 9):
        c, t = nsum(U1, 2, 10, at, 8, 1)
        E1[:, at - 7 : at + 1, :] = (0.2 * c + S * (G1[2:12, at : at + 8, :] + t)) * inverse(W1[2:12, at : at + 8, :])
    o = select_dot(E1[...].reshape(160, 128), up).reshape(10, 16, 128)
    F0 = r["F0"]
    O1 = r["O1"]
    O1[...] = o
    F0[:, pl.ds(6, 10, stride=2), :] = O1[:, 0:10, :]
    F0[:, pl.ds(7, 10, stride=2), :] = O1[:, 0:10, :]
    acc = zero
    for x in range(8):
        e = E1[x + 1, 1:9, :]
        for p in range(2):
            base = 6 * (2 * x + p + 2)
            acc = jnp.where(lane == base + 1, roll(e, base + 1 - 31), acc)
            acc = jnp.where(lane == base + 4, roll(e, base + 4 - 96), acc)
    UQ = r["UQ"]
    FQ = r["FQ"]
    FQ[...] = acc
    UQ[pl.ds(8, 8, stride=2), :] = FQ[...]
    UQ[pl.ds(9, 8, stride=2), :] = FQ[...]
    UQ[8:24, :] = VQ[8:24, :] + r["WQ"][8:24, :] * UQ[8:24, :]
    for i in range(18):
        V0[1 + i, 7:25, :] = V0[1 + i, 7:25, :] + W0[1 + i, 7:25, :] * F0[(i + 1) // 2, 7:25, :]
    inject(UQ, range(2, 18), (8, 16))
    for at in (8, 16):
        c, t = sum0(V0, 2, 16, at)
        out_ref[:, at - 8 : at, :] = (0.2 * c + S * (G0[2:18, at : at + 8, :] + t)) / w_ref[:, at - 8 : at, :]

    wait_send(G0.at[pl.ds(2, 2), gsl], 0)
    wait_send(G0.at[pl.ds(16, 2), gsl], 1)
    wait_send(r["YS"].at[0], 2)
    wait_send(r["YS"].at[1], 3)
    for name, key in (("RXY", 4), ("RQ", 5), ("RQE", 6), ("RW", 7), ("RYW", 14), ("RQW", 15), ("RSX", 20), ("RSY", 21)):
        wait_send(r[name], key)
    wait_send(W0.at[pl.ds(2, 1), gsl], 12)
    wait_send(W0.at[pl.ds(17, 1), gsl], 13)
    for n, key in (("w", 8), ("g", 16)):
        for i, name in enumerate(("RX1", "RY1", "RXY1", "RZ1")):
            wait_send(r[name + n], key + i)
    wait_send(r["RC"], 22)
    wait_send(GA.at[pl.ds(0, n_y - 1)], 23)
    wait_send(GB.at[pl.ds(0, xn - 1)], 24)
    wait_send(r["RD"], 25)
    wait_send(GC.at[pl.ds(0, nz - 1)], 26)
    wait_send(r["RE"], 27)


def scratch(dims):
    nx, ny, nz = dims
    xn = ny // 2
    v = {
        "G0": (20, 32, 128), "W0": (20, 32, 128), "V0": (20, 32, 128), "INJ": (20, 32, 128),
        "GQ": (32, 128), "VQ": (32, 128), "WQ": (32, 128), "UQ": (32, 128),
        "YS": (2, 16, 2, 128), "RY": (2, 16, 2, 128), "RXY": (4, 2, 128),
        "QS": (16, 128), "QW": (16, 128), "RQ": (6, 16, 128), "QE": (2, 1, 128), "RQE": (4, 1, 128),
        "YW": (2, 16, 1, 128), "RYW": (2, 16, 1, 128), "RQW": (2, 16, 128),
        "C0": (8, 16, 128), "C1": (4, 8, 128), "C2": (4, 8, 128),
        "S1": (8, 8, 128), "SW": (8, 128), "RW": (26, 8, 128),
        "G1": (14, 24, 128), "W1": (14, 24, 128), "V1": (14, 24, 128), "U1": (14, 24, 128),
        "G2": (12, 24, 128), "W2": (12, 24, 128), "V2": (12, 24, 128), "U2": (12, 24, 128),
        "P2": (12, 24, 128), "Q2": (12, 24, 128),
        "G3": (10, 24, 128), "W3": (10, 24, 128), "V3": (10, 24, 128), "U3": (10, 24, 128), "P3": (10, 24, 128),
        "T4": (5, 24, 128), "SX": (2, 8, 128), "SY": (2, 8, 128), "RSX": (2, 8, 128), "RSY": (2, 8, 128),
        "SC": (4, 128), "RC": (26, 4, 128), "SD": (2, 128), "RD": (26, 2, 128), "SE": (4, 128), "RE": (26, 4, 128),
        "SA": (8, 128), "SB": (8, 128), "SZ": (2, 8, 128),
        "GA": (2 * nx, 8, 128), "GB": (xn, 8, 128), "GC": (nz, 2, 8, 128), "CP": (nx * nz, 8, 128),
        "E3": (4, 8, 128), "F2": (4, 8, 128), "E2": (6, 8, 128), "F1": (6, 16, 128),
        "E1": (10, 16, 128), "O1": (10, 16, 128), "F0": (10, 32, 128), "FQ": (8, 128),
    }
    for n in "wg":
        v["S1" + n] = (8, 8, 128)
        v["YS1" + n] = (2, 8, 4, 128)
        v["ZS1" + n] = (8, 128)
        v["RX1" + n] = (2, 3, 8, 128)
        v["RY1" + n] = (2, 8, 4, 128)
        v["RXY1" + n] = (4, 3, 4, 128)
        v["RZ1" + n] = (18, 8, 128)
    return v


def solution(mesh):
    dims = tuple(mesh.shape[a] for a in ("gx", "gy", "gz"))
    sizes = scratch(dims)

    def body(*args):
        names = ["b", "w", "c", "out"] + list(sizes) + ["ssem", "rsem"]
        kernel(dims, dict(zip(names, args)))

    def per_device(sources, stiffness, coarse_inverse):
        vmem = pl.BlockSpec(memory_space=pltpu.VMEM)
        e = pl.pallas_call(
            body,
            out_shape=jax.ShapeDtypeStruct((16, 16, 128), F32),
            in_specs=[vmem] * 3,
            out_specs=vmem,
            scratch_shapes=[pltpu.VMEM(s, F32) for s in sizes.values()] + [pltpu.SemaphoreType.DMA((28,))] * 2,
            compiler_params=pltpu.CompilerParams(collective_id=0, has_side_effects=True),
            name="vcycle",
        )(sources, stiffness, coarse_inverse)
        return e[None]

    return jax.shard_map(
        per_device,
        mesh=mesh,
        in_specs=(P(None, "gx", "gy", "gz"), P("gx", "gy", "gz"), P(("gx", "gy", "gz"), None)),
        out_specs=P(None, "gx", "gy", "gz"),
        check_vma=False,
    )
```

time: 401 us -> 67.6 us (0.17)
  the two profiles are of different devices: /device:TPU:14 before, /device:TPU:1 now
where the time goes in v1:
time: 67.6 us; the launch traced here: 67.4 us
  Pallas kernels  65.8 us (97%)
  local copies, waits for them, and re-layouts  1.57 us (2%)
    pallas_call x1, Pallas kernels, per_device(): pl.pallas_call(body, out_shape=jax.ShapeDtypeStruct((16, 16, 128), F32),...  65.8 us
    unnamed x1, local copies, waits for them, and re-layouts  1.57 us

profile of v1, /device:TPU:1, one launch (start us, length us, event | category | flops | bytes accessed | tf_op | source)
XLA Modules:
  0.0 67.4 jit_solution(9237230890115746930)
XLA Ops:
  0.0 65.8 %vcycle.1 = f32[16,16,128]{2,1,0:T(8,128)} custom-call(f32[1,16,16,128]{3,2,1,0:T(8,128)} %args_0_.4, f32[16,16,128]{2,1,0:T(8,128)} %args_1_.4, f32[8,8192]{1,0:T(8,128)} %args_2_.4), custom_call_target="tpu_custom_call" | custom-call | tf_op jit(solution)/shard_map/vcycle/pallas_call | solution.py:711
  65.8 1.6 %copy.5 = f32[1,16,16,128]{3,2,1,0:T(8,128)} copy(f32[1,16,16,128]{3,2,1,0:T(8,128)} %bitcast.1) | data formatting | bytes 262144

commit v2 on v1

--- a/solution.py
+++ b/solution.py
@@ -53,19 +53,55 @@
             "gz": lax.rem(iz + dz + nz, nz),
         }
 
-    def copy(src, dst, key, device):
-        c = pltpu.make_async_remote_copy(
+    def copy(src, dst, key, slot, device):
+        return pltpu.make_async_remote_copy(
             src_ref=src,
             dst_ref=dst,
-            send_sem=r["ssem"].at[key],
-            recv_sem=r["rsem"].at[key],
+            send_sem=r["ssem"].at[key, slot],
+            recv_sem=r["rsem"].at[key, slot],
             device_id=device,
             device_id_type=MESH,
         )
-        return c
-
-    def send(src, dst, key, device):
-        copy(src, dst, key, device).start()
+
+    cx = {-1: ix > 0, 1: ix < nx - 1}
+    cy = {-1: iy > 0, 1: iy < ny - 1}
+    cz = {-1: iz > 0, 1: iz < nz - 1}
+
+    def has(o):
+        c = [f[v] for f, v in zip((cx, cy, cz), o) if v]
+        return functools.reduce(jnp.logical_and, c)
+
+    def keep(v, *o):
+        return jnp.where(has(o), v, 0.0) if any(o) else v
+
+    sent = []
+
+    def exchange(key, o, src, dst, back):
+        slot = SLOT[o]
+        sent.append((o, src, key, slot))
+
+        @pl.when(has(o))
+        def _():
+            copy(src, dst, key, slot, dev(*o)).start()
+
+        def wait():
+            @pl.when(has(neg(o)))
+            def _():
+                copy(back, back, key, slot, right).wait_recv()
+
+        return wait
+
+    def to_group(key, src, dst, group):
+        for k, d in enumerate(group):
+            copy(src, dst, key, k, d).start()
+
+    def from_group(key, buf, n):
+        for k in range(n):
+            copy(buf.at[0], buf.at[0], key, k, right).wait_recv()
+
+    def run(waits):
+        for w in waits:
+            w()
 
     me = {"gx": ix, "gy": iy, "gz": iz}
     right = {"gx": lax.rem(ix + 1, nx), "gy": iy, "gz": iz}
@@ -78,9 +114,18 @@
     group_z = [{"gx": ix, "gy": iy, "gz": lax.rem(iz + k, nz)} for k in range(1, nz)]
 
     barrier = pltpu.get_barrier_semaphore()
-    partners = [dev(*o) for o in OFFS] + group_y + group_x + group_z
-    for d in partners:
+    loads = [pltpu.make_async_copy(r[a], r[b], r["lsem"].at[i]) for i, (a, b) in enumerate((("b", "B0"), ("w", "A0"), ("c", "CM")))]
+    for c in loads:
+        c.start()
+    for o in OFFS:
+
+        @pl.when(has(o))
+        def _():
+            pl.semaphore_signal(barrier, inc=1, device_id=dev(*o), device_id_type=MESH)
+
+    for d in group_y + group_x + group_z:
         pl.semaphore_signal(barrier, inc=1, device_id=d, device_id_type=MESH)
+    partners = sum(jnp.where(has(o), 1, 0) for o in OFFS) + len(group_y + group_x + group_z)
 
     lane = lax.broadcasted_iota(jnp.int32, (8, 128), 1)
     row = lax.broadcasted_iota(jnp.int32, (8, 128), 0)
@@ -94,15 +139,11 @@
     mz = {-1: flag(iz > 0), 0: jnp.float32(1), 1: flag(iz < nz - 1)}
     zmask = jnp.where(lane < 32, mz[-1], jnp.where(lane >= 96, mz[1], 1.0))
 
-    b_ref, w_ref, c_ref, out_ref = r["b"], r["w"], r["c"], r["out"]
-    for name in ("G0", "W0", "V0"):
-        a = r[name]
-        a[:, 0:8, :] = jnp.zeros((20, 8, 128), F32)
-        a[:, 24:32, :] = jnp.zeros((20, 8, 128), F32)
-    for name in ("GQ", "WQ", "VQ", "UQ", "G1", "W1", "V1", "U1", "G2", "W2", "V2", "U2", "P2", "Q2", "G3", "W3", "V3", "U3", "P3", "T4"):
-        r[name][...] = jnp.zeros(r[name].shape, F32)
+    b_ref, w_ref, c_ref, out_ref = r["B0"], r["A0"], r["CM"], r["out"]
 
     G0, W0, V0 = r["G0"], r["W0"], r["V0"]
+    loads[0].wait()
+    loads[1].wait()
     w0 = w_ref[...]
     g0 = b_ref[0] / w0
     W0[2:18, 8:24, :] = w0
@@ -125,20 +166,32 @@
     r["QE"][0] = r["QS"][0:1, :]
     r["QE"][1] = r["QS"][15:16, :]
 
-    pl.semaphore_wait(barrier, len(partners))
+    pl.semaphore_wait(barrier, partners)
 
     gsl = pl.ds(8, 16)
-    send(G0.at[pl.ds(2, 2), gsl], G0.at[pl.ds(18, 2), gsl], 0, dev(-1, 0, 0))
-    send(G0.at[pl.ds(16, 2), gsl], G0.at[pl.ds(0, 2), gsl], 1, dev(1, 0, 0))
+    wait_g0 = [
+        exchange(0, (-1, 0, 0), G0.at[pl.ds(2, 2), gsl], G0.at[pl.ds(18, 2), gsl], G0.at[pl.ds(18, 2), gsl]),
+        exchange(0, (1, 0, 0), G0.at[pl.ds(16, 2), gsl], G0.at[pl.ds(0, 2), gsl], G0.at[pl.ds(0, 2), gsl]),
+    ]
     for i, d in enumerate((-1, 1)):
-        send(r["YS"].at[i], r["RY"].at[1 - i], 2 + i, dev(0, d, 0))
+        wait_g0.append(exchange(0, (0, d, 0), r["YS"].at[i], r["RY"].at[1 - i], r["RY"].at[1 - i]))
     for dx, dy in XY:
         src = r["YS"].at[(dy + 1) // 2, 0 if dx < 0 else 15]
-        send(src, r["RXY"].at[XY.index((-dx, -dy))], 4, dev(dx, dy, 0))
+        dst = r["RXY"].at[XY.index((-dx, -dy))]
+        wait_g0.append(exchange(0, (dx, dy, 0), src, dst, dst))
     for dx, dz in XZ:
-        send(r["QS"], r["RQ"].at[XZ.index((-dx, -dz))], 5, dev(dx, 0, dz))
+        dst = r["RQ"].at[XZ.index((-dx, -dz))]
+        wait_g0.append(exchange(0, (dx, 0, dz), r["QS"], dst, dst))
     for dy, dz in XY:
-        send(r["QE"].at[(dy + 1) // 2], r["RQE"].at[XY.index((-dy, -dz))], 6, dev(0, dy, dz))
+        dst = r["RQE"].at[XY.index((-dy, -dz))]
+        wait_g0.append(exchange(0, (0, dy, dz), r["QE"].at[(dy + 1) // 2], dst, dst))
+
+    for name in ("G0", "W0", "V0"):
+        a = r[name]
+        a[:, 0:8, :] = jnp.zeros((20, 8, 128), F32)
+        a[:, 24:32, :] = jnp.zeros((20, 8, 128), F32)
+    for name in ("GQ", "WQ", "VQ", "UQ", "G1", "W1", "V1", "U1", "G2", "W2", "V2", "U2", "P2", "Q2", "G3", "W3", "V3", "U3", "P3", "T4"):
+        r[name][...] = jnp.zeros(r[name].shape, F32)
 
     zr = lax.broadcasted_iota(jnp.int32, (256, 128), 0) % 128
     zc = lax.broadcasted_iota(jnp.int32, (256, 128), 1)
@@ -190,16 +243,9 @@
     SW[6:8, :] = jnp.zeros((2, 128), F32)
 
     def send_all(src, dst, key):
-        for o in OFFS:
-            send(src, dst.at[SLOT[neg(o)]], key, dev(*o))
-
-    def wait_recv(dst, key):
-        copy(dst, dst, key, right).wait_recv()
-
-    def wait_send(like, key):
-        copy(like, like, key, right).wait_send()
-
-    send_all(SW, r["RW"], 7)
+        return [exchange(key, o, src, dst.at[SLOT[neg(o)]], dst.at[SLOT[neg(o)]]) for o in OFFS]
+
+    wait_w = send_all(SW, r["RW"], 1)
 
     def send1(own, n, key):
         s1, ys, zs = r["S1" + n], r["YS1" + n], r["ZS1" + n]
@@ -211,19 +257,24 @@
             acc = jnp.where((lane >= 16 * x) & (lane < 16 * x + 4), roll(own[x], 16 * x - 32), acc)
             acc = jnp.where((lane >= 16 * x + 4) & (lane < 16 * x + 8), roll(own[x], 16 * x + 4 - 92), acc)
         zs[...] = acc
-        send(s1.at[pl.ds(0, 3)], r["RX1" + n].at[1], key, dev(-1, 0, 0))
-        send(s1.at[pl.ds(5, 3)], r["RX1" + n].at[0], key, dev(1, 0, 0))
-        send(ys.at[0], r["RY1" + n].at[1], key + 1, dev(0, -1, 0))
-        send(ys.at[1], r["RY1" + n].at[0], key + 1, dev(0, 1, 0))
+        rx, ry, rxy, rz = (r[name + n] for name in ("RX1", "RY1", "RXY1", "RZ1"))
+        waits = [
+            exchange(key, (-1, 0, 0), s1.at[pl.ds(0, 3)], rx.at[1], rx.at[1]),
+            exchange(key, (1, 0, 0), s1.at[pl.ds(5, 3)], rx.at[0], rx.at[0]),
+            exchange(key, (0, -1, 0), ys.at[0], ry.at[1], ry.at[1]),
+            exchange(key, (0, 1, 0), ys.at[1], ry.at[0], ry.at[0]),
+        ]
         for dx, dy in XY:
             src = ys.at[(dy + 1) // 2, pl.ds(0 if dx < 0 else 5, 3)]
-            send(src, r["RXY1" + n].at[XY.index((-dx, -dy))], key + 2, dev(dx, dy, 0))
+            dst = rxy.at[XY.index((-dx, -dy))]
+            waits.append(exchange(key, (dx, dy, 0), src, dst, dst))
         for o in ZOFFS:
-            send(zs, r["RZ1" + n].at[ZSLOT[neg(o)]], key + 3, dev(*o))
+            if n == "g" or 0 in o:
+                waits.append(exchange(key, o, zs, rz.at[ZSLOT[neg(o)]], rz.at[ZSLOT[neg(o)]]))
+        return waits
 
     def recv1(own, n, key, dst):
-        for i, name in enumerate(("RX1", "RY1", "RXY1", "RZ1")):
-            wait_recv(r[name + n], key + i)
+        run(key)
         for x in range(14):
             dx = -1 if x < 3 else (1 if x > 10 else 0)
             for dy in (-1, 0, 1):
@@ -240,57 +291,37 @@
                 lo = r["RZ1" + n][ZSLOT[(dx, dy, -1)], rows, :]
                 hi = r["RZ1" + n][ZSLOT[(dx, dy, 1)], rows, :]
                 ln = lane[0:8] if dy == 0 else lane4
-                v = jnp.where((ln >= 28) & (ln < 32), roll(lo, 28 - 16 * x0(sx) - 4) * mz[-1], base)
-                v = jnp.where((ln >= 96) & (ln < 100), roll(hi, 96 - 16 * x0(sx)) * mz[1], v)
-                if dx != 0 or dy != 0:
-                    v = v * (mx[dx] * my[dy])
+                v = keep(base, dx, dy, 0)
+                if n == "g" or dx == 0 or dy == 0:
+                    v = jnp.where((ln >= 28) & (ln < 32), keep(roll(lo, 28 - 16 * sx - 4), dx, dy, -1), v)
+                    v = jnp.where((ln >= 96) & (ln < 100), keep(roll(hi, 96 - 16 * sx), dx, dy, 1), v)
                 at = 8 if dy == 0 else (4 if dy < 0 else 16)
                 dst[x, at : at + (8 if dy == 0 else 4), :] = v
 
-    def x0(v):
-        return v
-
-    send1(w1, "w", 8)
+    wait_w1 = send1(w1, "w", 2)
 
     r["YW"][0] = W0[2:18, 8:9, :]
     r["YW"][1] = W0[2:18, 23:24, :]
     pack_q(W0, r["QW"])
-    send(W0.at[pl.ds(2, 1), gsl], W0.at[pl.ds(18, 1), gsl], 12, dev(-1, 0, 0))
-    send(W0.at[pl.ds(17, 1), gsl], W0.at[pl.ds(1, 1), gsl], 13, dev(1, 0, 0))
+    wait_w0 = [
+        exchange(3, (-1, 0, 0), W0.at[pl.ds(2, 1), gsl], W0.at[pl.ds(18, 1), gsl], W0.at[pl.ds(18, 1), gsl]),
+        exchange(3, (1, 0, 0), W0.at[pl.ds(17, 1), gsl], W0.at[pl.ds(1, 1), gsl], W0.at[pl.ds(1, 1), gsl]),
+    ]
     for i, d in enumerate((-1, 1)):
-        send(r["YW"].at[i], r["RYW"].at[1 - i], 14, dev(0, d, 0))
-        send(r["QW"], r["RQW"].at[1 - i], 15, dev(0, 0, d))
+        wait_w0.append(exchange(3, (0, d, 0), r["YW"].at[i], r["RYW"].at[1 - i], r["RYW"].at[1 - i]))
+        wait_w0.append(exchange(3, (0, 0, d), r["QW"], r["RQW"].at[1 - i], r["RQW"].at[1 - i]))
 
     wi1 = 1.0 / jnp.where(own1, w1, 1.0)
     wi2 = 1.0 / jnp.where(own1[0:4], w2, 1.0)
-    wi3 = 1.0 / jnp.where(own1[0:2], w3, 1.0)
-
-    cp = r["CP"]
-
-    @pl.loop(0, nx)
-    def _(x):
-        for z in range(nz):
-            acc = zero
-            for p in range(ny // 2):
-                tile = c_ref[:, pl.ds(pl.multiple_of((x * (ny // 2) + p) * 128, 128), 128)]
-                for q in range(2):
-                    y = 2 * p + q
-                    at = 8 * y
-                    acc = jnp.where((lane >= at) & (lane < at + 8), roll(tile, at - 64 * q - 8 * z), acc)
-            cp[x * nz + z] = acc
 
     GQ, VQ = r["GQ"], r["VQ"]
-    for key, dst in ((0, G0.at[pl.ds(18, 2), gsl]), (1, G0.at[pl.ds(0, 2), gsl]), (2, r["RY"].at[1]), (3, r["RY"].at[0])):
-        wait_recv(dst, key)
-    wait_recv(r["RXY"], 4)
-    wait_recv(r["RQ"], 5)
-    wait_recv(r["RQE"], 6)
-    G0[0:2, 8:24, :] = G0[0:2, 8:24, :] * mx[-1]
-    G0[18:20, 8:24, :] = G0[18:20, 8:24, :] * mx[1]
-    G0[2:18, 6:8, :] = r["RY"][0] * my[-1]
-    G0[2:18, 24:26, :] = r["RY"][1] * my[1]
+    run(wait_g0)
+    G0[0:2, 8:24, :] = keep(G0[0:2, 8:24, :], -1, 0, 0)
+    G0[18:20, 8:24, :] = keep(G0[18:20, 8:24, :], 1, 0, 0)
+    G0[2:18, 6:8, :] = keep(r["RY"][0], 0, -1, 0)
+    G0[2:18, 24:26, :] = keep(r["RY"][1], 0, 1, 0)
     for dx, dy in XY:
-        v = r["RXY"][XY.index((dx, dy))] * (mx[dx] * my[dy])
+        v = keep(r["RXY"][XY.index((dx, dy))], dx, dy, 0)
         G0[1 if dx < 0 else 18, 7 if dy < 0 else 24, :] = v[1 if dy < 0 else 0, :]
 
     def qj(ln):
@@ -300,15 +331,14 @@
         sl = slice(8 * h, 8 * h + 8)
         own = r["QS"][sl, :]
         j = qj(lane)
-        v = jnp.where(j < 2, r["RQ"][0, sl, :] * mz[-1], jnp.where(j > 3, r["RQ"][1, sl, :] * mz[1], own))
-        lo = jnp.where(j < 2, r["RQ"][2, sl, :] * mz[-1], jnp.where(j > 3, r["RQ"][3, sl, :] * mz[1], 0.0)) * mx[-1]
-        hi = jnp.where(j < 2, r["RQ"][4, sl, :] * mz[-1], jnp.where(j > 3, r["RQ"][5, sl, :] * mz[1], 0.0)) * mx[1]
+        q = [keep(r["RQ"][i, sl, :], dx, 0, dz) for i, (dx, dz) in enumerate(XZ)]
+        v, lo, hi = (jnp.where(j < 2, q[2 * i], jnp.where(j > 3, q[2 * i + 1], own if i == 0 else 0.0)) for i in range(3))
         v = jnp.where((lane >= 6) & (lane < 12), roll(lo, 6 - 102), jnp.where((lane >= 108) & (lane < 114), roll(hi, 108 - 12), v))
         GQ[8 + 8 * h : 16 + 8 * h, :] = jnp.where((lane >= 6) & (lane < 114), v, 0.0)
     for dy, at in ((-1, 7), (1, 24)):
         j = qj(lane[0:1])
-        lo = r["RQE"][XY.index((dy, -1))] * (my[dy] * mz[-1])
-        hi = r["RQE"][XY.index((dy, 1))] * (my[dy] * mz[1])
+        lo = keep(r["RQE"][XY.index((dy, -1))], 0, dy, -1)
+        hi = keep(r["RQE"][XY.index((dy, 1))], 0, dy, 1)
         v = jnp.where(j < 2, lo, jnp.where(j > 3, hi, 0.0))
         GQ[at : at + 1, :] = jnp.where((lane[0:1] >= 12) & (lane[0:1] < 108), v, 0.0)
 
@@ -346,9 +376,9 @@
         t = roll(c, 1) + roll(c, -1) + roll(c, 6) + roll(c, -6)
         t = t + GQ[at - 1 : at + 7, :] + GQ[at + 1 : at + 9, :]
         j = qj(lane)
-        keep = jnp.where(j == 1, mz[-1], jnp.where(j == 4, mz[1], 0.0))
-        keep = jnp.where((lane >= 12) & (lane < 108), keep, 0.0)
-        VQ[at : at + 8, :] = S * (1.2 * c + S * t) * keep
+        mask = jnp.where(j == 1, mz[-1], jnp.where(j == 4, mz[1], 0.0))
+        mask = jnp.where((lane >= 12) & (lane < 108), mask, 0.0)
+        VQ[at : at + 8, :] = S * (1.2 * c + S * t) * mask
 
     inject(VQ, range(2, 18), (8, 16))
     halves = []
@@ -357,16 +387,15 @@
         halves.append(W0[2:18, at : at + 8, :] * (G0[2:18, at : at + 8, :] - 6.0 * c + t))
     r0 = jnp.concatenate(halves, axis=1)
     g1 = jnp.where(own1, coarsen0(r0, 0.125) * wi1, 0.0)
-    send1(g1, "g", 16)
+    wait_g1 = send1(g1, "g", 4)
 
     G1, W1, V1, U1 = r["G1"], r["W1"], r["V1"], r["U1"]
     G2, W2, V2, U2, P2, Q2 = r["G2"], r["W2"], r["V2"], r["U2"], r["P2"], r["Q2"]
     G3, W3, V3, U3, P3 = r["G3"], r["W3"], r["V3"], r["U3"], r["P3"]
-    wait_recv(r["RW"], 7)
-
-    def spread(m0, lo, hi, l, m):
-        c = jnp.where((l // 32) % 2 == 1, lo * mz[-1], hi * mz[1]) * m
-        return m0 * m, c
+    run(wait_w)
+
+    def spread(m0, lo, hi, l, dx, dy):
+        return keep(m0, dx, dy, 0), jnp.where((l // 32) % 2 == 1, keep(lo, dx, dy, -1), keep(hi, dx, dy, 1))
 
     def place(m0, c, l, h):
         a = roll(m0, 32 if h == 0 else 96)
@@ -380,7 +409,7 @@
         rows = slice(0, 4)
         for dx in (-1, 0, 1):
             for dy in (-1, 0, 1):
-                m0, c = spread(*[piece(buf, own, rows, (dx, dy, dz)) for dz in (0, -1, 1)], lane4, mx[dx] * my[dy])
+                m0, c = spread(*[piece(buf, own, rows, (dx, dy, dz)) for dz in (0, -1, 1)], lane4, dx, dy)
                 for p in range(2):
                     take = lane4 % 2 == p
                     a = jnp.where(take, m0, roll(m0, 1 if p == 0 else -1))
@@ -392,7 +421,7 @@
         l = lane[0:2]
         for dx in (-1, 0, 1):
             for dy in (-1, 0, 1):
-                m0, c = spread(*[piece(buf, own, rows, (dx, dy, dz)) for dz in (0, -1, 1)], l, mx[dx] * my[dy])
+                m0, c = spread(*[piece(buf, own, rows, (dx, dy, dz)) for dz in (0, -1, 1)], l, dx, dy)
                 for h in range(2):
                     dst[4 + 2 * dx + h, 11 + 2 * dy : 13 + 2 * dy, :] = place(m0, c, l, h)
 
@@ -403,37 +432,27 @@
     for i in range(8):
         r["SY"][0, i : i + 1, :] = W3[i + 1, 13:14, :]
         r["SY"][1, i : i + 1, :] = W3[i + 1, 10:11, :]
+    wait_s = []
     for i, d in enumerate((-1, 1)):
-        send(r["SX"].at[i], r["RSX"].at[1 - i], 20, dev(d, 0, 0))
-        send(r["SY"].at[i], r["RSY"].at[1 - i], 21, dev(0, d, 0))
-
-    recv1(w1, "w", 8, W1)
-    wait_recv(W0.at[pl.ds(18, 1), gsl], 12)
-    wait_recv(W0.at[pl.ds(1, 1), gsl], 13)
-    wait_recv(r["RYW"], 14)
-    wait_recv(r["RQW"], 15)
-    W0[1:2, 8:24, :] = W0[1:2, 8:24, :] * mx[-1]
-    W0[18:19, 8:24, :] = W0[18:19, 8:24, :] * mx[1]
-    W0[2:18, 7:8, :] = r["RYW"][0] * my[-1]
-    W0[2:18, 24:25, :] = r["RYW"][1] * my[1]
+        wait_s.append(exchange(5, (d, 0, 0), r["SX"].at[i], r["RSX"].at[1 - i], r["RSX"].at[1 - i]))
+        wait_s.append(exchange(5, (0, d, 0), r["SY"].at[i], r["RSY"].at[1 - i], r["RSY"].at[1 - i]))
+
+    recv1(w1, "w", wait_w1, W1)
+    run(wait_w0)
+    W0[1:2, 8:24, :] = keep(W0[1:2, 8:24, :], -1, 0, 0)
+    W0[18:19, 8:24, :] = keep(W0[18:19, 8:24, :], 1, 0, 0)
+    W0[2:18, 7:8, :] = keep(r["RYW"][0], 0, -1, 0)
+    W0[2:18, 24:25, :] = keep(r["RYW"][1], 0, 1, 0)
     for h in range(2):
         sl = slice(8 * h, 8 * h + 8)
         j = qj(lane)
-        v = jnp.where(j == 1, r["RQW"][0, sl, :] * mz[-1], jnp.where(j == 4, r["RQW"][1, sl, :] * mz[1], 0.0))
+        v = jnp.where(j == 1, keep(r["RQW"][0, sl, :], 0, 0, -1), jnp.where(j == 4, keep(r["RQW"][1, sl, :], 0, 0, 1), 0.0))
         r["WQ"][8 + 8 * h : 16 + 8 * h, :] = v
-
-    wait_recv(r["RSX"], 20)
-    wait_recv(r["RSY"], 21)
-    W3[1, 8:16, :] = r["RSX"][0] * mx[-1]
-    W3[8, 8:16, :] = r["RSX"][1] * mx[1]
-    for i in range(1, 7):
-        W3[i + 1, 8:9, :] = r["RSY"][0, i : i + 1, :] * my[-1]
-        W3[i + 1, 15:16, :] = r["RSY"][1, i : i + 1, :] * my[1]
 
     def inverse(w):
         return jnp.where(w > 0.0, 1.0 / jnp.where(w > 0.0, w, 1.0), 0.0)
 
-    recv1(g1, "g", 16, G1)
+    recv1(g1, "g", wait_g1, G1)
 
     def nsum(a, x, n, at, rows, dil):
         c = a[x : x + n, at : at + rows, :]
@@ -460,9 +479,6 @@
     c, t = nsum(V1, 3, 8, 8, 8, 1)
     r1 = W1[3:11, 8:16, :] * (G1[3:11, 8:16, :] - 6.0 * c + t)
     g2 = jnp.where(own1[0:4], coarsen1(r1, 0.125) * wi2, 0.0)
-    SC = r["SC"]
-    SC[...] = pack2(g2)
-    send_all(SC, r["RC"], 22)
 
     P2[4:8, 8:12, :] = g2
     c, t = nsum(P2, 2, 8, 6, 8, 2)
@@ -473,6 +489,17 @@
     C2[...] = jnp.sum(res.reshape(4, 2, 8, 128), axis=1)
     t = C2[:, pl.ds(0, 4, stride=2), :] + C2[:, pl.ds(1, 4, stride=2), :]
     b3 = pair_z(t, 2) * 0.125
+    SC = r["SC"]
+    SC[0:4, :] = pack2(g2)
+    l4 = lane4 % 4
+    SC[4:8, :] = jnp.where(l4 < 2, jnp.where(l4 == 0, b3[0], b3[1]), jnp.where(l4 == 2, b3[2], b3[3]))
+    wait_c = send_all(SC, r["RC"], 6)
+    run(wait_s)
+    W3[1, 8:16, :] = keep(r["RSX"][0], -1, 0, 0)
+    W3[8, 8:16, :] = keep(r["RSX"][1], 1, 0, 0)
+    for i in range(1, 7):
+        W3[i + 1, 8:9, :] = keep(r["RSY"][0, i : i + 1, :], 0, -1, 0)
+        W3[i + 1, 15:16, :] = keep(r["RSY"][1, i : i + 1, :], 0, 1, 0)
     P3[3:7, 10:14, :] = b3 * inverse(W3[3:7, 10:14, :])
     c, t = nsum(P3, 1, 8, 8, 8, 4)
     V3[1:9, 8:16, :] = S * (1.2 * c + S * t) * rowmask(8, 8, 11, 13)
@@ -503,30 +530,29 @@
     SA, SB, SZ = r["SA"], r["SB"], r["SZ"]
     SA[...] = msg
     ga_at = ih * nx + ix
-    for d in group_y:
-        send(SA, GA.at[ga_at], 23, d)
-
-    wait_recv(GA.at[pl.ds(0, n_y - 1)], 23)
+    to_group(8, SA, GA.at[ga_at], group_y)
+
+    cp = r["CP"]
+    loads[2].wait()
+
+    @pl.loop(0, nx)
+    def _(x):
+        for z in range(nz):
+            acc = zero
+            for p in range(ny // 2):
+                tile = c_ref[:, pl.ds(pl.multiple_of((x * (ny // 2) + p) * 128, 128), 128)]
+                for q in range(2):
+                    y = 2 * p + q
+                    at = 8 * y
+                    acc = jnp.where((lane >= at) & (lane < at + 8), roll(tile, at - 64 * q - 8 * z), acc)
+            cp[x * nz + z] = acc
+
+    from_group(8, GA, n_y - 1)
     GA[ga_at] = msg
     SB[...] = jnp.sum(GA[...], axis=0)
-    for d in group_x:
-        send(SB, GB.at[ixx], 24, d)
-
-    wait_recv(r["RC"], 22)
-    unpack2(r["RC"], SC, G2)
-    c, t = nsum(G2, 2, 8, 6, 8, 2)
-    V2[2:10, 6:14, :] = S * (1.2 * c + S * t) * rowmask(6, 8, 8, 12)
-    xmask(V2, 4, 8, 2, 8, 6, 8)
-    c, t = nsum(V2, 4, 4, 8, 4, 2)
-    res = W2[4:8, 8:12, :] * (G2[4:8, 8:12, :] - 6.0 * c + t)
-    C2[0:2, 0:4, :] = jnp.sum(res.reshape(2, 2, 4, 128), axis=1)
-    t = C2[0:2, pl.ds(0, 2, stride=2), :] + C2[0:2, pl.ds(1, 2, stride=2), :]
-    g3 = jnp.where(own1[0:2], pair_z(t, 2) * 0.125 * wi3, 0.0)
-    SD = r["SD"]
-    SD[...] = pack3(g3)
-    send_all(SD, r["RD"], 25)
-
-    wait_recv(GB.at[pl.ds(0, xn - 1)], 24)
+    to_group(9, SB, GB.at[ixx], group_x)
+
+    from_group(9, GB, xn - 1)
     GB[ixx] = SB[...]
     main = zero
     edges = [zero] * 5
@@ -549,18 +575,41 @@
         edge = edge + roll(edges[dy], 4 * dy - 40)
     SZ[0] = main
     SZ[1] = edge
-    for d in group_z:
-        send(SZ, GC.at[iz], 26, d)
-
-    wait_recv(r["RD"], 25)
-    unpack3(r["RD"], SD, slice(0, 2), G3)
+    to_group(10, SZ, GC.at[iz], group_z)
+
+    run(wait_c)
+    unpack2(r["RC"], SC, G2)
+    c, t = nsum(G2, 2, 8, 6, 8, 2)
+    V2[2:10, 6:14, :] = S * (1.2 * c + S * t) * rowmask(6, 8, 8, 12)
+    xmask(V2, 4, 8, 2, 8, 6, 8)
+
+    TB, TC, RC = r["TB"], r["TC"], r["RC"]
+    for dy in (-1, 0, 1):
+        acc = jnp.zeros((4, 128), F32)
+        for dx in (-1, 0, 1):
+            m0, lo, hi = (keep(piece(RC, SC, slice(4, 8), (dx, dy, dz)), dx, dy, dz) for dz in (0, -1, 1))
+            e = jnp.where((lane4 >= 92) & (lane4 < 100), lo, jnp.where((lane4 >= 28) & (lane4 < 36), hi, 0.0))
+            q = m0 + roll(e, 64)
+            if dx < 0:
+                q = jnp.where(l4 < 2, roll(q, -2), 0.0)
+            if dx > 0:
+                q = jnp.where(l4 >= 2, roll(q, 2), 0.0)
+            acc = acc + q
+        TB[dy + 1] = acc
+    TC[0:2, :] = TB[1, 0:2, :] + TB[0, 2:4, :]
+    TC[2:4, :] = TB[1, 2:4, :] + TB[2, 0:2, :]
+    for i in range(4):
+        v = roll(jnp.where(l4 == i, TC[...], 0.0), -i)
+        v = v + roll(v, 1)
+        v = v + roll(v, 2)
+        G3[3 + i, 10:14, :] = v * inverse(W3[3 + i, 10:14, :])
     c, t = nsum(G3, 4, 2, 11, 2, 4)
     v3 = jnp.where(own1[0:2], S * (1.2 * c + S * t), 0.0)
     SE = r["SE"]
     SE[2:4, :] = pack3(v3)
     SE[1:2, :] = jnp.zeros((1, 128), F32)
 
-    wait_recv(GC.at[pl.ds(0, nz - 1)], 26)
+    from_group(10, GC, nz - 1)
     GC[iz, 0] = SZ[0]
     GC[iz, 1] = SZ[1]
     acc = [zero] * 4
@@ -576,9 +625,8 @@
     tot = jnp.sum(acc, axis=1, keepdims=True)
     e4 = jnp.sum(jnp.where((lane >= 32 + 8 * row) & (lane < 40 + 8 * row), tot, 0.0), axis=0, keepdims=True)
     SE[0:1, :] = e4
-    send_all(SE, r["RE"], 27)
     RE = r["RE"]
-    wait_recv(RE, 27)
+    run(send_all(SE, RE, 7))
 
     unpack3(RE, SE, slice(2, 4), V3)
     for x in (1, 8):
@@ -592,8 +640,8 @@
         v = zero
         for dy in (-1, 0, 1):
             o = (dx, dy, 0)
-            own = SE[0:1, :] if o == (0, 0, 0) else RE[SLOT[o], 0:1, :]
-            lo, hi = RE[SLOT[(dx, dy, -1)], 0:1, :], RE[SLOT[(dx, dy, 1)], 0:1, :]
+            own = SE[0:1, :] if o == (0, 0, 0) else keep(RE[SLOT[o], 0:1, :], *o)
+            lo, hi = (keep(RE[SLOT[(dx, dy, dz)], 0:1, :], dx, dy, dz) for dz in (-1, 1))
             e = jnp.where((l1 >= 32) & (l1 < 96), own, roll(jnp.where(l1 < 64, hi, lo), 64))
             y = 3 + 2 * dy
             v = jnp.where((row == y) | (row == y + 1), e, v)
@@ -644,31 +692,25 @@
     inject(UQ, range(2, 18), (8, 16))
     for at in (8, 16):
         c, t = sum0(V0, 2, 16, at)
-        out_ref[:, at - 8 : at, :] = (0.2 * c + S * (G0[2:18, at : at + 8, :] + t)) / w_ref[:, at - 8 : at, :]
-
-    wait_send(G0.at[pl.ds(2, 2), gsl], 0)
-    wait_send(G0.at[pl.ds(16, 2), gsl], 1)
-    wait_send(r["YS"].at[0], 2)
-    wait_send(r["YS"].at[1], 3)
-    for name, key in (("RXY", 4), ("RQ", 5), ("RQE", 6), ("RW", 7), ("RYW", 14), ("RQW", 15), ("RSX", 20), ("RSY", 21)):
-        wait_send(r[name], key)
-    wait_send(W0.at[pl.ds(2, 1), gsl], 12)
-    wait_send(W0.at[pl.ds(17, 1), gsl], 13)
-    for n, key in (("w", 8), ("g", 16)):
-        for i, name in enumerate(("RX1", "RY1", "RXY1", "RZ1")):
-            wait_send(r[name + n], key + i)
-    wait_send(r["RC"], 22)
-    wait_send(GA.at[pl.ds(0, n_y - 1)], 23)
-    wait_send(GB.at[pl.ds(0, xn - 1)], 24)
-    wait_send(r["RD"], 25)
-    wait_send(GC.at[pl.ds(0, nz - 1)], 26)
-    wait_send(r["RE"], 27)
+        out_ref[:, at - 8 : at, :] = 0.2 * c + S * (G0[2:18, at : at + 8, :] + t)
+
+    def drain(o, src, key, slot):
+        @pl.when(has(o))
+        def _():
+            copy(src, src, key, slot, right).wait_send()
+
+    for item in sent:
+        drain(*item)
+    for key, src, n in ((8, SA, n_y - 1), (9, SB, xn - 1), (10, SZ, nz - 1)):
+        for k in range(n):
+            copy(src, src, key, k, right).wait_send()
 
 
 def scratch(dims):
     nx, ny, nz = dims
     xn = ny // 2
     v = {
+        "B0": (1, 16, 16, 128), "A0": (16, 16, 128), "CM": (8, nx * ny * nz * 8),
         "G0": (20, 32, 128), "W0": (20, 32, 128), "V0": (20, 32, 128), "INJ": (20, 32, 128),
         "GQ": (32, 128), "VQ": (32, 128), "WQ": (32, 128), "UQ": (32, 128),
         "YS": (2, 16, 2, 128), "RY": (2, 16, 2, 128), "RXY": (4, 2, 128),
@@ -681,7 +723,7 @@
         "P2": (12, 24, 128), "Q2": (12, 24, 128),
         "G3": (10, 24, 128), "W3": (10, 24, 128), "V3": (10, 24, 128), "U3": (10, 24, 128), "P3": (10, 24, 128),
         "T4": (5, 24, 128), "SX": (2, 8, 128), "SY": (2, 8, 128), "RSX": (2, 8, 128), "RSY": (2, 8, 128),
-        "SC": (4, 128), "RC": (26, 4, 128), "SD": (2, 128), "RD": (26, 2, 128), "SE": (4, 128), "RE": (26, 4, 128),
+        "SC": (8, 128), "RC": (26, 8, 128), "TB": (3, 4, 128), "TC": (4, 128), "SE": (4, 128), "RE": (26, 4, 128),
         "SA": (8, 128), "SB": (8, 128), "SZ": (2, 8, 128),
         "GA": (2 * nx, 8, 128), "GB": (xn, 8, 128), "GC": (nz, 2, 8, 128), "CP": (nx * nz, 8, 128),
         "E3": (4, 8, 128), "F2": (4, 8, 128), "E2": (6, 8, 128), "F1": (6, 16, 128),
@@ -703,7 +745,7 @@
     sizes = scratch(dims)
 
     def body(*args):
-        names = ["b", "w", "c", "out"] + list(sizes) + ["ssem", "rsem"]
+        names = ["b", "w", "c", "out"] + list(sizes) + ["ssem", "rsem", "lsem"]
         kernel(dims, dict(zip(names, args)))
 
     def per_device(sources, stiffness, coarse_inverse):
@@ -711,13 +753,13 @@
         e = pl.pallas_call(
             body,
             out_shape=jax.ShapeDtypeStruct((16, 16, 128), F32),
-            in_specs=[vmem] * 3,
+            in_specs=[pl.BlockSpec(memory_space=pltpu.HBM)] * 3,
             out_specs=vmem,
-            scratch_shapes=[pltpu.VMEM(s, F32) for s in sizes.values()] + [pltpu.SemaphoreType.DMA((28,))] * 2,
-            compiler_params=pltpu.CompilerParams(collective_id=0, has_side_effects=True),
+            scratch_shapes=[pltpu.VMEM(s, F32) for s in sizes.values()] + [pltpu.SemaphoreType.DMA((11, 26))] * 2 + [pltpu.SemaphoreType.DMA((3,))],
+            compiler_params=pltpu.CompilerParams(collective_id=0, has_side_effects=True, vmem_limit_bytes=24 * 2**20),
             name="vcycle",
-        )(sources, stiffness, coarse_inverse)
-        return e[None]
+        )(*[pltpu.with_memory_space_constraint(a, pltpu.HBM) for a in (sources, stiffness, coarse_inverse)])
+        return (e / stiffness)[None]
 
     return jax.shard_map(
         per_device,

time: 67.6 us -> 63.9 us (0.945)
  the two profiles are of different devices: /device:TPU:1 before, /device:TPU:7 now
where the time goes in v2:
time: 63.9 us; the launch traced here: 63.7 us
  Pallas kernels  63 us (99%)
  other arithmetic  0.68 us (1%)
    pallas_call x1, Pallas kernels, per_device(): pl.pallas_call(body, out_shape=jax.ShapeDtypeStruct((16, 16, 128), F32),...  63 us

profile of v2, /device:TPU:7, one launch (start us, length us, event | category | flops | bytes accessed | tf_op | source)
XLA Modules:
  0.0 63.7 jit_solution(9319341029617845927)
XLA Ops:
  0.0 0.0 copy-start
  0.0 63.0 %vcycle.1 = f32[16,16,128]{2,1,0:T(8,128)S(1)} custom-call(f32[1,16,16,128]{3,2,1,0:T(8,128)} %args_0_.4, f32[16,16,128]{2,1,0:T(8,128)} %args_1_.4, f32[8,8192]{1,0:T(8,128)} %args_2_.4), custom_call_target="tpu_custom_call" | custom-call | tf_op jit(solution)/shard_map/vcycle/pallas_call | solution.py:753
  63.1 0.0 copy-done
  63.1 0.7 %divide_bitcast_fusion = f32[1,16,16,128]{3,2,1,0:T(8,128)} fusion(f32[16,16,128]{2,1,0:T(8,128)S(1)} %vcycle.1, f32[16,16,128]{2,1,0:T(8,128)S(1)} %copy-done), kind=kLoop, calls=%fused_computation | loop fusion | flops 32768 | bytes 393216 | tf_op jit(solution)/shard_map/broadcast_in_dim | solution.py:762
Async XLA Ops:
  0.0 63.1 %copy-start = (f32[16,16,128]{2,1,0:T(8,128)S(1)}, f32[16,16,128]{2,1,0:T(8,128)}, u32[]{:S(2)}) copy-start(f32[16,16,128]{2,1,0:T(8,128)} %args_1_.4) | copy-start | bytes 393220

commit v3 on v2

--- a/solution.py
+++ b/solution.py
@@ -53,12 +53,12 @@
             "gz": lax.rem(iz + dz + nz, nz),
         }
 
-    def copy(src, dst, key, slot, device):
+    def copy(src, dst, key, device):
         return pltpu.make_async_remote_copy(
             src_ref=src,
             dst_ref=dst,
-            send_sem=r["ssem"].at[key, slot],
-            recv_sem=r["rsem"].at[key, slot],
+            send_sem=r["ssem"].at[key],
+            recv_sem=r["rsem"].at[key],
             device_id=device,
             device_id_type=MESH,
         )
@@ -76,28 +76,39 @@
 
     sent = []
 
-    def exchange(key, o, src, dst, back):
-        slot = SLOT[o]
-        sent.append((o, src, key, slot))
-
-        @pl.when(has(o))
-        def _():
-            copy(src, dst, key, slot, dev(*o)).start()
+    def round_of(key, items, slots):
+        for o, src, dst in items:
+
+            @pl.when(has(o))
+            def _():
+                copy(src, dst, key, dev(*o)).start()
+
+        offs = [o for o, _, _ in items]
+        count = sum(jnp.where(has(o), 1, 0) for o in offs)
+        sizes = set()
+        for ends in itertools.product((((-1, 1), (-1,), (1,), ())), repeat=3):
+            sizes.add(sum(all(v == 0 or v in e for v, e in zip(o, ends)) for o in offs))
+        sizes = sorted(n for n in sizes if n)
+        sent.append((key, slots, count, sizes))
 
         def wait():
-            @pl.when(has(neg(o)))
-            def _():
-                copy(back, back, key, slot, right).wait_recv()
+            for n in sizes:
+
+                @pl.when(count == n)
+                def _():
+                    copy(slots(n), slots(n), key, right).wait_recv()
 
         return wait
 
+    def first(ref):
+        return lambda n: ref.at[pl.ds(0, n)]
+
     def to_group(key, src, dst, group):
-        for k, d in enumerate(group):
-            copy(src, dst, key, k, d).start()
+        for d in group:
+            copy(src, dst, key, d).start()
 
     def from_group(key, buf, n):
-        for k in range(n):
-            copy(buf.at[0], buf.at[0], key, k, right).wait_recv()
+        copy(buf.at[pl.ds(0, n)], buf.at[pl.ds(0, n)], key, right).wait_recv()
 
     def run(waits):
         for w in waits:
@@ -170,21 +181,30 @@
 
     gsl = pl.ds(8, 16)
     wait_g0 = [
-        exchange(0, (-1, 0, 0), G0.at[pl.ds(2, 2), gsl], G0.at[pl.ds(18, 2), gsl], G0.at[pl.ds(18, 2), gsl]),
-        exchange(0, (1, 0, 0), G0.at[pl.ds(16, 2), gsl], G0.at[pl.ds(0, 2), gsl], G0.at[pl.ds(0, 2), gsl]),
+        round_of(
+            0,
+            [
+                ((-1, 0, 0), G0.at[pl.ds(2, 2), gsl], G0.at[pl.ds(18, 2), gsl]),
+                ((1, 0, 0), G0.at[pl.ds(16, 2), gsl], G0.at[pl.ds(0, 2), gsl]),
+            ],
+            lambda n: G0.at[pl.ds(0, 2 * n), gsl],
+        ),
+        round_of(1, [((0, d, 0), r["YS"].at[i], r["RY"].at[1 - i]) for i, d in enumerate((-1, 1))], first(r["RY"])),
+        round_of(
+            2,
+            [
+                ((dx, dy, 0), r["YS"].at[(dy + 1) // 2, 0 if dx < 0 else 15], r["RXY"].at[XY.index((-dx, -dy))])
+                for dx, dy in XY
+            ],
+            first(r["RXY"]),
+        ),
+        round_of(3, [((dx, 0, dz), r["QS"], r["RQ"].at[XZ.index((-dx, -dz))]) for dx, dz in XZ], first(r["RQ"])),
+        round_of(
+            4,
+            [((0, dy, dz), r["QE"].at[(dy + 1) // 2], r["RQE"].at[XY.index((-dy, -dz))]) for dy, dz in XY],
+            first(r["RQE"]),
+        ),
     ]
-    for i, d in enumerate((-1, 1)):
-        wait_g0.append(exchange(0, (0, d, 0), r["YS"].at[i], r["RY"].at[1 - i], r["RY"].at[1 - i]))
-    for dx, dy in XY:
-        src = r["YS"].at[(dy + 1) // 2, 0 if dx < 0 else 15]
-        dst = r["RXY"].at[XY.index((-dx, -dy))]
-        wait_g0.append(exchange(0, (dx, dy, 0), src, dst, dst))
-    for dx, dz in XZ:
-        dst = r["RQ"].at[XZ.index((-dx, -dz))]
-        wait_g0.append(exchange(0, (dx, 0, dz), r["QS"], dst, dst))
-    for dy, dz in XY:
-        dst = r["RQE"].at[XY.index((-dy, -dz))]
-        wait_g0.append(exchange(0, (0, dy, dz), r["QE"].at[(dy + 1) // 2], dst, dst))
 
     for name in ("G0", "W0", "V0"):
         a = r[name]
@@ -243,9 +263,9 @@
     SW[6:8, :] = jnp.zeros((2, 128), F32)
 
     def send_all(src, dst, key):
-        return [exchange(key, o, src, dst.at[SLOT[neg(o)]], dst.at[SLOT[neg(o)]]) for o in OFFS]
-
-    wait_w = send_all(SW, r["RW"], 1)
+        return [round_of(key, [(o, src, dst.at[SLOT[neg(o)]]) for o in OFFS], first(dst))]
+
+    wait_w = send_all(SW, r["RW"], 5)
 
     def send1(own, n, key):
         s1, ys, zs = r["S1" + n], r["YS1" + n], r["ZS1" + n]
@@ -258,20 +278,24 @@
             acc = jnp.where((lane >= 16 * x + 4) & (lane < 16 * x + 8), roll(own[x], 16 * x + 4 - 92), acc)
         zs[...] = acc
         rx, ry, rxy, rz = (r[name + n] for name in ("RX1", "RY1", "RXY1", "RZ1"))
-        waits = [
-            exchange(key, (-1, 0, 0), s1.at[pl.ds(0, 3)], rx.at[1], rx.at[1]),
-            exchange(key, (1, 0, 0), s1.at[pl.ds(5, 3)], rx.at[0], rx.at[0]),
-            exchange(key, (0, -1, 0), ys.at[0], ry.at[1], ry.at[1]),
-            exchange(key, (0, 1, 0), ys.at[1], ry.at[0], ry.at[0]),
+        zo = [o for o in ZOFFS if n == "g" or 0 in o]
+        return [
+            round_of(
+                key,
+                [((-1, 0, 0), s1.at[pl.ds(0, 3)], rx.at[1]), ((1, 0, 0), s1.at[pl.ds(5, 3)], rx.at[0])],
+                first(rx),
+            ),
+            round_of(key + 1, [((0, -1, 0), ys.at[0], ry.at[1]), ((0, 1, 0), ys.at[1], ry.at[0])], first(ry)),
+            round_of(
+                key + 2,
+                [
+                    ((dx, dy, 0), ys.at[(dy + 1) // 2, pl.ds(0 if dx < 0 else 5, 3)], rxy.at[XY.index((-dx, -dy))])
+                    for dx, dy in XY
+                ],
+                first(rxy),
+            ),
+            round_of(key + 3, [(o, zs, rz.at[ZSLOT[neg(o)]]) for o in zo], first(rz)),
         ]
-        for dx, dy in XY:
-            src = ys.at[(dy + 1) // 2, pl.ds(0 if dx < 0 else 5, 3)]
-            dst = rxy.at[XY.index((-dx, -dy))]
-            waits.append(exchange(key, (dx, dy, 0), src, dst, dst))
-        for o in ZOFFS:
-            if n == "g" or 0 in o:
-                waits.append(exchange(key, o, zs, rz.at[ZSLOT[neg(o)]], rz.at[ZSLOT[neg(o)]]))
-        return waits
 
     def recv1(own, n, key, dst):
         run(key)
@@ -298,18 +322,23 @@
                 at = 8 if dy == 0 else (4 if dy < 0 else 16)
                 dst[x, at : at + (8 if dy == 0 else 4), :] = v
 
-    wait_w1 = send1(w1, "w", 2)
+    wait_w1 = send1(w1, "w", 6)
 
     r["YW"][0] = W0[2:18, 8:9, :]
     r["YW"][1] = W0[2:18, 23:24, :]
     pack_q(W0, r["QW"])
     wait_w0 = [
-        exchange(3, (-1, 0, 0), W0.at[pl.ds(2, 1), gsl], W0.at[pl.ds(18, 1), gsl], W0.at[pl.ds(18, 1), gsl]),
-        exchange(3, (1, 0, 0), W0.at[pl.ds(17, 1), gsl], W0.at[pl.ds(1, 1), gsl], W0.at[pl.ds(1, 1), gsl]),
+        round_of(
+            14,
+            [
+                ((-1, 0, 0), W0.at[pl.ds(2, 1), gsl], W0.at[pl.ds(18, 1), gsl]),
+                ((1, 0, 0), W0.at[pl.ds(17, 1), gsl], W0.at[pl.ds(1, 1), gsl]),
+            ],
+            lambda n: W0.at[pl.ds(0, n), gsl],
+        ),
+        round_of(15, [((0, d, 0), r["YW"].at[i], r["RYW"].at[1 - i]) for i, d in enumerate((-1, 1))], first(r["RYW"])),
+        round_of(16, [((0, 0, d), r["QW"], r["RQW"].at[1 - i]) for i, d in enumerate((-1, 1))], first(r["RQW"])),
     ]
-    for i, d in enumerate((-1, 1)):
-        wait_w0.append(exchange(3, (0, d, 0), r["YW"].at[i], r["RYW"].at[1 - i], r["RYW"].at[1 - i]))
-        wait_w0.append(exchange(3, (0, 0, d), r["QW"], r["RQW"].at[1 - i], r["RQW"].at[1 - i]))
 
     wi1 = 1.0 / jnp.where(own1, w1, 1.0)
     wi2 = 1.0 / jnp.where(own1[0:4], w2, 1.0)
@@ -387,7 +416,7 @@
         halves.append(W0[2:18, at : at + 8, :] * (G0[2:18, at : at + 8, :] - 6.0 * c + t))
     r0 = jnp.concatenate(halves, axis=1)
     g1 = jnp.where(own1, coarsen0(r0, 0.125) * wi1, 0.0)
-    wait_g1 = send1(g1, "g", 4)
+    wait_g1 = send1(g1, "g", 10)
 
     G1, W1, V1, U1 = r["G1"], r["W1"], r["V1"], r["U1"]
     G2, W2, V2, U2, P2, Q2 = r["G2"], r["W2"], r["V2"], r["U2"], r["P2"], r["Q2"]
@@ -432,10 +461,10 @@
     for i in range(8):
         r["SY"][0, i : i + 1, :] = W3[i + 1, 13:14, :]
         r["SY"][1, i : i + 1, :] = W3[i + 1, 10:11, :]
-    wait_s = []
-    for i, d in enumerate((-1, 1)):
-        wait_s.append(exchange(5, (d, 0, 0), r["SX"].at[i], r["RSX"].at[1 - i], r["RSX"].at[1 - i]))
-        wait_s.append(exchange(5, (0, d, 0), r["SY"].at[i], r["RSY"].at[1 - i], r["RSY"].at[1 - i]))
+    wait_s = [
+        round_of(17, [((d, 0, 0), r["SX"].at[i], r["RSX"].at[1 - i]) for i, d in enumerate((-1, 1))], first(r["RSX"])),
+        round_of(18, [((0, d, 0), r["SY"].at[i], r["RSY"].at[1 - i]) for i, d in enumerate((-1, 1))], first(r["RSY"])),
+    ]
 
     recv1(w1, "w", wait_w1, W1)
     run(wait_w0)
@@ -493,7 +522,7 @@
     SC[0:4, :] = pack2(g2)
     l4 = lane4 % 4
     SC[4:8, :] = jnp.where(l4 < 2, jnp.where(l4 == 0, b3[0], b3[1]), jnp.where(l4 == 2, b3[2], b3[3]))
-    wait_c = send_all(SC, r["RC"], 6)
+    wait_c = send_all(SC, r["RC"], 19)
     run(wait_s)
     W3[1, 8:16, :] = keep(r["RSX"][0], -1, 0, 0)
     W3[8, 8:16, :] = keep(r["RSX"][1], 1, 0, 0)
@@ -530,7 +559,7 @@
     SA, SB, SZ = r["SA"], r["SB"], r["SZ"]
     SA[...] = msg
     ga_at = ih * nx + ix
-    to_group(8, SA, GA.at[ga_at], group_y)
+    to_group(21, SA, GA.at[ga_at], group_y)
 
     cp = r["CP"]
     loads[2].wait()
@@ -547,12 +576,12 @@
                     acc = jnp.where((lane >= at) & (lane < at + 8), roll(tile, at - 64 * q - 8 * z), acc)
             cp[x * nz + z] = acc
 
-    from_group(8, GA, n_y - 1)
+    from_group(21, GA, n_y - 1)
     GA[ga_at] = msg
     SB[...] = jnp.sum(GA[...], axis=0)
-    to_group(9, SB, GB.at[ixx], group_x)
-
-    from_group(9, GB, xn - 1)
+    to_group(22, SB, GB.at[ixx], group_x)
+
+    from_group(22, GB, xn - 1)
     GB[ixx] = SB[...]
     main = zero
     edges = [zero] * 5
@@ -575,7 +604,7 @@
         edge = edge + roll(edges[dy], 4 * dy - 40)
     SZ[0] = main
     SZ[1] = edge
-    to_group(10, SZ, GC.at[iz], group_z)
+    to_group(23, SZ, GC.at[iz], group_z)
 
     run(wait_c)
     unpack2(r["RC"], SC, G2)
@@ -609,7 +638,7 @@
     SE[2:4, :] = pack3(v3)
     SE[1:2, :] = jnp.zeros((1, 128), F32)
 
-    from_group(10, GC, nz - 1)
+    from_group(23, GC, nz - 1)
     GC[iz, 0] = SZ[0]
     GC[iz, 1] = SZ[1]
     acc = [zero] * 4
@@ -626,7 +655,7 @@
     e4 = jnp.sum(jnp.where((lane >= 32 + 8 * row) & (lane < 40 + 8 * row), tot, 0.0), axis=0, keepdims=True)
     SE[0:1, :] = e4
     RE = r["RE"]
-    run(send_all(SE, RE, 7))
+    run(send_all(SE, RE, 20))
 
     unpack3(RE, SE, slice(2, 4), V3)
     for x in (1, 8):
@@ -694,16 +723,17 @@
         c, t = sum0(V0, 2, 16, at)
         out_ref[:, at - 8 : at, :] = 0.2 * c + S * (G0[2:18, at : at + 8, :] + t)
 
-    def drain(o, src, key, slot):
-        @pl.when(has(o))
-        def _():
-            copy(src, src, key, slot, right).wait_send()
+    def drain(key, slots, count, sizes):
+        for n in sizes:
+
+            @pl.when(count == n)
+            def _():
+                copy(slots(n), slots(n), key, right).wait_send()
 
     for item in sent:
         drain(*item)
-    for key, src, n in ((8, SA, n_y - 1), (9, SB, xn - 1), (10, SZ, nz - 1)):
-        for k in range(n):
-            copy(src, src, key, k, right).wait_send()
+    for key, buf, n in ((21, GA, n_y - 1), (22, GB, xn - 1), (23, GC, nz - 1)):
+        copy(buf.at[pl.ds(0, n)], buf.at[pl.ds(0, n)], key, right).wait_send()
 
 
 def scratch(dims):
@@ -755,7 +785,7 @@
             out_shape=jax.ShapeDtypeStruct((16, 16, 128), F32),
             in_specs=[pl.BlockSpec(memory_space=pltpu.HBM)] * 3,
             out_specs=vmem,
-            scratch_shapes=[pltpu.VMEM(s, F32) for s in sizes.values()] + [pltpu.SemaphoreType.DMA((11, 26))] * 2 + [pltpu.SemaphoreType.DMA((3,))],
+            scratch_shapes=[pltpu.VMEM(s, F32) for s in sizes.values()] + [pltpu.SemaphoreType.DMA((24,))] * 2 + [pltpu.SemaphoreType.DMA((3,))],
             compiler_params=pltpu.CompilerParams(collective_id=0, has_side_effects=True, vmem_limit_bytes=24 * 2**20),
             name="vcycle",
         )(*[pltpu.with_memory_space_constraint(a, pltpu.HBM) for a in (sources, stiffness, coarse_inverse)])

time: 63.9 us -> 59 us (0.923)
  Pallas kernels: 63 us -> 58.1 us
    pallas_call x1, Pallas kernels: 63 us -> 58.1 us  [per_device(): pl.pallas_call(body, out_shape=jax.ShapeDtypeStruct((16, 16, 128), F32),...]
where the time goes in v3:
time: 59 us; the launch traced here: 58.8 us
  Pallas kernels  58.1 us (98%)
  other arithmetic  0.68 us (1%)
    pallas_call x1, Pallas kernels, per_device(): pl.pallas_call(body, out_shape=jax.ShapeDtypeStruct((16, 16, 128), F32),...  58.1 us

profile of v3, /device:TPU:7, one launch (start us, length us, event | category | flops | bytes accessed | tf_op | source)
XLA Modules:
  0.0 58.8 jit_solution(15350285911012012271)
XLA Ops:
  0.0 0.0 copy-start
  0.0 58.1 %vcycle.1 = f32[16,16,128]{2,1,0:T(8,128)S(1)} custom-call(f32[1,16,16,128]{3,2,1,0:T(8,128)} %args_0_.4, f32[16,16,128]{2,1,0:T(8,128)} %args_1_.4, f32[8,8192]{1,0:T(8,128)} %args_2_.4), custom_call_target="tpu_custom_call" | custom-call | tf_op jit(solution)/shard_map/vcycle/pallas_call | solution.py:783
  58.2 0.0 copy-done
  58.2 0.7 %divide_bitcast_fusion = f32[1,16,16,128]{3,2,1,0:T(8,128)} fusion(f32[16,16,128]{2,1,0:T(8,128)S(1)} %vcycle.1, f32[16,16,128]{2,1,0:T(8,128)S(1)} %copy-done), kind=kLoop, calls=%fused_computation | loop fusion | flops 32768 | bytes 393216 | tf_op jit(solution)/shard_map/broadcast_in_dim | solution.py:792
Async XLA Ops:
  0.0 58.2 %copy-start = (f32[16,16,128]{2,1,0:T(8,128)S(1)}, f32[16,16,128]{2,1,0:T(8,128)}, u32[]{:S(2)}) copy-start(f32[16,16,128]{2,1,0:T(8,128)} %args_1_.4) | copy-start | bytes 393220

commit v4 on v3

--- a/solution.py
+++ b/solution.py
@@ -12,6 +12,10 @@
 F32 = jnp.float32
 S = 0.8 / 6.0
 OFFS = [o for o in itertools.product((-1, 0, 1), repeat=3) if o != (0, 0, 0)]
+OFFS.sort(key=lambda o: (-abs(o[1]), -abs(o[2]), -abs(o[0])))
+OFF2X = [(2 * a, b, c) for a in (-1, 1) for b in (-1, 0, 1) for c in (-1, 0, 1)]
+OFF2Y = [(b, 2 * a, c) for a in (-1, 1) for b in (-1, 0, 1) for c in (-1, 0, 1)]
+FLAT = [o for o in OFFS if o[2] == 0]
 SLOT = {o: i for i, o in enumerate(OFFS)}
 ZOFFS = [o for o in OFFS if o[2] != 0]
 ZSLOT = {o: i for i, o in enumerate(ZOFFS)}
@@ -63,8 +67,8 @@
             device_id_type=MESH,
         )
 
-    cx = {-1: ix > 0, 1: ix < nx - 1}
-    cy = {-1: iy > 0, 1: iy < ny - 1}
+    cx = {-2: ix > 1, -1: ix > 0, 1: ix < nx - 1, 2: ix < nx - 2}
+    cy = {-2: iy > 1, -1: iy > 0, 1: iy < ny - 1, 2: iy < ny - 2}
     cz = {-1: iz > 0, 1: iz < nz - 1}
 
     def has(o):
@@ -85,9 +89,8 @@
 
         offs = [o for o, _, _ in items]
         count = sum(jnp.where(has(o), 1, 0) for o in offs)
-        sizes = set()
-        for ends in itertools.product((((-1, 1), (-1,), (1,), ())), repeat=3):
-            sizes.add(sum(all(v == 0 or v in e for v, e in zip(o, ends)) for o in offs))
+        spots = [sorted({0, 1, 2, n - 3, n - 2, n - 1} & set(range(n))) for n in dims]
+        sizes = {sum(all(0 <= v + p < n for v, p, n in zip(o, at, dims)) for o in offs) for at in itertools.product(*spots)}
         sizes = sorted(n for n in sizes if n)
         sent.append((key, slots, count, sizes))
 
@@ -128,7 +131,7 @@
     loads = [pltpu.make_async_copy(r[a], r[b], r["lsem"].at[i]) for i, (a, b) in enumerate((("b", "B0"), ("w", "A0"), ("c", "CM")))]
     for c in loads:
         c.start()
-    for o in OFFS:
+    for o in OFFS + OFF2X + OFF2Y:
 
         @pl.when(has(o))
         def _():
@@ -136,7 +139,7 @@
 
     for d in group_y + group_x + group_z:
         pl.semaphore_signal(barrier, inc=1, device_id=d, device_id_type=MESH)
-    partners = sum(jnp.where(has(o), 1, 0) for o in OFFS) + len(group_y + group_x + group_z)
+    partners = sum(jnp.where(has(o), 1, 0) for o in OFFS + OFF2X + OFF2Y) + len(group_y + group_x + group_z)
 
     lane = lax.broadcasted_iota(jnp.int32, (8, 128), 1)
     row = lax.broadcasted_iota(jnp.int32, (8, 128), 0)
@@ -148,7 +151,6 @@
     mx = {-1: flag(ix > 0), 0: jnp.float32(1), 1: flag(ix < nx - 1)}
     my = {-1: flag(iy > 0), 0: jnp.float32(1), 1: flag(iy < ny - 1)}
     mz = {-1: flag(iz > 0), 0: jnp.float32(1), 1: flag(iz < nz - 1)}
-    zmask = jnp.where(lane < 32, mz[-1], jnp.where(lane >= 96, mz[1], 1.0))
 
     b_ref, w_ref, c_ref, out_ref = r["B0"], r["A0"], r["CM"], r["out"]
 
@@ -210,7 +212,7 @@
         a = r[name]
         a[:, 0:8, :] = jnp.zeros((20, 8, 128), F32)
         a[:, 24:32, :] = jnp.zeros((20, 8, 128), F32)
-    for name in ("GQ", "WQ", "VQ", "UQ", "G1", "W1", "V1", "U1", "G2", "W2", "V2", "U2", "P2", "Q2", "G3", "W3", "V3", "U3", "P3", "T4"):
+    for name in ("GQ", "WQ", "VQ", "UQ", "G1", "W1", "V1", "U1", "G2", "W2", "V2", "U2", "P2", "Q2", "G3", "W3", "V3", "U3", "P3", "T4", "A1", "Q1", "R2", "PT", "QT", "Q3"):
         r[name][...] = jnp.zeros(r[name].shape, F32)
 
     zr = lax.broadcasted_iota(jnp.int32, (256, 128), 0) % 128
@@ -237,7 +239,6 @@
         t = C1[:, pl.ds(0, 4, stride=2), :] + C1[:, pl.ds(1, 4, stride=2), :]
         return pair_z(t, 1) * scale
 
-    S1 = r["S1"]
     w1 = coarsen0(w0, 0.0625)
     own1 = (lane >= 32) & (lane < 96)
     w2 = coarsen1(w1, 0.0625)
@@ -257,28 +258,86 @@
     def pack3(v):
         return jnp.where(lane[0:2] < 64, roll(v[0], -32), roll(v[1], 32))
 
-    SW = r["SW"]
-    SW[0:4, :] = pack2(w2)
-    SW[4:6, :] = pack3(w3)
-    SW[6:8, :] = jnp.zeros((2, 128), F32)
+    SW2, SW3, SWZ = r["SW2"], r["SW3"], r["SWZ"]
+    p2 = pack2(w2)
+    SW2[...] = p2
+    SW3[...] = pack3(w3)
+    zp = jnp.zeros((4, 128), F32)
+    for h in range(2):
+        zp = jnp.where((lane4 >= 16 * h) & (lane4 < 16 * h + 8), roll(p2, -48 * h), zp)
+        zp = jnp.where((lane4 >= 16 * h + 8) & (lane4 < 16 * h + 16), roll(p2, -48 * h - 48), zp)
+    row4 = row[0:4]
+    SWZ[...] = sum(roll(jnp.sum(jnp.where(row4 == y, zp, 0.0), axis=0, keepdims=True), 32 * y) for y in range(4))
 
     def send_all(src, dst, key):
         return [round_of(key, [(o, src, dst.at[SLOT[neg(o)]]) for o in OFFS], first(dst))]
 
-    wait_w = send_all(SW, r["RW"], 5)
+    def pack_z1(own, zs):
+        acc = zero
+        for x in range(8):
+            acc = jnp.where((lane >= 16 * x) & (lane < 16 * x + 4), roll(own[x], 16 * x - 32), acc)
+            acc = jnp.where((lane >= 16 * x + 4) & (lane < 16 * x + 8), roll(own[x], 16 * x + 4 - 92), acc)
+        zs[...] = acc
+
+    s1w, ysw, zsw, yzw = r["S1w"], r["YS1w"], r["ZS1w"], r["YZ1w"]
+    s1w[...] = w1
+    ysw[0] = s1w[:, 0:2, :]
+    ysw[1] = s1w[:, 6:8, :]
+    pack_z1(w1, zsw)
+    yzw[0] = zsw[0:2, :]
+    yzw[1] = zsw[6:8, :]
+    RX, RY, RXY, RZ, RYZ = (r[name + "w"] for name in ("RX1", "RY1", "RXY1", "RZ1", "RYZ1"))
+    wait_w = [
+        round_of(7, [((0, -1, 0), ysw.at[0], RY.at[1]), ((0, 1, 0), ysw.at[1], RY.at[0])], first(RY)),
+        round_of(
+            8,
+            [
+                ((dx, dy, 0), ysw.at[(dy + 1) // 2, 0 if dx < 0 else 7], RXY.at[XY.index((-dx, -dy))])
+                for dx, dy in XY
+            ],
+            first(RXY),
+        ),
+        round_of(
+            27,
+            [((0, dy, dz), yzw.at[(dy + 1) // 2], RYZ.at[XY.index((-dy, -dz))]) for dy, dz in XY],
+            first(RYZ),
+        ),
+        round_of(5, [(o, SW2, r["RW2"].at[FLAT.index(neg(o))]) for o in FLAT], first(r["RW2"])),
+        round_of(17, [(o, SWZ, r["RWZ"].at[ZSLOT[neg(o)]]) for o in ZOFFS], first(r["RWZ"])),
+        round_of(18, [(o, SW3, r["RW3"].at[SLOT[neg(o)]]) for o in OFFS], first(r["RW3"])),
+        round_of(25, [(o, SW3, r["RW3Y"].at[OFF2Y.index(neg(o))]) for o in OFF2Y], first(r["RW3Y"])),
+        round_of(24, [(o, SW3, r["RW3X"].at[OFF2X.index(neg(o))]) for o in OFF2X], first(r["RW3X"])),
+        round_of(6, [((-1, 0, 0), s1w.at[pl.ds(0, 2)], RX.at[1]), ((1, 0, 0), s1w.at[pl.ds(6, 2)], RX.at[0])], first(RX)),
+        round_of(9, [((dx, 0, dz), zsw, RZ.at[XZ.index((-dx, -dz))]) for dx, dz in XZ], first(RZ)),
+    ]
+
+    def recv1w(dst):
+        for x in range(1, 13):
+            dx = -1 if x < 3 else (1 if x > 10 else 0)
+            sx = x - 3 if dx == 0 else (x + 5 if dx < 0 else x - 11)
+
+            def ends(v, ln, lo, hi, dx, dy):
+                v = jnp.where((ln >= 28) & (ln < 32), keep(roll(lo, 28 - 16 * sx - 4), dx, dy, -1), v)
+                return jnp.where((ln >= 96) & (ln < 100), keep(roll(hi, 96 - 16 * sx), dx, dy, 1), v)
+
+            base = w1[x - 3] if dx == 0 else keep(RX[(dx + 1) // 2, x - 1 if dx < 0 else x - 11], dx, 0, 0)
+            lo, hi = (RZ[XZ.index((dx, dz))] for dz in (-1, 1))
+            dst[x, 8:16, :] = ends(base, lane, lo, hi, dx, 0)
+            for dy, at in ((-1, 6), (1, 16)):
+                if dx == 0:
+                    lo, hi = (RYZ[XY.index((dy, dz))] for dz in (-1, 1))
+                    v = keep(RY[(dy + 1) // 2, x - 3], 0, dy, 0)
+                    dst[x, at : at + 2, :] = ends(v, lane[0:2], lo, hi, 0, dy)
+                elif x in (2, 11):
+                    dst[x, at : at + 2, :] = keep(RXY[XY.index((dx, dy))], dx, dy, 0)
 
     def send1(own, n, key):
         s1, ys, zs = r["S1" + n], r["YS1" + n], r["ZS1" + n]
         s1[...] = own
         ys[0] = s1[:, 0:4, :]
         ys[1] = s1[:, 4:8, :]
-        acc = zero
-        for x in range(8):
-            acc = jnp.where((lane >= 16 * x) & (lane < 16 * x + 4), roll(own[x], 16 * x - 32), acc)
-            acc = jnp.where((lane >= 16 * x + 4) & (lane < 16 * x + 8), roll(own[x], 16 * x + 4 - 92), acc)
-        zs[...] = acc
+        pack_z1(own, zs)
         rx, ry, rxy, rz = (r[name + n] for name in ("RX1", "RY1", "RXY1", "RZ1"))
-        zo = [o for o in ZOFFS if n == "g" or 0 in o]
         return [
             round_of(
                 key,
@@ -294,7 +353,7 @@
                 ],
                 first(rxy),
             ),
-            round_of(key + 3, [(o, zs, rz.at[ZSLOT[neg(o)]]) for o in zo], first(rz)),
+            round_of(key + 3, [(o, zs, rz.at[ZSLOT[neg(o)]]) for o in ZOFFS], first(rz)),
         ]
 
     def recv1(own, n, key, dst):
@@ -316,13 +375,10 @@
                 hi = r["RZ1" + n][ZSLOT[(dx, dy, 1)], rows, :]
                 ln = lane[0:8] if dy == 0 else lane4
                 v = keep(base, dx, dy, 0)
-                if n == "g" or dx == 0 or dy == 0:
-                    v = jnp.where((ln >= 28) & (ln < 32), keep(roll(lo, 28 - 16 * sx - 4), dx, dy, -1), v)
-                    v = jnp.where((ln >= 96) & (ln < 100), keep(roll(hi, 96 - 16 * sx), dx, dy, 1), v)
+                v = jnp.where((ln >= 28) & (ln < 32), keep(roll(lo, 28 - 16 * sx - 4), dx, dy, -1), v)
+                v = jnp.where((ln >= 96) & (ln < 100), keep(roll(hi, 96 - 16 * sx), dx, dy, 1), v)
                 at = 8 if dy == 0 else (4 if dy < 0 else 16)
                 dst[x, at : at + (8 if dy == 0 else 4), :] = v
-
-    wait_w1 = send1(w1, "w", 6)
 
     r["YW"][0] = W0[2:18, 8:9, :]
     r["YW"][1] = W0[2:18, 23:24, :]
@@ -422,6 +478,7 @@
     G2, W2, V2, U2, P2, Q2 = r["G2"], r["W2"], r["V2"], r["U2"], r["P2"], r["Q2"]
     G3, W3, V3, U3, P3 = r["G3"], r["W3"], r["V3"], r["U3"], r["P3"]
     run(wait_w)
+    recv1w(W1)
 
     def spread(m0, lo, hi, l, dx, dy):
         return keep(m0, dx, dy, 0), jnp.where((l // 32) % 2 == 1, keep(lo, dx, dy, -1), keep(hi, dx, dy, 1))
@@ -439,49 +496,50 @@
         for dx in (-1, 0, 1):
             for dy in (-1, 0, 1):
                 m0, c = spread(*[piece(buf, own, rows, (dx, dy, dz)) for dz in (0, -1, 1)], lane4, dx, dy)
-                for p in range(2):
-                    take = lane4 % 2 == p
-                    a = jnp.where(take, m0, roll(m0, 1 if p == 0 else -1))
-                    e = jnp.where(take, c, roll(c, 1 if p == 0 else -1))
-                    for h in range(2):
-                        dst[4 + 4 * dx + 2 * h + p, 8 + 4 * dy : 12 + 4 * dy, :] = place(a, e, lane4, h)
-
-    def unpack3(buf, own, rows, dst):
+                spread2(m0, c, dst, dx, dy)
+
+    def spread2(m0, c, dst, dx, dy):
+        for p in range(2):
+            take = lane4 % 2 == p
+            a = jnp.where(take, m0, roll(m0, 1 if p == 0 else -1))
+            e = jnp.where(take, c, roll(c, 1 if p == 0 else -1))
+            for h in range(2):
+                dst[4 + 4 * dx + 2 * h + p, 8 + 4 * dy : 12 + 4 * dy, :] = place(a, e, lane4, h)
+
+    def unpack3(get, spots, dst):
         l = lane[0:2]
-        for dx in (-1, 0, 1):
-            for dy in (-1, 0, 1):
-                m0, c = spread(*[piece(buf, own, rows, (dx, dy, dz)) for dz in (0, -1, 1)], l, dx, dy)
-                for h in range(2):
-                    dst[4 + 2 * dx + h, 11 + 2 * dy : 13 + 2 * dy, :] = place(m0, c, l, h)
-
-    unpack2(r["RW"], SW, W2)
-    unpack3(r["RW"], SW, slice(4, 6), W3)
-    r["SX"][0] = W3[6, 8:16, :]
-    r["SX"][1] = W3[3, 8:16, :]
-    for i in range(8):
-        r["SY"][0, i : i + 1, :] = W3[i + 1, 13:14, :]
-        r["SY"][1, i : i + 1, :] = W3[i + 1, 10:11, :]
-    wait_s = [
-        round_of(17, [((d, 0, 0), r["SX"].at[i], r["RSX"].at[1 - i]) for i, d in enumerate((-1, 1))], first(r["RSX"])),
-        round_of(18, [((0, d, 0), r["SY"].at[i], r["RSY"].at[1 - i]) for i, d in enumerate((-1, 1))], first(r["RSY"])),
-    ]
-
-    recv1(w1, "w", wait_w1, W1)
-    run(wait_w0)
-    W0[1:2, 8:24, :] = keep(W0[1:2, 8:24, :], -1, 0, 0)
-    W0[18:19, 8:24, :] = keep(W0[18:19, 8:24, :], 1, 0, 0)
-    W0[2:18, 7:8, :] = keep(r["RYW"][0], 0, -1, 0)
-    W0[2:18, 24:25, :] = keep(r["RYW"][1], 0, 1, 0)
-    for h in range(2):
-        sl = slice(8 * h, 8 * h + 8)
-        j = qj(lane)
-        v = jnp.where(j == 1, keep(r["RQW"][0, sl, :], 0, 0, -1), jnp.where(j == 4, keep(r["RQW"][1, sl, :], 0, 0, 1), 0.0))
-        r["WQ"][8 + 8 * h : 16 + 8 * h, :] = v
+        for dx, dy in spots:
+            m0, c = spread(*[get((dx, dy, dz)) for dz in (0, -1, 1)], l, dx, dy)
+            for h in range(2):
+                dst[5 + 2 * dx + h, 12 + 2 * dy : 14 + 2 * dy, :] = place(m0, c, l, h)
+
+    for dx in (-1, 0, 1):
+        for dy in (-1, 0, 1):
+            m0 = keep(SW2[...] if dx == dy == 0 else r["RW2"][FLAT.index((dx, dy, 0))], dx, dy, 0)
+            lo, hi = (keep(r["RWZ"][ZSLOT[(dx, dy, dz)]], dx, dy, dz) for dz in (-1, 1))
+            line = jnp.where(lane[0:1] % 16 >= 8, lo, hi)
+            e = jnp.zeros((4, 128), F32)
+            for y in range(4):
+                e = jnp.where(row4 == y, roll(line, -32 * y), e)
+            c = jnp.zeros((4, 128), F32)
+            for h in range(2):
+                c = jnp.where((lane4 >= 64 * h) & (lane4 < 64 * h + 8), roll(e, 48 * h), c)
+                c = jnp.where((lane4 >= 64 * h + 56) & (lane4 < 64 * h + 64), roll(e, 48 * h + 48), c)
+            spread2(m0, c, W2, dx, dy)
+
+    def piece3(o):
+        if o == (0, 0, 0):
+            return SW3[...]
+        if abs(o[0]) == 2:
+            return r["RW3X"][OFF2X.index(o)]
+        if abs(o[1]) == 2:
+            return r["RW3Y"][OFF2Y.index(o)]
+        return r["RW3"][SLOT[o]]
+
+    unpack3(piece3, [(a, b) for a in range(-2, 3) for b in range(-2, 3) if abs(a) < 2 or abs(b) < 2], W3)
 
     def inverse(w):
         return jnp.where(w > 0.0, 1.0 / jnp.where(w > 0.0, w, 1.0), 0.0)
-
-    recv1(g1, "g", wait_g1, G1)
 
     def nsum(a, x, n, at, rows, dil):
         c = a[x : x + n, at : at + rows, :]
@@ -501,49 +559,41 @@
         if x + n > high:
             a[high : x + n, at : at + rows, :] = a[high : x + n, at : at + rows, :] * mx[1]
 
+    A1, Q1, R2, PT, QT, Q3 = r["A1"], r["Q1"], r["R2"], r["PT"], r["QT"], r["Q3"]
+    A1[3:11, 8:16, :] = g1
     for at in (4, 12):
-        c, t = nsum(G1, 1, 12, at, 8, 1)
-        V1[1:13, at : at + 8, :] = S * (1.2 * c + S * t) * rowmask(at, 8, 8, 16)
-    xmask(V1, 3, 11, 1, 12, 4, 16)
-    c, t = nsum(V1, 3, 8, 8, 8, 1)
-    r1 = W1[3:11, 8:16, :] * (G1[3:11, 8:16, :] - 6.0 * c + t)
-    g2 = jnp.where(own1[0:4], coarsen1(r1, 0.125) * wi2, 0.0)
-
-    P2[4:8, 8:12, :] = g2
+        c, t = nsum(A1, 1, 12, at, 8, 1)
+        Q1[1:13, at : at + 8, :] = S * (1.2 * c + S * t) * rowmask(at, 8, 8, 16)
+    xmask(Q1, 3, 11, 1, 12, 4, 16)
+    C3 = r["C3"]
+    for at in (6, 10):
+        c, t = nsum(Q1, 1, 12, at, 8, 1)
+        res = W1[1:13, at : at + 8, :] * (A1[1:13, at : at + 8, :] - 6.0 * c + t)
+        C3[:, at - 6 : at + 2, :] = jnp.sum(res.reshape(6, 2, 8, 128), axis=1)
+    t = C3[:, pl.ds(0, 6, stride=2), :] + C3[:, pl.ds(1, 6, stride=2), :]
+    P2[3:9, 7:13, :] = pair_z(t, 1) * 0.125 * inverse(W2[3:9, 7:13, :])
     c, t = nsum(P2, 2, 8, 6, 8, 2)
     Q2[2:10, 6:14, :] = S * (1.2 * c + S * t) * rowmask(6, 8, 8, 12)
     xmask(Q2, 4, 8, 2, 8, 6, 8)
-    c, t = nsum(Q2, 2, 8, 6, 8, 2)
-    res = W2[2:10, 6:14, :] * (P2[2:10, 6:14, :] - 6.0 * c + t)
-    C2[...] = jnp.sum(res.reshape(4, 2, 8, 128), axis=1)
-    t = C2[:, pl.ds(0, 4, stride=2), :] + C2[:, pl.ds(1, 4, stride=2), :]
+    for at in (5, 7):
+        c, t = nsum(Q2, 1, 10, at, 8, 2)
+        R2[1:11, at : at + 8, :] = W2[1:11, at : at + 8, :] * (P2[1:11, at : at + 8, :] - 6.0 * c + t)
+    C3[...] = jnp.sum(R2[:, 4:20, :].reshape(6, 2, 16, 128), axis=1)
+    t = C3[:, pl.ds(0, 6, stride=2), :] + C3[:, pl.ds(1, 6, stride=2), :]
     b3 = pair_z(t, 2) * 0.125
-    SC = r["SC"]
-    SC[0:4, :] = pack2(g2)
-    l4 = lane4 % 4
-    SC[4:8, :] = jnp.where(l4 < 2, jnp.where(l4 == 0, b3[0], b3[1]), jnp.where(l4 == 2, b3[2], b3[3]))
-    wait_c = send_all(SC, r["RC"], 19)
-    run(wait_s)
-    W3[1, 8:16, :] = keep(r["RSX"][0], -1, 0, 0)
-    W3[8, 8:16, :] = keep(r["RSX"][1], 1, 0, 0)
-    for i in range(1, 7):
-        W3[i + 1, 8:9, :] = keep(r["RSY"][0, i : i + 1, :], 0, -1, 0)
-        W3[i + 1, 15:16, :] = keep(r["RSY"][1, i : i + 1, :], 0, 1, 0)
-    P3[3:7, 10:14, :] = b3 * inverse(W3[3:7, 10:14, :])
-    c, t = nsum(P3, 1, 8, 8, 8, 4)
-    V3[1:9, 8:16, :] = S * (1.2 * c + S * t) * rowmask(8, 8, 11, 13)
-    xmask(V3, 4, 6, 1, 8, 8, 8)
-    c, t = nsum(V3, 1, 8, 8, 8, 4)
-    res = W3[1:9, 8:16, :] * (P3[1:9, 8:16, :] - 6.0 * c + t)
+    P3[3:9, 10:16, :] = b3 * inverse(W3[3:9, 10:16, :])
+    c, t = nsum(P3, 2, 8, 9, 8, 4)
+    Q3[2:10, 9:17, :] = S * (1.2 * c + S * t) * rowmask(9, 8, 12, 14)
+    xmask(Q3, 5, 7, 2, 8, 9, 8)
     T4 = r["T4"]
-    T4[0, 8:16, :] = res[0]
-    for i in range(3):
-        T4[1 + i, 8:16, :] = res[1 + 2 * i] + res[2 + 2 * i]
-    T4[4, 8:16, :] = res[7]
-    t = T4[:, pl.ds(7, 8, stride=2), :] + T4[:, pl.ds(8, 8, stride=2), :]
+    for at in (8, 10):
+        c, t = nsum(Q3, 1, 10, at, 8, 4)
+        res = W3[1:11, at : at + 8, :] * (P3[1:11, at : at + 8, :] - 6.0 * c + t)
+        T4[:, at : at + 8, :] = jnp.sum(res.reshape(5, 2, 8, 128), axis=1)
+    t = T4[:, pl.ds(8, 8, stride=2), :] + T4[:, pl.ds(9, 8, stride=2), :]
     patch = pair_z(t, 4) * 0.125
 
-    msg = zero
+    lines = []
     for dx in range(5):
         v = patch[dx]
         main = zero
@@ -552,12 +602,13 @@
             main = jnp.where((lane >= 2 * q) & (lane < 2 * q + 2), roll(v, 2 * q - lo), main)
         edge = jnp.where(lane < 2, roll(v, 0 - 23), jnp.where(lane < 4, roll(v, 2 - 103), 0.0))
         line = pltpu.roll(main, 0, 1, stride=8, stride_axis=0) + pltpu.roll(edge, 40, 1, stride=4, stride_axis=0)
-        line = jnp.sum(line, axis=0, keepdims=True)
-        msg = jnp.where(row == ix + (dx - 2), line, msg)
-    msg = jnp.where(ih == 1, roll(msg, 64), msg)
+        lines.append(jnp.sum(line, axis=0, keepdims=True))
     GA, GB, GC = r["GA"], r["GB"], r["GC"]
     SA, SB, SZ = r["SA"], r["SB"], r["SZ"]
-    SA[...] = msg
+    for p in range(2):
+        SA[p : p + 1, :] = lines[2 * p] + roll(lines[2 * p + 1], 64)
+    SA[2:3, :] = lines[4]
+    SA[3:4, :] = jnp.zeros((1, 128), F32)
     ga_at = ih * nx + ix
     to_group(21, SA, GA.at[ga_at], group_y)
 
@@ -576,10 +627,56 @@
                     acc = jnp.where((lane >= at) & (lane < at + 8), roll(tile, at - 64 * q - 8 * z), acc)
             cp[x * nz + z] = acc
 
+    run(wait_w0)
+    W0[1:2, 8:24, :] = keep(W0[1:2, 8:24, :], -1, 0, 0)
+    W0[18:19, 8:24, :] = keep(W0[18:19, 8:24, :], 1, 0, 0)
+    W0[2:18, 7:8, :] = keep(r["RYW"][0], 0, -1, 0)
+    W0[2:18, 24:25, :] = keep(r["RYW"][1], 0, 1, 0)
+    for h in range(2):
+        sl = slice(8 * h, 8 * h + 8)
+        j = qj(lane)
+        v = jnp.where(j == 1, keep(r["RQW"][0, sl, :], 0, 0, -1), jnp.where(j == 4, keep(r["RQW"][1, sl, :], 0, 0, 1), 0.0))
+        r["WQ"][8 + 8 * h : 16 + 8 * h, :] = v
+
     from_group(21, GA, n_y - 1)
-    GA[ga_at] = msg
-    SB[...] = jnp.sum(GA[...], axis=0)
+    GA[ga_at] = SA[...]
+    sums = []
+    for h in range(2):
+        even, odd = zero, zero
+        for p in range(3):
+            m = zero
+            for g in range(nx):
+                m = jnp.where(row == g, GA[h * nx + g, p : p + 1, :], m)
+            even = even + (m if p == 1 else pltpu.roll(m, (2 * p - 2) % 8, 0))
+            if p < 2:
+                odd = odd + pltpu.roll(m, (2 * p - 1) % 8, 0)
+        sums.append(jnp.where(lane < 64, even, 0.0) + roll(jnp.where(lane < 64, 0.0, odd), 64))
+    SB[...] = sums[0] + roll(sums[1], 64)
     to_group(22, SB, GB.at[ixx], group_x)
+
+    recv1(g1, "g", wait_g1, G1)
+    for at in (4, 12):
+        c, t = nsum(G1, 1, 12, at, 8, 1)
+        V1[1:13, at : at + 8, :] = S * (1.2 * c + S * t) * rowmask(at, 8, 8, 16)
+    xmask(V1, 3, 11, 1, 12, 4, 16)
+    c, t = nsum(V1, 3, 8, 8, 8, 1)
+    r1 = W1[3:11, 8:16, :] * (G1[3:11, 8:16, :] - 6.0 * c + t)
+    g2 = jnp.where(own1[0:4], coarsen1(r1, 0.125) * wi2, 0.0)
+
+    PT[4:8, 8:12, :] = g2
+    c, t = nsum(PT, 2, 8, 6, 8, 2)
+    QT[2:10, 6:14, :] = S * (1.2 * c + S * t) * rowmask(6, 8, 8, 12)
+    xmask(QT, 4, 8, 2, 8, 6, 8)
+    c, t = nsum(QT, 2, 8, 6, 8, 2)
+    res = W2[2:10, 6:14, :] * (PT[2:10, 6:14, :] - 6.0 * c + t)
+    C2[...] = jnp.sum(res.reshape(4, 2, 8, 128), axis=1)
+    t = C2[:, pl.ds(0, 4, stride=2), :] + C2[:, pl.ds(1, 4, stride=2), :]
+    b3 = pair_z(t, 2) * 0.125
+    SC = r["SC"]
+    SC[0:4, :] = pack2(g2)
+    l4 = lane4 % 4
+    SC[4:8, :] = jnp.where(l4 < 2, jnp.where(l4 == 0, b3[0], b3[1]), jnp.where(l4 == 2, b3[2], b3[3]))
+    wait_c = send_all(SC, r["RC"], 19)
 
     from_group(22, GB, xn - 1)
     GB[ixx] = SB[...]
@@ -631,12 +728,12 @@
         v = roll(jnp.where(l4 == i, TC[...], 0.0), -i)
         v = v + roll(v, 1)
         v = v + roll(v, 2)
-        G3[3 + i, 10:14, :] = v * inverse(W3[3 + i, 10:14, :])
-    c, t = nsum(G3, 4, 2, 11, 2, 4)
+        G3[4 + i, 11:15, :] = v * inverse(W3[4 + i, 11:15, :])
+    c, t = nsum(G3, 5, 2, 12, 2, 4)
     v3 = jnp.where(own1[0:2], S * (1.2 * c + S * t), 0.0)
-    SE = r["SE"]
-    SE[2:4, :] = pack3(v3)
-    SE[1:2, :] = jnp.zeros((1, 128), F32)
+    SE, SV, RE, RV = r["SE"], r["SV"], r["RE"], r["RV"]
+    SV[...] = pack3(v3)
+    wait_v = send_all(SV, RV, 26)
 
     from_group(23, GC, nz - 1)
     GC[iz, 0] = SZ[0]
@@ -653,36 +750,33 @@
     acc = (acc[0] + acc[1]) + (acc[2] + acc[3])
     tot = jnp.sum(acc, axis=1, keepdims=True)
     e4 = jnp.sum(jnp.where((lane >= 32 + 8 * row) & (lane < 40 + 8 * row), tot, 0.0), axis=0, keepdims=True)
-    SE[0:1, :] = e4
-    RE = r["RE"]
-    run(send_all(SE, RE, 20))
-
-    unpack3(RE, SE, slice(2, 4), V3)
-    for x in (1, 8):
-        V3[x, 8:16, :] = zero
-    for x in range(2, 8):
-        V3[x, 8:9, :] = zero[0:1]
-        V3[x, 15:16, :] = zero[0:1]
+    SE[...] = e4
+    wait_e = send_all(SE, RE, 20)
+    run(wait_v)
+
+    near = [(a, b) for a in (-1, 0, 1) for b in (-1, 0, 1)]
+    unpack3(lambda o: SV[...] if o == (0, 0, 0) else RV[SLOT[o]], near, V3)
+    run(wait_e)
     l1 = lane[0:1]
     par = []
     for dx in (-1, 0, 1):
         v = zero
         for dy in (-1, 0, 1):
             o = (dx, dy, 0)
-            own = SE[0:1, :] if o == (0, 0, 0) else keep(RE[SLOT[o], 0:1, :], *o)
+            own = SE[...] if o == (0, 0, 0) else keep(RE[SLOT[o], 0:1, :], *o)
             lo, hi = (keep(RE[SLOT[(dx, dy, dz)], 0:1, :], dx, dy, dz) for dz in (-1, 1))
             e = jnp.where((l1 >= 32) & (l1 < 96), own, roll(jnp.where(l1 < 64, hi, lo), 64))
-            y = 3 + 2 * dy
+            y = 4 + 2 * dy
             v = jnp.where((row == y) | (row == y + 1), e, v)
         par.append(v)
     for i in range(6):
-        U3[2 + i, 8:16, :] = V3[2 + i, 8:16, :] + W3[2 + i, 8:16, :] * par[i // 2]
-    c, t = nsum(U3, 3, 4, 8, 8, 4)
+        U3[3 + i, 8:16, :] = V3[3 + i, 8:16, :] + W3[3 + i, 8:16, :] * par[i // 2]
+    c, t = nsum(U3, 4, 4, 8, 8, 4)
     E3 = r["E3"]
-    E3[...] = (0.2 * c + S * (G3[3:7, 8:16, :] + t)) * inverse(W3[3:7, 8:16, :])
+    E3[...] = (0.2 * c + S * (G3[4:8, 8:16, :] + t)) * inverse(W3[4:8, 8:16, :])
     F2 = r["F2"]
-    F2[:, pl.ds(0, 4, stride=2), :] = E3[:, 2:6, :]
-    F2[:, pl.ds(1, 4, stride=2), :] = E3[:, 2:6, :]
+    F2[:, pl.ds(0, 4, stride=2), :] = E3[:, 3:7, :]
+    F2[:, pl.ds(1, 4, stride=2), :] = E3[:, 3:7, :]
     for i in range(8):
         U2[2 + i, 6:14, :] = V2[2 + i, 6:14, :] + W2[2 + i, 6:14, :] * F2[i // 2]
     c, t = nsum(U2, 3, 6, 6, 8, 2)
@@ -747,26 +841,38 @@
         "QS": (16, 128), "QW": (16, 128), "RQ": (6, 16, 128), "QE": (2, 1, 128), "RQE": (4, 1, 128),
         "YW": (2, 16, 1, 128), "RYW": (2, 16, 1, 128), "RQW": (2, 16, 128),
         "C0": (8, 16, 128), "C1": (4, 8, 128), "C2": (4, 8, 128),
-        "S1": (8, 8, 128), "SW": (8, 128), "RW": (26, 8, 128),
+        "SW2": (4, 128), "SW3": (2, 128), "SWZ": (1, 128), "RW2": (8, 4, 128), "RWZ": (18, 1, 128),
+        "RW3": (26, 2, 128), "RW3X": (18, 2, 128), "RW3Y": (18, 2, 128), "C3": (6, 16, 128),
+        "A1": (14, 24, 128), "Q1": (14, 24, 128), "R2": (12, 24, 128), "PT": (12, 24, 128), "QT": (12, 24, 128),
         "G1": (14, 24, 128), "W1": (14, 24, 128), "V1": (14, 24, 128), "U1": (14, 24, 128),
         "G2": (12, 24, 128), "W2": (12, 24, 128), "V2": (12, 24, 128), "U2": (12, 24, 128),
         "P2": (12, 24, 128), "Q2": (12, 24, 128),
-        "G3": (10, 24, 128), "W3": (10, 24, 128), "V3": (10, 24, 128), "U3": (10, 24, 128), "P3": (10, 24, 128),
-        "T4": (5, 24, 128), "SX": (2, 8, 128), "SY": (2, 8, 128), "RSX": (2, 8, 128), "RSY": (2, 8, 128),
-        "SC": (8, 128), "RC": (26, 8, 128), "TB": (3, 4, 128), "TC": (4, 128), "SE": (4, 128), "RE": (26, 4, 128),
-        "SA": (8, 128), "SB": (8, 128), "SZ": (2, 8, 128),
-        "GA": (2 * nx, 8, 128), "GB": (xn, 8, 128), "GC": (nz, 2, 8, 128), "CP": (nx * nz, 8, 128),
+        "G3": (12, 24, 128), "W3": (12, 24, 128), "V3": (12, 24, 128), "U3": (12, 24, 128), "P3": (12, 24, 128), "Q3": (12, 24, 128),
+        "T4": (5, 24, 128),
+        "SC": (8, 128), "RC": (26, 8, 128), "TB": (3, 4, 128), "TC": (4, 128), "SE": (1, 128), "RE": (26, 1, 128), "SV": (2, 128), "RV": (26, 2, 128),
+        "SA": (4, 128), "SB": (8, 128), "SZ": (2, 8, 128),
+        "GA": (2 * nx, 4, 128), "GB": (xn, 8, 128), "GC": (nz, 2, 8, 128), "CP": (nx * nz, 8, 128),
         "E3": (4, 8, 128), "F2": (4, 8, 128), "E2": (6, 8, 128), "F1": (6, 16, 128),
         "E1": (10, 16, 128), "O1": (10, 16, 128), "F0": (10, 32, 128), "FQ": (8, 128),
     }
-    for n in "wg":
-        v["S1" + n] = (8, 8, 128)
-        v["YS1" + n] = (2, 8, 4, 128)
-        v["ZS1" + n] = (8, 128)
-        v["RX1" + n] = (2, 3, 8, 128)
-        v["RY1" + n] = (2, 8, 4, 128)
-        v["RXY1" + n] = (4, 3, 4, 128)
-        v["RZ1" + n] = (18, 8, 128)
+    n = "g"
+    v["S1" + n] = (8, 8, 128)
+    v["YS1" + n] = (2, 8, 4, 128)
+    v["ZS1" + n] = (8, 128)
+    v["RX1" + n] = (2, 3, 8, 128)
+    v["RY1" + n] = (2, 8, 4, 128)
+    v["RXY1" + n] = (4, 3, 4, 128)
+    v["RZ1" + n] = (18, 8, 128)
+    n = "w"
+    v["S1" + n] = (8, 8, 128)
+    v["YS1" + n] = (2, 8, 2, 128)
+    v["ZS1" + n] = (8, 128)
+    v["YZ1" + n] = (2, 2, 128)
+    v["RX1" + n] = (2, 2, 8, 128)
+    v["RY1" + n] = (2, 8, 2, 128)
+    v["RXY1" + n] = (4, 2, 128)
+    v["RZ1" + n] = (6, 8, 128)
+    v["RYZ1" + n] = (4, 2, 128)
     return v
 
 
@@ -785,7 +891,7 @@
             out_shape=jax.ShapeDtypeStruct((16, 16, 128), F32),
             in_specs=[pl.BlockSpec(memory_space=pltpu.HBM)] * 3,
             out_specs=vmem,
-            scratch_shapes=[pltpu.VMEM(s, F32) for s in sizes.values()] + [pltpu.SemaphoreType.DMA((24,))] * 2 + [pltpu.SemaphoreType.DMA((3,))],
+            scratch_shapes=[pltpu.VMEM(s, F32) for s in sizes.values()] + [pltpu.SemaphoreType.DMA((28,))] * 2 + [pltpu.SemaphoreType.DMA((3,))],
             compiler_params=pltpu.CompilerParams(collective_id=0, has_side_effects=True, vmem_limit_bytes=24 * 2**20),
             name="vcycle",
         )(*[pltpu.with_memory_space_constraint(a, pltpu.HBM) for a in (sources, stiffness, coarse_inverse)])

time: 59 us -> 53.5 us (0.907)
  the two profiles are of different devices: /device:TPU:7 before, /device:TPU:14 now
where the time goes in v4:
time: 53.5 us; the launch traced here: 53.4 us
  Pallas kernels  52.7 us (99%)
  other arithmetic  0.68 us (1%)
    pallas_call x1, Pallas kernels, per_device(): pl.pallas_call(body, out_shape=jax.ShapeDtypeStruct((16, 16, 128), F32),...  52.7 us

profile of v4, /device:TPU:14, one launch (start us, length us, event | category | flops | bytes accessed | tf_op | source)
XLA Modules:
  0.0 53.4 jit_solution(1249132102757212219)
XLA Ops:
  0.0 0.0 copy-start
  0.0 52.7 %vcycle.1 = f32[16,16,128]{2,1,0:T(8,128)S(1)} custom-call(f32[1,16,16,128]{3,2,1,0:T(8,128)} %args_0_.4, f32[16,16,128]{2,1,0:T(8,128)} %args_1_.4, f32[8,8192]{1,0:T(8,128)} %args_2_.4), custom_call_target="tpu_custom_call" | custom-call | tf_op jit(solution)/shard_map/vcycle/pallas_call | solution.py:889
  52.7 0.0 copy-done
  52.7 0.7 %divide_bitcast_fusion = f32[1,16,16,128]{3,2,1,0:T(8,128)} fusion(f32[16,16,128]{2,1,0:T(8,128)S(1)} %vcycle.1, f32[16,16,128]{2,1,0:T(8,128)S(1)} %copy-done), kind=kLoop, calls=%fused_computation | loop fusion | flops 32768 | bytes 393216 | tf_op jit(solution)/shard_map/broadcast_in_dim | solution.py:898
Async XLA Ops:
  0.0 52.7 %copy-start = (f32[16,16,128]{2,1,0:T(8,128)S(1)}, f32[16,16,128]{2,1,0:T(8,128)}, u32[]{:S(2)}) copy-start(f32[16,16,128]{2,1,0:T(8,128)} %args_1_.4) | copy-start | bytes 393220

commit v5 on v4

--- a/solution.py
+++ b/solution.py
@@ -15,7 +15,6 @@
 OFFS.sort(key=lambda o: (-abs(o[1]), -abs(o[2]), -abs(o[0])))
 OFF2X = [(2 * a, b, c) for a in (-1, 1) for b in (-1, 0, 1) for c in (-1, 0, 1)]
 OFF2Y = [(b, 2 * a, c) for a in (-1, 1) for b in (-1, 0, 1) for c in (-1, 0, 1)]
-FLAT = [o for o in OFFS if o[2] == 0]
 SLOT = {o: i for i, o in enumerate(OFFS)}
 ZOFFS = [o for o in OFFS if o[2] != 0]
 ZSLOT = {o: i for i, o in enumerate(ZOFFS)}
@@ -131,14 +130,15 @@
     loads = [pltpu.make_async_copy(r[a], r[b], r["lsem"].at[i]) for i, (a, b) in enumerate((("b", "B0"), ("w", "A0"), ("c", "CM")))]
     for c in loads:
         c.start()
-    for o in OFFS + OFF2X + OFF2Y:
+    for d in group_x + group_y + group_z:
+        pl.semaphore_signal(barrier, inc=1, device_id=d, device_id_type=MESH)
+
+    for o in OFFS + OFF2Y + OFF2X:
 
         @pl.when(has(o))
         def _():
             pl.semaphore_signal(barrier, inc=1, device_id=dev(*o), device_id_type=MESH)
 
-    for d in group_y + group_x + group_z:
-        pl.semaphore_signal(barrier, inc=1, device_id=d, device_id_type=MESH)
     partners = sum(jnp.where(has(o), 1, 0) for o in OFFS + OFF2X + OFF2Y) + len(group_y + group_x + group_z)
 
     lane = lax.broadcasted_iota(jnp.int32, (8, 128), 1)
@@ -171,26 +171,95 @@
             for x in range(16):
                 m = src[x + 2, 8 + 8 * h : 16 + 8 * h, :]
                 base = 6 * (x + 2)
-                acc = jnp.where((lane >= base) & (lane < base + 3), roll(m, base - 126), acc)
-                acc = jnp.where((lane >= base + 3) & (lane < base + 6), roll(m, base + 3 - 127), acc)
+                acc = jnp.where(lane == base, roll(m, base - 1), acc)
+                acc = jnp.where((lane >= base + 1) & (lane < base + 3), roll(m, base + 1 - 127), acc)
+                acc = jnp.where((lane >= base + 3) & (lane < base + 5), roll(m, base + 3 - 127), acc)
+                acc = jnp.where(lane == base + 5, roll(m, base + 5 - 126), acc)
             dst[8 * h : 8 * h + 8, :] = acc
 
     pack_q(G0, r["QS"])
     r["QE"][0] = r["QS"][0:1, :]
     r["QE"][1] = r["QS"][15:16, :]
 
+    for name in ("G0", "W0", "V0"):
+        a = r[name]
+        a[:, 0:8, :] = jnp.zeros((20, 8, 128), F32)
+        a[:, 24:32, :] = jnp.zeros((20, 8, 128), F32)
+    for name in ("GQ", "WQ", "VQ", "UQ", "G1", "W1", "V1", "U1", "G2", "W2", "V2", "U2", "P2", "Q2", "G3", "W3", "V3", "U3", "P3", "T4", "A1", "Q1", "R2", "PT", "QT", "Q3"):
+        r[name][...] = jnp.zeros(r[name].shape, F32)
+
+    zr = lax.broadcasted_iota(jnp.int32, (256, 128), 0) % 128
+    zc = lax.broadcasted_iota(jnp.int32, (256, 128), 1)
+    down = jnp.where(zc == 32 + zr // 2, jnp.float32(1), jnp.float32(0)).astype(jnp.bfloat16)
+    up = jnp.where(zr == 32 + zc // 2, jnp.float32(1), jnp.float32(0)).astype(jnp.bfloat16)
+
+    C0 = r["C0"]
+
+    def coarsen0(values, scale):
+        C0[...] = jnp.sum(values.reshape(8, 2, 16, 128), axis=1)
+        t = C0[:, pl.ds(0, 8, stride=2), :] + C0[:, pl.ds(1, 8, stride=2), :]
+        return (select_dot(t.reshape(64, 128), down) * scale).reshape(8, 8, 128)
+
+    def pair_z(t, dil):
+        ln = lax.broadcasted_iota(jnp.int32, t.shape, t.ndim - 1)
+        return t + jnp.where((ln // dil) % 2 == 0, roll(t, -dil), roll(t, dil))
+
+    C1, C2 = r["C1"], r["C2"]
+
+    def coarsen1(values, scale):
+        n = values.shape[0] // 2
+        C1[...] = jnp.sum(values.reshape(n, 2, 8, 128), axis=1)
+        t = C1[:, pl.ds(0, 4, stride=2), :] + C1[:, pl.ds(1, 4, stride=2), :]
+        return pair_z(t, 1) * scale
+
+    w1 = coarsen0(w0, 0.0625)
+    own1 = (lane >= 32) & (lane < 96)
+    w2 = coarsen1(w1, 0.0625)
+    C2[0:4, 0:4, :] = w2
+    t = C2[0:4, pl.ds(0, 2, stride=2), :] + C2[0:4, pl.ds(1, 2, stride=2), :]
+    w3 = pair_z(jnp.sum(t.reshape(2, 2, 2, 128), axis=1), 2) * 0.0625
+
+    lane4 = lane[0:4]
+
+    def pack2(v):
+        halves = []
+        for h in range(2):
+            a = jnp.where(lane4 % 2 == 0, v[2 * h], v[2 * h + 1])
+            halves.append(roll(a, -32 if h == 0 else 32))
+        return jnp.where(lane4 < 64, halves[0], halves[1])
+
+    def pack3(v):
+        return jnp.where(lane[0:2] < 64, roll(v[0], -32), roll(v[1], 32))
+
+    SW2, SW3 = r["SW2"], r["SW3"]
+    SW2[...] = pack2(w2)
+    SW3[...] = pack3(w3)
+    def send_all(src, dst, key):
+        return [round_of(key, [(o, src, dst.at[SLOT[neg(o)]]) for o in OFFS], first(dst))]
+
+    def pack_z1(own, zs):
+        acc = zero
+        for x in range(8):
+            acc = jnp.where((lane >= 16 * x) & (lane < 16 * x + 4), roll(own[x], 16 * x - 32), acc)
+            acc = jnp.where((lane >= 16 * x + 4) & (lane < 16 * x + 8), roll(own[x], 16 * x + 4 - 92), acc)
+        zs[...] = acc
+
+    s1w, ysw, zsw, yzw = r["S1w"], r["YS1w"], r["ZS1w"], r["YZ1w"]
+    s1w[...] = w1
+    ysw[0] = s1w[:, 0:2, :]
+    ysw[1] = s1w[:, 6:8, :]
+    pack_z1(w1, zsw)
+    yzw[0] = zsw[0:2, :]
+    yzw[1] = zsw[6:8, :]
+    RX, RY, RXY, RZ, RYZ = (r[name + "w"] for name in ("RX1", "RY1", "RXY1", "RZ1", "RYZ1"))
+    r["YW"][0] = W0[2:18, 8:9, :]
+    r["YW"][1] = W0[2:18, 23:24, :]
+    pack_q(W0, r["QW"])
+
     pl.semaphore_wait(barrier, partners)
 
     gsl = pl.ds(8, 16)
     wait_g0 = [
-        round_of(
-            0,
-            [
-                ((-1, 0, 0), G0.at[pl.ds(2, 2), gsl], G0.at[pl.ds(18, 2), gsl]),
-                ((1, 0, 0), G0.at[pl.ds(16, 2), gsl], G0.at[pl.ds(0, 2), gsl]),
-            ],
-            lambda n: G0.at[pl.ds(0, 2 * n), gsl],
-        ),
         round_of(1, [((0, d, 0), r["YS"].at[i], r["RY"].at[1 - i]) for i, d in enumerate((-1, 1))], first(r["RY"])),
         round_of(
             2,
@@ -200,93 +269,22 @@
             ],
             first(r["RXY"]),
         ),
-        round_of(3, [((dx, 0, dz), r["QS"], r["RQ"].at[XZ.index((-dx, -dz))]) for dx, dz in XZ], first(r["RQ"])),
         round_of(
             4,
             [((0, dy, dz), r["QE"].at[(dy + 1) // 2], r["RQE"].at[XY.index((-dy, -dz))]) for dy, dz in XY],
             first(r["RQE"]),
         ),
+        round_of(3, [((dx, 0, dz), r["QS"], r["RQ"].at[XZ.index((-dx, -dz))]) for dx, dz in XZ], first(r["RQ"])),
+        round_of(
+            0,
+            [
+                ((-1, 0, 0), G0.at[pl.ds(2, 2), gsl], G0.at[pl.ds(18, 2), gsl]),
+                ((1, 0, 0), G0.at[pl.ds(16, 2), gsl], G0.at[pl.ds(0, 2), gsl]),
+            ],
+            lambda n: G0.at[pl.ds(0, 2 * n), gsl],
+        ),
     ]
 
-    for name in ("G0", "W0", "V0"):
-        a = r[name]
-        a[:, 0:8, :] = jnp.zeros((20, 8, 128), F32)
-        a[:, 24:32, :] = jnp.zeros((20, 8, 128), F32)
-    for name in ("GQ", "WQ", "VQ", "UQ", "G1", "W1", "V1", "U1", "G2", "W2", "V2", "U2", "P2", "Q2", "G3", "W3", "V3", "U3", "P3", "T4", "A1", "Q1", "R2", "PT", "QT", "Q3"):
-        r[name][...] = jnp.zeros(r[name].shape, F32)
-
-    zr = lax.broadcasted_iota(jnp.int32, (256, 128), 0) % 128
-    zc = lax.broadcasted_iota(jnp.int32, (256, 128), 1)
-    down = jnp.where(zc == 32 + zr // 2, jnp.float32(1), jnp.float32(0)).astype(jnp.bfloat16)
-    up = jnp.where(zr == 32 + zc // 2, jnp.float32(1), jnp.float32(0)).astype(jnp.bfloat16)
-
-    C0 = r["C0"]
-
-    def coarsen0(values, scale):
-        C0[...] = jnp.sum(values.reshape(8, 2, 16, 128), axis=1)
-        t = C0[:, pl.ds(0, 8, stride=2), :] + C0[:, pl.ds(1, 8, stride=2), :]
-        return (select_dot(t.reshape(64, 128), down) * scale).reshape(8, 8, 128)
-
-    def pair_z(t, dil):
-        ln = lax.broadcasted_iota(jnp.int32, t.shape, t.ndim - 1)
-        return t + jnp.where((ln // dil) % 2 == 0, roll(t, -dil), roll(t, dil))
-
-    C1, C2 = r["C1"], r["C2"]
-
-    def coarsen1(values, scale):
-        n = values.shape[0] // 2
-        C1[...] = jnp.sum(values.reshape(n, 2, 8, 128), axis=1)
-        t = C1[:, pl.ds(0, 4, stride=2), :] + C1[:, pl.ds(1, 4, stride=2), :]
-        return pair_z(t, 1) * scale
-
-    w1 = coarsen0(w0, 0.0625)
-    own1 = (lane >= 32) & (lane < 96)
-    w2 = coarsen1(w1, 0.0625)
-    C2[0:4, 0:4, :] = w2
-    t = C2[0:4, pl.ds(0, 2, stride=2), :] + C2[0:4, pl.ds(1, 2, stride=2), :]
-    w3 = pair_z(jnp.sum(t.reshape(2, 2, 2, 128), axis=1), 2) * 0.0625
-
-    lane4 = lane[0:4]
-
-    def pack2(v):
-        halves = []
-        for h in range(2):
-            a = jnp.where(lane4 % 2 == 0, v[2 * h], v[2 * h + 1])
-            halves.append(roll(a, -32 if h == 0 else 32))
-        return jnp.where(lane4 < 64, halves[0], halves[1])
-
-    def pack3(v):
-        return jnp.where(lane[0:2] < 64, roll(v[0], -32), roll(v[1], 32))
-
-    SW2, SW3, SWZ = r["SW2"], r["SW3"], r["SWZ"]
-    p2 = pack2(w2)
-    SW2[...] = p2
-    SW3[...] = pack3(w3)
-    zp = jnp.zeros((4, 128), F32)
-    for h in range(2):
-        zp = jnp.where((lane4 >= 16 * h) & (lane4 < 16 * h + 8), roll(p2, -48 * h), zp)
-        zp = jnp.where((lane4 >= 16 * h + 8) & (lane4 < 16 * h + 16), roll(p2, -48 * h - 48), zp)
-    row4 = row[0:4]
-    SWZ[...] = sum(roll(jnp.sum(jnp.where(row4 == y, zp, 0.0), axis=0, keepdims=True), 32 * y) for y in range(4))
-
-    def send_all(src, dst, key):
-        return [round_of(key, [(o, src, dst.at[SLOT[neg(o)]]) for o in OFFS], first(dst))]
-
-    def pack_z1(own, zs):
-        acc = zero
-        for x in range(8):
-            acc = jnp.where((lane >= 16 * x) & (lane < 16 * x + 4), roll(own[x], 16 * x - 32), acc)
-            acc = jnp.where((lane >= 16 * x + 4) & (lane < 16 * x + 8), roll(own[x], 16 * x + 4 - 92), acc)
-        zs[...] = acc
-
-    s1w, ysw, zsw, yzw = r["S1w"], r["YS1w"], r["ZS1w"], r["YZ1w"]
-    s1w[...] = w1
-    ysw[0] = s1w[:, 0:2, :]
-    ysw[1] = s1w[:, 6:8, :]
-    pack_z1(w1, zsw)
-    yzw[0] = zsw[0:2, :]
-    yzw[1] = zsw[6:8, :]
-    RX, RY, RXY, RZ, RYZ = (r[name + "w"] for name in ("RX1", "RY1", "RXY1", "RZ1", "RYZ1"))
     wait_w = [
         round_of(7, [((0, -1, 0), ysw.at[0], RY.at[1]), ((0, 1, 0), ysw.at[1], RY.at[0])], first(RY)),
         round_of(
@@ -302,8 +300,7 @@
             [((0, dy, dz), yzw.at[(dy + 1) // 2], RYZ.at[XY.index((-dy, -dz))]) for dy, dz in XY],
             first(RYZ),
         ),
-        round_of(5, [(o, SW2, r["RW2"].at[FLAT.index(neg(o))]) for o in FLAT], first(r["RW2"])),
-        round_of(17, [(o, SWZ, r["RWZ"].at[ZSLOT[neg(o)]]) for o in ZOFFS], first(r["RWZ"])),
+        round_of(5, [(o, SW2, r["RW2"].at[SLOT[neg(o)]]) for o in OFFS], first(r["RW2"])),
         round_of(18, [(o, SW3, r["RW3"].at[SLOT[neg(o)]]) for o in OFFS], first(r["RW3"])),
         round_of(25, [(o, SW3, r["RW3Y"].at[OFF2Y.index(neg(o))]) for o in OFF2Y], first(r["RW3Y"])),
         round_of(24, [(o, SW3, r["RW3X"].at[OFF2X.index(neg(o))]) for o in OFF2X], first(r["RW3X"])),
@@ -380,9 +377,6 @@
                 at = 8 if dy == 0 else (4 if dy < 0 else 16)
                 dst[x, at : at + (8 if dy == 0 else 4), :] = v
 
-    r["YW"][0] = W0[2:18, 8:9, :]
-    r["YW"][1] = W0[2:18, 23:24, :]
-    pack_q(W0, r["QW"])
     wait_w0 = [
         round_of(
             14,
@@ -417,14 +411,17 @@
         own = r["QS"][sl, :]
         j = qj(lane)
         q = [keep(r["RQ"][i, sl, :], dx, 0, dz) for i, (dx, dz) in enumerate(XZ)]
-        v, lo, hi = (jnp.where(j < 2, q[2 * i], jnp.where(j > 3, q[2 * i + 1], own if i == 0 else 0.0)) for i in range(3))
+        v, lo, hi = (
+            jnp.where((j == 3) | (j == 5), q[2 * i], jnp.where((j == 0) | (j == 2), q[2 * i + 1], own if i == 0 else 0.0))
+            for i in range(3)
+        )
         v = jnp.where((lane >= 6) & (lane < 12), roll(lo, 6 - 102), jnp.where((lane >= 108) & (lane < 114), roll(hi, 108 - 12), v))
         GQ[8 + 8 * h : 16 + 8 * h, :] = jnp.where((lane >= 6) & (lane < 114), v, 0.0)
     for dy, at in ((-1, 7), (1, 24)):
         j = qj(lane[0:1])
         lo = keep(r["RQE"][XY.index((dy, -1))], 0, dy, -1)
         hi = keep(r["RQE"][XY.index((dy, 1))], 0, dy, 1)
-        v = jnp.where(j < 2, lo, jnp.where(j > 3, hi, 0.0))
+        v = jnp.where((j == 3) | (j == 5), lo, jnp.where((j == 0) | (j == 2), hi, 0.0))
         GQ[at : at + 1, :] = jnp.where((lane[0:1] >= 12) & (lane[0:1] < 108), v, 0.0)
 
     INJ = r["INJ"]
@@ -433,9 +430,7 @@
         for at in tiles:
             m = q[at : at + 8, :]
             for xp in xs:
-                a = roll(m, -(6 * xp + 1))
-                c = roll(m, 127 - (6 * xp + 4))
-                INJ[xp, at : at + 8, :] = jnp.where(lane == 0, a, jnp.where(lane == 127, c, 0.0))
+                INJ[xp, at : at + 8, :] = jnp.where((lane == 0) | (lane == 127), roll(m, -(6 * xp + 3)), 0.0)
 
     def sum0(a, x, n, at):
         c = a[x : x + n, at : at + 8, :]
@@ -458,10 +453,10 @@
 
     for at in (8, 16):
         c = GQ[at : at + 8, :]
-        t = roll(c, 1) + roll(c, -1) + roll(c, 6) + roll(c, -6)
+        t = jnp.where(qj(lane) == 3, roll(c, -1) + roll(c, -2), roll(c, 1) + roll(c, 2)) + (roll(c, 6) + roll(c, -6))
         t = t + GQ[at - 1 : at + 7, :] + GQ[at + 1 : at + 9, :]
         j = qj(lane)
-        mask = jnp.where(j == 1, mz[-1], jnp.where(j == 4, mz[1], 0.0))
+        mask = jnp.where(j == 3, mz[-1], jnp.where(j == 2, mz[1], 0.0))
         mask = jnp.where((lane >= 12) & (lane < 108), mask, 0.0)
         VQ[at : at + 8, :] = S * (1.2 * c + S * t) * mask
 
@@ -496,15 +491,12 @@
         for dx in (-1, 0, 1):
             for dy in (-1, 0, 1):
                 m0, c = spread(*[piece(buf, own, rows, (dx, dy, dz)) for dz in (0, -1, 1)], lane4, dx, dy)
-                spread2(m0, c, dst, dx, dy)
-
-    def spread2(m0, c, dst, dx, dy):
-        for p in range(2):
-            take = lane4 % 2 == p
-            a = jnp.where(take, m0, roll(m0, 1 if p == 0 else -1))
-            e = jnp.where(take, c, roll(c, 1 if p == 0 else -1))
-            for h in range(2):
-                dst[4 + 4 * dx + 2 * h + p, 8 + 4 * dy : 12 + 4 * dy, :] = place(a, e, lane4, h)
+                for p in range(2):
+                    take = lane4 % 2 == p
+                    a = jnp.where(take, m0, roll(m0, 1 if p == 0 else -1))
+                    e = jnp.where(take, c, roll(c, 1 if p == 0 else -1))
+                    for h in range(2):
+                        dst[4 + 4 * dx + 2 * h + p, 8 + 4 * dy : 12 + 4 * dy, :] = place(a, e, lane4, h)
 
     def unpack3(get, spots, dst):
         l = lane[0:2]
@@ -513,19 +505,7 @@
             for h in range(2):
                 dst[5 + 2 * dx + h, 12 + 2 * dy : 14 + 2 * dy, :] = place(m0, c, l, h)
 
-    for dx in (-1, 0, 1):
-        for dy in (-1, 0, 1):
-            m0 = keep(SW2[...] if dx == dy == 0 else r["RW2"][FLAT.index((dx, dy, 0))], dx, dy, 0)
-            lo, hi = (keep(r["RWZ"][ZSLOT[(dx, dy, dz)]], dx, dy, dz) for dz in (-1, 1))
-            line = jnp.where(lane[0:1] % 16 >= 8, lo, hi)
-            e = jnp.zeros((4, 128), F32)
-            for y in range(4):
-                e = jnp.where(row4 == y, roll(line, -32 * y), e)
-            c = jnp.zeros((4, 128), F32)
-            for h in range(2):
-                c = jnp.where((lane4 >= 64 * h) & (lane4 < 64 * h + 8), roll(e, 48 * h), c)
-                c = jnp.where((lane4 >= 64 * h + 56) & (lane4 < 64 * h + 64), roll(e, 48 * h + 48), c)
-            spread2(m0, c, W2, dx, dy)
+    unpack2(r["RW2"], SW2, W2)
 
     def piece3(o):
         if o == (0, 0, 0):
@@ -635,7 +615,7 @@
     for h in range(2):
         sl = slice(8 * h, 8 * h + 8)
         j = qj(lane)
-        v = jnp.where(j == 1, keep(r["RQW"][0, sl, :], 0, 0, -1), jnp.where(j == 4, keep(r["RQW"][1, sl, :], 0, 0, 1), 0.0))
+        v = jnp.where(j == 3, keep(r["RQW"][0, sl, :], 0, 0, -1), jnp.where(j == 2, keep(r["RQW"][1, sl, :], 0, 0, 1), 0.0))
         r["WQ"][8 + 8 * h : 16 + 8 * h, :] = v
 
     from_group(21, GA, n_y - 1)
@@ -734,6 +714,17 @@
     SE, SV, RE, RV = r["SE"], r["SV"], r["RE"], r["RV"]
     SV[...] = pack3(v3)
     wait_v = send_all(SV, RV, 26)
+
+    def drain(key, slots, count, sizes):
+        for n in sizes:
+
+            @pl.when(count == n)
+            def _():
+                copy(slots(n), slots(n), key, right).wait_send()
+
+    early = len(sent) - 1
+    for item in sent[:early]:
+        drain(*item)
 
     from_group(23, GC, nz - 1)
     GC[iz, 0] = SZ[0]
@@ -802,8 +793,8 @@
         e = E1[x + 1, 1:9, :]
         for p in range(2):
             base = 6 * (2 * x + p + 2)
-            acc = jnp.where(lane == base + 1, roll(e, base + 1 - 31), acc)
-            acc = jnp.where(lane == base + 4, roll(e, base + 4 - 96), acc)
+            acc = jnp.where(lane == base + 3, roll(e, base + 3 - 31), acc)
+            acc = jnp.where(lane == base + 2, roll(e, base + 2 - 96), acc)
     UQ = r["UQ"]
     FQ = r["FQ"]
     FQ[...] = acc
@@ -817,14 +808,7 @@
         c, t = sum0(V0, 2, 16, at)
         out_ref[:, at - 8 : at, :] = 0.2 * c + S * (G0[2:18, at : at + 8, :] + t)
 
-    def drain(key, slots, count, sizes):
-        for n in sizes:
-
-            @pl.when(count == n)
-            def _():
-                copy(slots(n), slots(n), key, right).wait_send()
-
-    for item in sent:
+    for item in sent[early:]:
         drain(*item)
     for key, buf, n in ((21, GA, n_y - 1), (22, GB, xn - 1), (23, GC, nz - 1)):
         copy(buf.at[pl.ds(0, n)], buf.at[pl.ds(0, n)], key, right).wait_send()
@@ -841,7 +825,7 @@
         "QS": (16, 128), "QW": (16, 128), "RQ": (6, 16, 128), "QE": (2, 1, 128), "RQE": (4, 1, 128),
         "YW": (2, 16, 1, 128), "RYW": (2, 16, 1, 128), "RQW": (2, 16, 128),
         "C0": (8, 16, 128), "C1": (4, 8, 128), "C2": (4, 8, 128),
-        "SW2": (4, 128), "SW3": (2, 128), "SWZ": (1, 128), "RW2": (8, 4, 128), "RWZ": (18, 1, 128),
+        "SW2": (4, 128), "SW3": (2, 128), "RW2": (26, 4, 128),
         "RW3": (26, 2, 128), "RW3X": (18, 2, 128), "RW3Y": (18, 2, 128), "C3": (6, 16, 128),
         "A1": (14, 24, 128), "Q1": (14, 24, 128), "R2": (12, 24, 128), "PT": (12, 24, 128), "QT": (12, 24, 128),
         "G1": (14, 24, 128), "W1": (14, 24, 128), "V1": (14, 24, 128), "U1": (14, 24, 128),

time: 53.5 us -> 52.8 us (0.987)
  Pallas kernels: 52.7 us -> 51.6 us
    pallas_call x1, Pallas kernels: 52.7 us -> 51.6 us  [per_device(): pl.pallas_call(body, out_shape=jax.ShapeDtypeStruct((16, 16, 128), F32),...]
where the time goes in v5:
time: 52.8 us; the launch traced here: 52.3 us
  Pallas kernels  51.6 us (98%)
  other arithmetic  0.68 us (1%)
    pallas_call x1, Pallas kernels, per_device(): pl.pallas_call(body, out_shape=jax.ShapeDtypeStruct((16, 16, 128), F32),...  51.6 us

profile of v5, /device:TPU:14, one launch (start us, length us, event | category | flops | bytes accessed | tf_op | source)
XLA Modules:
  0.0 52.3 jit_solution(4164799640119510512)
XLA Ops:
  0.0 0.0 copy-start
  0.0 51.6 %vcycle.1 = f32[16,16,128]{2,1,0:T(8,128)S(1)} custom-call(f32[1,16,16,128]{3,2,1,0:T(8,128)} %args_0_.4, f32[16,16,128]{2,1,0:T(8,128)} %args_1_.4, f32[8,8192]{1,0:T(8,128)} %args_2_.4), custom_call_target="tpu_custom_call" | custom-call | tf_op jit(solution)/shard_map/vcycle/pallas_call | solution.py:873
  51.6 0.0 copy-done
  51.6 0.7 %divide_bitcast_fusion = f32[1,16,16,128]{3,2,1,0:T(8,128)} fusion(f32[16,16,128]{2,1,0:T(8,128)S(1)} %vcycle.1, f32[16,16,128]{2,1,0:T(8,128)S(1)} %copy-done), kind=kLoop, calls=%fused_computation | loop fusion | flops 32768 | bytes 393216 | tf_op jit(solution)/shard_map/broadcast_in_dim | solution.py:882
Async XLA Ops:
  0.0 51.6 %copy-start = (f32[16,16,128]{2,1,0:T(8,128)S(1)}, f32[16,16,128]{2,1,0:T(8,128)}, u32[]{:S(2)}) copy-start(f32[16,16,128]{2,1,0:T(8,128)} %args_1_.4) | copy-start | bytes 393220

commit v6 on v5

--- a/solution.py
+++ b/solution.py
@@ -13,11 +13,13 @@
 S = 0.8 / 6.0
 OFFS = [o for o in itertools.product((-1, 0, 1), repeat=3) if o != (0, 0, 0)]
 OFFS.sort(key=lambda o: (-abs(o[1]), -abs(o[2]), -abs(o[0])))
-OFF2X = [(2 * a, b, c) for a in (-1, 1) for b in (-1, 0, 1) for c in (-1, 0, 1)]
-OFF2Y = [(b, 2 * a, c) for a in (-1, 1) for b in (-1, 0, 1) for c in (-1, 0, 1)]
+OFF2X = [(2 * a, b, 0) for a in (-1, 1) for b in (-1, 0, 1)]
+OFF2Y = [(b, 2 * a, 0) for a in (-1, 1) for b in (-1, 0, 1)]
+FLAT = [o for o in OFFS if o[2] == 0]
 SLOT = {o: i for i, o in enumerate(OFFS)}
 ZOFFS = [o for o in OFFS if o[2] != 0]
 ZSLOT = {o: i for i, o in enumerate(ZOFFS)}
+ZY = [o for o in ZOFFS if o[1] != 0]
 XY = [(-1, -1), (-1, 1), (1, -1), (1, 1)]
 XZ = [(0, -1), (0, 1)] + XY
 
@@ -232,8 +234,17 @@
         return jnp.where(lane[0:2] < 64, roll(v[0], -32), roll(v[1], 32))
 
     SW2, SW3 = r["SW2"], r["SW3"]
-    SW2[...] = pack2(w2)
+    p2 = pack2(w2)
+    SW2[...] = p2
     SW3[...] = pack3(w3)
+    zp = jnp.zeros((4, 128), F32)
+    for h in range(2):
+        zp = jnp.where((lane4 >= 16 * h) & (lane4 < 16 * h + 8), roll(p2, -48 * h), zp)
+        zp = jnp.where((lane4 >= 16 * h + 8) & (lane4 < 16 * h + 16), roll(p2, -48 * h - 48), zp)
+    row4 = row[0:4]
+    SWZ = r["SWZ"]
+    SWZ[...] = sum(roll(jnp.sum(jnp.where(row4 == y, zp, 0.0), axis=0, keepdims=True), 32 * y) for y in range(4))
+
     def send_all(src, dst, key):
         return [round_of(key, [(o, src, dst.at[SLOT[neg(o)]]) for o in OFFS], first(dst))]
 
@@ -243,6 +254,11 @@
             acc = jnp.where((lane >= 16 * x) & (lane < 16 * x + 4), roll(own[x], 16 * x - 32), acc)
             acc = jnp.where((lane >= 16 * x + 4) & (lane < 16 * x + 8), roll(own[x], 16 * x + 4 - 92), acc)
         zs[...] = acc
+
+    def place(m0, c, l, h):
+        a = roll(m0, 32 if h == 0 else 96)
+        e = roll(c, 96 if h == 0 else 32)
+        return jnp.where((l >= 32) & (l < 96), a, e)
 
     s1w, ysw, zsw, yzw = r["S1w"], r["YS1w"], r["ZS1w"], r["YZ1w"]
     s1w[...] = w1
@@ -285,6 +301,7 @@
         ),
     ]
 
+    wait_z = round_of(28, [((0, 0, d), SW3, r["RW3"].at[1 - i]) for i, d in enumerate((-1, 1))], first(r["RW3"]))
     wait_w = [
         round_of(7, [((0, -1, 0), ysw.at[0], RY.at[1]), ((0, 1, 0), ysw.at[1], RY.at[0])], first(RY)),
         round_of(
@@ -300,10 +317,8 @@
             [((0, dy, dz), yzw.at[(dy + 1) // 2], RYZ.at[XY.index((-dy, -dz))]) for dy, dz in XY],
             first(RYZ),
         ),
-        round_of(5, [(o, SW2, r["RW2"].at[SLOT[neg(o)]]) for o in OFFS], first(r["RW2"])),
-        round_of(18, [(o, SW3, r["RW3"].at[SLOT[neg(o)]]) for o in OFFS], first(r["RW3"])),
-        round_of(25, [(o, SW3, r["RW3Y"].at[OFF2Y.index(neg(o))]) for o in OFF2Y], first(r["RW3Y"])),
-        round_of(24, [(o, SW3, r["RW3X"].at[OFF2X.index(neg(o))]) for o in OFF2X], first(r["RW3X"])),
+        round_of(5, [(o, SW2, r["RW2"].at[FLAT.index(neg(o))]) for o in FLAT], first(r["RW2"])),
+        round_of(17, [(o, SWZ, r["RWZ"].at[ZSLOT[neg(o)]]) for o in ZOFFS], first(r["RWZ"])),
         round_of(6, [((-1, 0, 0), s1w.at[pl.ds(0, 2)], RX.at[1]), ((1, 0, 0), s1w.at[pl.ds(6, 2)], RX.at[0])], first(RX)),
         round_of(9, [((dx, 0, dz), zsw, RZ.at[XZ.index((-dx, -dz))]) for dx, dz in XZ], first(RZ)),
     ]
@@ -331,27 +346,36 @@
     def send1(own, n, key):
         s1, ys, zs = r["S1" + n], r["YS1" + n], r["ZS1" + n]
         s1[...] = own
-        ys[0] = s1[:, 0:4, :]
-        ys[1] = s1[:, 4:8, :]
+        for q in range(4):
+            v = jnp.where(lane < 64, roll(own[2 * q], -32), roll(own[2 * q + 1], 32))
+            ys[0, q] = v[0:4]
+            ys[1, q] = v[4:8]
         pack_z1(own, zs)
-        rx, ry, rxy, rz = (r[name + n] for name in ("RX1", "RY1", "RXY1", "RZ1"))
+        zy = r["ZY1g"]
+        zy[0] = zs[0:4, :]
+        zy[1] = zs[4:8, :]
+        rx, ry, rxy, rz, rzy = (r[name + n] for name in ("RX1", "RY1", "RXY1", "RZ1", "RZY1"))
         return [
+            round_of(key + 1, [((0, -1, 0), ys.at[0], ry.at[1]), ((0, 1, 0), ys.at[1], ry.at[0])], first(ry)),
+            round_of(
+                key + 2,
+                [
+                    ((dx, dy, 0), ys.at[(dy + 1) // 2, 0 if dx < 0 else 3], rxy.at[XY.index((-dx, -dy))])
+                    for dx, dy in XY
+                ],
+                first(rxy),
+            ),
+            round_of(29, [(o, zy.at[(o[1] + 1) // 2], rzy.at[ZY.index(neg(o))]) for o in ZY], first(rzy)),
             round_of(
                 key,
                 [((-1, 0, 0), s1.at[pl.ds(0, 3)], rx.at[1]), ((1, 0, 0), s1.at[pl.ds(5, 3)], rx.at[0])],
                 first(rx),
             ),
-            round_of(key + 1, [((0, -1, 0), ys.at[0], ry.at[1]), ((0, 1, 0), ys.at[1], ry.at[0])], first(ry)),
-            round_of(
-                key + 2,
-                [
-                    ((dx, dy, 0), ys.at[(dy + 1) // 2, pl.ds(0 if dx < 0 else 5, 3)], rxy.at[XY.index((-dx, -dy))])
-                    for dx, dy in XY
-                ],
-                first(rxy),
-            ),
-            round_of(key + 3, [(o, zs, rz.at[ZSLOT[neg(o)]]) for o in ZOFFS], first(rz)),
+            round_of(key + 3, [((dx, 0, dz), zs, rz.at[XZ.index((-dx, -dz))]) for dx, dz in XZ], first(rz)),
         ]
+
+    def half(m, q):
+        return jnp.where((lane4 >= 32) & (lane4 < 96), roll(m, 32 if q == 0 else 96), 0.0)
 
     def recv1(own, n, key, dst):
         run(key)
@@ -363,13 +387,16 @@
                 elif dy == 0:
                     base = r["RX1" + n][(dx + 1) // 2, x if dx < 0 else x - 11]
                 elif dx == 0:
-                    base = r["RY1" + n][(dy + 1) // 2, x - 3]
+                    base = half(r["RY1" + n][(dy + 1) // 2, (x - 3) // 2], (x - 3) % 2)
+                elif x in (0, 13):
+                    base = jnp.zeros((4, 128), F32)
                 else:
-                    base = r["RXY1" + n][XY.index((dx, dy)), x if dx < 0 else x - 11]
+                    base = half(r["RXY1" + n][XY.index((dx, dy))], (x - 1 if dx < 0 else x - 11) % 2)
                 sx = x - 3 if dx == 0 else (x + 5 if dx < 0 else x - 11)
-                rows = slice(0, 8) if dy == 0 else (slice(4, 8) if dy < 0 else slice(0, 4))
-                lo = r["RZ1" + n][ZSLOT[(dx, dy, -1)], rows, :]
-                hi = r["RZ1" + n][ZSLOT[(dx, dy, 1)], rows, :]
+                if dy == 0:
+                    lo, hi = (r["RZ1" + n][XZ.index((dx, dz))] for dz in (-1, 1))
+                else:
+                    lo, hi = (r["RZY1" + n][ZY.index((dx, dy, dz))] for dz in (-1, 1))
                 ln = lane[0:8] if dy == 0 else lane4
                 v = keep(base, dx, dy, 0)
                 v = jnp.where((ln >= 28) & (ln < 32), keep(roll(lo, 28 - 16 * sx - 4), dx, dy, -1), v)
@@ -377,17 +404,20 @@
                 at = 8 if dy == 0 else (4 if dy < 0 else 16)
                 dst[x, at : at + (8 if dy == 0 else 4), :] = v
 
-    wait_w0 = [
-        round_of(
-            14,
-            [
-                ((-1, 0, 0), W0.at[pl.ds(2, 1), gsl], W0.at[pl.ds(18, 1), gsl]),
-                ((1, 0, 0), W0.at[pl.ds(17, 1), gsl], W0.at[pl.ds(1, 1), gsl]),
-            ],
-            lambda n: W0.at[pl.ds(0, n), gsl],
-        ),
-        round_of(15, [((0, d, 0), r["YW"].at[i], r["RYW"].at[1 - i]) for i, d in enumerate((-1, 1))], first(r["RYW"])),
-        round_of(16, [((0, 0, d), r["QW"], r["RQW"].at[1 - i]) for i, d in enumerate((-1, 1))], first(r["RQW"])),
+    wait_z()
+    l2, l1 = lane[0:2], lane[0:1]
+    ends3 = jnp.where((l2 // 32) % 2 == 1, keep(r["RW3"][0], 0, 0, -1), keep(r["RW3"][1], 0, 0, 1))
+    own3 = [place(SW3[...], ends3, l2, h) for h in range(2)]
+    XW3 = r["XW3"]
+    XW3[...] = jnp.where(
+        l1 % 4 < 2,
+        jnp.where(l1 % 4 == 0, own3[0][0:1], own3[0][1:2]),
+        jnp.where(l1 % 4 == 2, own3[1][0:1], own3[1][1:2]),
+    )
+    wait_w += [
+        round_of(18, [(o, XW3, r["RWF"].at[FLAT.index(neg(o))]) for o in FLAT], first(r["RWF"])),
+        round_of(25, [(o, XW3, r["RW3Y"].at[OFF2Y.index(neg(o))]) for o in OFF2Y], first(r["RW3Y"])),
+        round_of(24, [(o, XW3, r["RW3X"].at[OFF2X.index(neg(o))]) for o in OFF2X], first(r["RW3X"])),
     ]
 
     wi1 = 1.0 / jnp.where(own1, w1, 1.0)
@@ -478,11 +508,6 @@
     def spread(m0, lo, hi, l, dx, dy):
         return keep(m0, dx, dy, 0), jnp.where((l // 32) % 2 == 1, keep(lo, dx, dy, -1), keep(hi, dx, dy, 1))
 
-    def place(m0, c, l, h):
-        a = roll(m0, 32 if h == 0 else 96)
-        e = roll(c, 96 if h == 0 else 32)
-        return jnp.where((l >= 32) & (l < 96), a, e)
-
     def piece(buf, own, rows, o):
         return own[rows, :] if o == (0, 0, 0) else buf[SLOT[o], rows, :]
 
@@ -491,12 +516,15 @@
         for dx in (-1, 0, 1):
             for dy in (-1, 0, 1):
                 m0, c = spread(*[piece(buf, own, rows, (dx, dy, dz)) for dz in (0, -1, 1)], lane4, dx, dy)
-                for p in range(2):
-                    take = lane4 % 2 == p
-                    a = jnp.where(take, m0, roll(m0, 1 if p == 0 else -1))
-                    e = jnp.where(take, c, roll(c, 1 if p == 0 else -1))
-                    for h in range(2):
-                        dst[4 + 4 * dx + 2 * h + p, 8 + 4 * dy : 12 + 4 * dy, :] = place(a, e, lane4, h)
+                spread2(m0, c, dst, dx, dy)
+
+    def spread2(m0, c, dst, dx, dy):
+        for p in range(2):
+            take = lane4 % 2 == p
+            a = jnp.where(take, m0, roll(m0, 1 if p == 0 else -1))
+            e = jnp.where(take, c, roll(c, 1 if p == 0 else -1))
+            for h in range(2):
+                dst[4 + 4 * dx + 2 * h + p, 8 + 4 * dy : 12 + 4 * dy, :] = place(a, e, lane4, h)
 
     def unpack3(get, spots, dst):
         l = lane[0:2]
@@ -505,18 +533,34 @@
             for h in range(2):
                 dst[5 + 2 * dx + h, 12 + 2 * dy : 14 + 2 * dy, :] = place(m0, c, l, h)
 
-    unpack2(r["RW2"], SW2, W2)
-
-    def piece3(o):
-        if o == (0, 0, 0):
-            return SW3[...]
-        if abs(o[0]) == 2:
-            return r["RW3X"][OFF2X.index(o)]
-        if abs(o[1]) == 2:
-            return r["RW3Y"][OFF2Y.index(o)]
-        return r["RW3"][SLOT[o]]
-
-    unpack3(piece3, [(a, b) for a in range(-2, 3) for b in range(-2, 3) if abs(a) < 2 or abs(b) < 2], W3)
+    for dx in (-1, 0, 1):
+        for dy in (-1, 0, 1):
+            m0 = keep(SW2[...] if dx == dy == 0 else r["RW2"][FLAT.index((dx, dy, 0))], dx, dy, 0)
+            lo, hi = (keep(r["RWZ"][ZSLOT[(dx, dy, dz)]], dx, dy, dz) for dz in (-1, 1))
+            line = jnp.where(lane[0:1] % 16 >= 8, lo, hi)
+            e = jnp.zeros((4, 128), F32)
+            for y in range(4):
+                e = jnp.where(row4 == y, roll(line, -32 * y), e)
+            c = jnp.zeros((4, 128), F32)
+            for h in range(2):
+                c = jnp.where((lane4 >= 64 * h) & (lane4 < 64 * h + 8), roll(e, 48 * h), c)
+                c = jnp.where((lane4 >= 64 * h + 56) & (lane4 < 64 * h + 64), roll(e, 48 * h + 48), c)
+            spread2(m0, c, W2, dx, dy)
+
+    W3[5, 12:14, :] = own3[0]
+    W3[6, 12:14, :] = own3[1]
+    ST, SU = r["ST"], r["SU"]
+    spots = [(o, r[n], i) for n, offs in (("RWF", FLAT), ("RW3Y", OFF2Y), ("RW3X", OFF2X)) for i, o in enumerate(offs)]
+    for k, (o, buf, i) in enumerate(spots):
+        ST[k : k + 1, :] = keep(buf[i], *o)
+    for q in range(4):
+        t = roll(jnp.where(lax.broadcasted_iota(jnp.int32, (24, 128), 1) % 4 == q, ST[...], 0.0), -q)
+        t = t + roll(t, 1)
+        SU[q] = t + roll(t, 2)
+    for k, ((dx, dy, _), _, _) in enumerate(spots):
+        for q in range(4):
+            at = 12 + 2 * dy + q % 2
+            W3[5 + 2 * dx + q // 2, at : at + 1, :] = SU[q, k : k + 1, :]
 
     def inverse(w):
         return jnp.where(w > 0.0, 1.0 / jnp.where(w > 0.0, w, 1.0), 0.0)
@@ -592,6 +636,19 @@
     ga_at = ih * nx + ix
     to_group(21, SA, GA.at[ga_at], group_y)
 
+    wait_w0 = [
+        round_of(
+            14,
+            [
+                ((-1, 0, 0), W0.at[pl.ds(2, 1), gsl], W0.at[pl.ds(18, 1), gsl]),
+                ((1, 0, 0), W0.at[pl.ds(17, 1), gsl], W0.at[pl.ds(1, 1), gsl]),
+            ],
+            lambda n: W0.at[pl.ds(0, n), gsl],
+        ),
+        round_of(15, [((0, d, 0), r["YW"].at[i], r["RYW"].at[1 - i]) for i, d in enumerate((-1, 1))], first(r["RYW"])),
+        round_of(16, [((0, 0, d), r["QW"], r["RQW"].at[1 - i]) for i, d in enumerate((-1, 1))], first(r["RQW"])),
+    ]
+
     cp = r["CP"]
     loads[2].wait()
 
@@ -606,17 +663,6 @@
                     at = 8 * y
                     acc = jnp.where((lane >= at) & (lane < at + 8), roll(tile, at - 64 * q - 8 * z), acc)
             cp[x * nz + z] = acc
-
-    run(wait_w0)
-    W0[1:2, 8:24, :] = keep(W0[1:2, 8:24, :], -1, 0, 0)
-    W0[18:19, 8:24, :] = keep(W0[18:19, 8:24, :], 1, 0, 0)
-    W0[2:18, 7:8, :] = keep(r["RYW"][0], 0, -1, 0)
-    W0[2:18, 24:25, :] = keep(r["RYW"][1], 0, 1, 0)
-    for h in range(2):
-        sl = slice(8 * h, 8 * h + 8)
-        j = qj(lane)
-        v = jnp.where(j == 3, keep(r["RQW"][0, sl, :], 0, 0, -1), jnp.where(j == 2, keep(r["RQW"][1, sl, :], 0, 0, 1), 0.0))
-        r["WQ"][8 + 8 * h : 16 + 8 * h, :] = v
 
     from_group(21, GA, n_y - 1)
     GA[ga_at] = SA[...]
@@ -682,6 +728,17 @@
     SZ[0] = main
     SZ[1] = edge
     to_group(23, SZ, GC.at[iz], group_z)
+
+    run(wait_w0)
+    W0[1:2, 8:24, :] = keep(W0[1:2, 8:24, :], -1, 0, 0)
+    W0[18:19, 8:24, :] = keep(W0[18:19, 8:24, :], 1, 0, 0)
+    W0[2:18, 7:8, :] = keep(r["RYW"][0], 0, -1, 0)
+    W0[2:18, 24:25, :] = keep(r["RYW"][1], 0, 1, 0)
+    for h in range(2):
+        sl = slice(8 * h, 8 * h + 8)
+        j = qj(lane)
+        v = jnp.where(j == 3, keep(r["RQW"][0, sl, :], 0, 0, -1), jnp.where(j == 2, keep(r["RQW"][1, sl, :], 0, 0, 1), 0.0))
+        r["WQ"][8 + 8 * h : 16 + 8 * h, :] = v
 
     run(wait_c)
     unpack2(r["RC"], SC, G2)
@@ -825,8 +882,8 @@
         "QS": (16, 128), "QW": (16, 128), "RQ": (6, 16, 128), "QE": (2, 1, 128), "RQE": (4, 1, 128),
         "YW": (2, 16, 1, 128), "RYW": (2, 16, 1, 128), "RQW": (2, 16, 128),
         "C0": (8, 16, 128), "C1": (4, 8, 128), "C2": (4, 8, 128),
-        "SW2": (4, 128), "SW3": (2, 128), "RW2": (26, 4, 128),
-        "RW3": (26, 2, 128), "RW3X": (18, 2, 128), "RW3Y": (18, 2, 128), "C3": (6, 16, 128),
+        "SW2": (4, 128), "SW3": (2, 128), "SWZ": (1, 128), "RW2": (8, 4, 128), "RWZ": (18, 1, 128), "XW3": (1, 128),
+        "RW3": (2, 2, 128), "RWF": (8, 1, 128), "RW3X": (6, 1, 128), "RW3Y": (6, 1, 128), "ST": (24, 128), "SU": (4, 24, 128), "C3": (6, 16, 128),
         "A1": (14, 24, 128), "Q1": (14, 24, 128), "R2": (12, 24, 128), "PT": (12, 24, 128), "QT": (12, 24, 128),
         "G1": (14, 24, 128), "W1": (14, 24, 128), "V1": (14, 24, 128), "U1": (14, 24, 128),
         "G2": (12, 24, 128), "W2": (12, 24, 128), "V2": (12, 24, 128), "U2": (12, 24, 128),
@@ -841,12 +898,14 @@
     }
     n = "g"
     v["S1" + n] = (8, 8, 128)
-    v["YS1" + n] = (2, 8, 4, 128)
+    v["YS1" + n] = (2, 4, 4, 128)
     v["ZS1" + n] = (8, 128)
+    v["ZY1" + n] = (2, 4, 128)
     v["RX1" + n] = (2, 3, 8, 128)
-    v["RY1" + n] = (2, 8, 4, 128)
-    v["RXY1" + n] = (4, 3, 4, 128)
-    v["RZ1" + n] = (18, 8, 128)
+    v["RY1" + n] = (2, 4, 4, 128)
+    v["RXY1" + n] = (4, 4, 128)
+    v["RZ1" + n] = (6, 8, 128)
+    v["RZY1" + n] = (12, 4, 128)
     n = "w"
     v["S1" + n] = (8, 8, 128)
     v["YS1" + n] = (2, 8, 2, 128)
@@ -875,7 +934,7 @@
             out_shape=jax.ShapeDtypeStruct((16, 16, 128), F32),
             in_specs=[pl.BlockSpec(memory_space=pltpu.HBM)] * 3,
             out_specs=vmem,
-            scratch_shapes=[pltpu.VMEM(s, F32) for s in sizes.values()] + [pltpu.SemaphoreType.DMA((28,))] * 2 + [pltpu.SemaphoreType.DMA((3,))],
+            scratch_shapes=[pltpu.VMEM(s, F32) for s in sizes.values()] + [pltpu.SemaphoreType.DMA((30,))] * 2 + [pltpu.SemaphoreType.DMA((3,))],
             compiler_params=pltpu.CompilerParams(collective_id=0, has_side_effects=True, vmem_limit_bytes=24 * 2**20),
             name="vcycle",
         )(*[pltpu.with_memory_space_constraint(a, pltpu.HBM) for a in (sources, stiffness, coarse_inverse)])

time: 52.8 us -> 53.7 us (1.017)
  Pallas kernels: 51.6 us -> 52.9 us
    pallas_call x1, Pallas kernels: 51.6 us -> 52.9 us  [per_device(): pl.pallas_call(body, out_shape=jax.ShapeDtypeStruct((16, 16, 128), F32),...]
where the time goes in v6:
time: 53.7 us; the launch traced here: 53.6 us
  Pallas kernels  52.9 us (99%)
  other arithmetic  0.68 us (1%)
    pallas_call x1, Pallas kernels, per_device(): pl.pallas_call(body, out_shape=jax.ShapeDtypeStruct((16, 16, 128), F32),...  52.9 us

profile of v6, /device:TPU:14, one launch (start us, length us, event | category | flops | bytes accessed | tf_op | source)
XLA Modules:
  0.0 53.6 jit_solution(8946896248216437133)
XLA Ops:
  0.0 0.0 copy-start
  0.0 52.9 %vcycle.1 = f32[16,16,128]{2,1,0:T(8,128)S(1)} custom-call(f32[1,16,16,128]{3,2,1,0:T(8,128)} %args_0_.4, f32[16,16,128]{2,1,0:T(8,128)} %args_1_.4, f32[8,8192]{1,0:T(8,128)} %args_2_.4), custom_call_target="tpu_custom_call" | custom-call | tf_op jit(solution)/shard_map/vcycle/pallas_call | solution.py:932
  52.9 0.0 copy-done
  52.9 0.7 %divide_bitcast_fusion = f32[1,16,16,128]{3,2,1,0:T(8,128)} fusion(f32[16,16,128]{2,1,0:T(8,128)S(1)} %vcycle.1, f32[16,16,128]{2,1,0:T(8,128)S(1)} %copy-done), kind=kLoop, calls=%fused_computation | loop fusion | flops 32768 | bytes 393216 | tf_op jit(solution)/shard_map/broadcast_in_dim | solution.py:941
Async XLA Ops:
  0.0 52.9 %copy-start = (f32[16,16,128]{2,1,0:T(8,128)S(1)}, f32[16,16,128]{2,1,0:T(8,128)}, u32[]{:S(2)}) copy-start(f32[16,16,128]{2,1,0:T(8,128)} %args_1_.4) | copy-start | bytes 393220

commit v7 on v6

--- a/solution.py
+++ b/solution.py
@@ -301,7 +301,7 @@
         ),
     ]
 
-    wait_z = round_of(28, [((0, 0, d), SW3, r["RW3"].at[1 - i]) for i, d in enumerate((-1, 1))], first(r["RW3"]))
+    wait_z = round_of(24, [((0, 0, d), SW3, r["RW3"].at[1 - i]) for i, d in enumerate((-1, 1))], first(r["RW3"]))
     wait_w = [
         round_of(7, [((0, -1, 0), ysw.at[0], RY.at[1]), ((0, 1, 0), ysw.at[1], RY.at[0])], first(RY)),
         round_of(
@@ -365,7 +365,7 @@
                 ],
                 first(rxy),
             ),
-            round_of(29, [(o, zy.at[(o[1] + 1) // 2], rzy.at[ZY.index(neg(o))]) for o in ZY], first(rzy)),
+            round_of(25, [(o, zy.at[(o[1] + 1) // 2], rzy.at[ZY.index(neg(o))]) for o in ZY], first(rzy)),
             round_of(
                 key,
                 [((-1, 0, 0), s1.at[pl.ds(0, 3)], rx.at[1]), ((1, 0, 0), s1.at[pl.ds(5, 3)], rx.at[0])],
@@ -414,11 +414,8 @@
         jnp.where(l1 % 4 == 0, own3[0][0:1], own3[0][1:2]),
         jnp.where(l1 % 4 == 2, own3[1][0:1], own3[1][1:2]),
     )
-    wait_w += [
-        round_of(18, [(o, XW3, r["RWF"].at[FLAT.index(neg(o))]) for o in FLAT], first(r["RWF"])),
-        round_of(25, [(o, XW3, r["RW3Y"].at[OFF2Y.index(neg(o))]) for o in OFF2Y], first(r["RW3Y"])),
-        round_of(24, [(o, XW3, r["RW3X"].at[OFF2X.index(neg(o))]) for o in OFF2X], first(r["RW3X"])),
-    ]
+    FAR = FLAT + OFF2Y + OFF2X
+    wait_w3 = round_of(18, [(o, XW3, r["RWF"].at[FAR.index(neg(o))]) for o in FAR], first(r["RWF"]))
 
     wi1 = 1.0 / jnp.where(own1, w1, 1.0)
     wi2 = 1.0 / jnp.where(own1[0:4], w2, 1.0)
@@ -546,21 +543,6 @@
                 c = jnp.where((lane4 >= 64 * h) & (lane4 < 64 * h + 8), roll(e, 48 * h), c)
                 c = jnp.where((lane4 >= 64 * h + 56) & (lane4 < 64 * h + 64), roll(e, 48 * h + 48), c)
             spread2(m0, c, W2, dx, dy)
-
-    W3[5, 12:14, :] = own3[0]
-    W3[6, 12:14, :] = own3[1]
-    ST, SU = r["ST"], r["SU"]
-    spots = [(o, r[n], i) for n, offs in (("RWF", FLAT), ("RW3Y", OFF2Y), ("RW3X", OFF2X)) for i, o in enumerate(offs)]
-    for k, (o, buf, i) in enumerate(spots):
-        ST[k : k + 1, :] = keep(buf[i], *o)
-    for q in range(4):
-        t = roll(jnp.where(lax.broadcasted_iota(jnp.int32, (24, 128), 1) % 4 == q, ST[...], 0.0), -q)
-        t = t + roll(t, 1)
-        SU[q] = t + roll(t, 2)
-    for k, ((dx, dy, _), _, _) in enumerate(spots):
-        for q in range(4):
-            at = 12 + 2 * dy + q % 2
-            W3[5 + 2 * dx + q // 2, at : at + 1, :] = SU[q, k : k + 1, :]
 
     def inverse(w):
         return jnp.where(w > 0.0, 1.0 / jnp.where(w > 0.0, w, 1.0), 0.0)
@@ -605,6 +587,20 @@
     C3[...] = jnp.sum(R2[:, 4:20, :].reshape(6, 2, 16, 128), axis=1)
     t = C3[:, pl.ds(0, 6, stride=2), :] + C3[:, pl.ds(1, 6, stride=2), :]
     b3 = pair_z(t, 2) * 0.125
+    wait_w3()
+    W3[5, 12:14, :] = own3[0]
+    W3[6, 12:14, :] = own3[1]
+    ST, SU = r["ST"], r["SU"]
+    for k, o in enumerate(FAR):
+        ST[k : k + 1, :] = keep(r["RWF"][k], *o)
+    for q in range(4):
+        t = roll(jnp.where(lax.broadcasted_iota(jnp.int32, (24, 128), 1) % 4 == q, ST[...], 0.0), -q)
+        t = t + roll(t, 1)
+        SU[q] = t + roll(t, 2)
+    for k, (dx, dy, _) in enumerate(FAR):
+        for q in range(4):
+            at = 12 + 2 * dy + q % 2
+            W3[5 + 2 * dx + q // 2, at : at + 1, :] = SU[q, k : k + 1, :]
     P3[3:9, 10:16, :] = b3 * inverse(W3[3:9, 10:16, :])
     c, t = nsum(P3, 2, 8, 9, 8, 4)
     Q3[2:10, 9:17, :] = S * (1.2 * c + S * t) * rowmask(9, 8, 12, 14)
@@ -883,7 +879,7 @@
         "YW": (2, 16, 1, 128), "RYW": (2, 16, 1, 128), "RQW": (2, 16, 128),
         "C0": (8, 16, 128), "C1": (4, 8, 128), "C2": (4, 8, 128),
         "SW2": (4, 128), "SW3": (2, 128), "SWZ": (1, 128), "RW2": (8, 4, 128), "RWZ": (18, 1, 128), "XW3": (1, 128),
-        "RW3": (2, 2, 128), "RWF": (8, 1, 128), "RW3X": (6, 1, 128), "RW3Y": (6, 1, 128), "ST": (24, 128), "SU": (4, 24, 128), "C3": (6, 16, 128),
+        "RW3": (2, 2, 128), "RWF": (20, 1, 128), "ST": (24, 128), "SU": (4, 24, 128), "C3": (6, 16, 128),
         "A1": (14, 24, 128), "Q1": (14, 24, 128), "R2": (12, 24, 128), "PT": (12, 24, 128), "QT": (12, 24, 128),
         "G1": (14, 24, 128), "W1": (14, 24, 128), "V1": (14, 24, 128), "U1": (14, 24, 128),
         "G2": (12, 24, 128), "W2": (12, 24, 128), "V2": (12, 24, 128), "U2": (12, 24, 128),
@@ -934,7 +930,7 @@
             out_shape=jax.ShapeDtypeStruct((16, 16, 128), F32),
             in_specs=[pl.BlockSpec(memory_space=pltpu.HBM)] * 3,
             out_specs=vmem,
-            scratch_shapes=[pltpu.VMEM(s, F32) for s in sizes.values()] + [pltpu.SemaphoreType.DMA((30,))] * 2 + [pltpu.SemaphoreType.DMA((3,))],
+            scratch_shapes=[pltpu.VMEM(s, F32) for s in sizes.values()] + [pltpu.SemaphoreType.DMA((28,))] * 2 + [pltpu.SemaphoreType.DMA((3,))],
             compiler_params=pltpu.CompilerParams(collective_id=0, has_side_effects=True, vmem_limit_bytes=24 * 2**20),
             name="vcycle",
         )(*[pltpu.with_memory_space_constraint(a, pltpu.HBM) for a in (sources, stiffness, coarse_inverse)])

time: 53.7 us -> 53.3 us (level)
  no operation moved by 1% of the time
where the time goes in v7:
time: 53.3 us; the launch traced here: 53.1 us
  Pallas kernels  52.4 us (98%)
  other arithmetic  0.68 us (1%)
    pallas_call x1, Pallas kernels, per_device(): pl.pallas_call(body, out_shape=jax.ShapeDtypeStruct((16, 16, 128), F32),...  52.4 us

profile of v7, /device:TPU:14, one launch (start us, length us, event | category | flops | bytes accessed | tf_op | source)
XLA Modules:
  0.0 53.1 jit_solution(11933888618128323166)
XLA Ops:
  0.0 0.0 copy-start
  0.0 52.4 %vcycle.1 = f32[16,16,128]{2,1,0:T(8,128)S(1)} custom-call(f32[1,16,16,128]{3,2,1,0:T(8,128)} %args_0_.4, f32[16,16,128]{2,1,0:T(8,128)} %args_1_.4, f32[8,8192]{1,0:T(8,128)} %args_2_.4), custom_call_target="tpu_custom_call" | custom-call | tf_op jit(solution)/shard_map/vcycle/pallas_call | solution.py:928
  52.5 0.0 copy-done
  52.5 0.7 %divide_bitcast_fusion = f32[1,16,16,128]{3,2,1,0:T(8,128)} fusion(f32[16,16,128]{2,1,0:T(8,128)S(1)} %vcycle.1, f32[16,16,128]{2,1,0:T(8,128)S(1)} %copy-done), kind=kLoop, calls=%fused_computation | loop fusion | flops 32768 | bytes 393216 | tf_op jit(solution)/shard_map/broadcast_in_dim | solution.py:937
Async XLA Ops:
  0.0 52.5 %copy-start = (f32[16,16,128]{2,1,0:T(8,128)S(1)}, f32[16,16,128]{2,1,0:T(8,128)}, u32[]{:S(2)}) copy-start(f32[16,16,128]{2,1,0:T(8,128)} %args_1_.4) | copy-start | bytes 393220

commit v8 on v7

--- a/solution.py
+++ b/solution.py
@@ -13,8 +13,8 @@
 S = 0.8 / 6.0
 OFFS = [o for o in itertools.product((-1, 0, 1), repeat=3) if o != (0, 0, 0)]
 OFFS.sort(key=lambda o: (-abs(o[1]), -abs(o[2]), -abs(o[0])))
-OFF2X = [(2 * a, b, 0) for a in (-1, 1) for b in (-1, 0, 1)]
-OFF2Y = [(b, 2 * a, 0) for a in (-1, 1) for b in (-1, 0, 1)]
+OFF2X = [(2 * a, b, c) for a in (-1, 1) for b in (-1, 0, 1) for c in (-1, 0, 1)]
+OFF2Y = [(b, 2 * a, c) for a in (-1, 1) for b in (-1, 0, 1) for c in (-1, 0, 1)]
 FLAT = [o for o in OFFS if o[2] == 0]
 SLOT = {o: i for i, o in enumerate(OFFS)}
 ZOFFS = [o for o in OFFS if o[2] != 0]
@@ -254,11 +254,6 @@
             acc = jnp.where((lane >= 16 * x) & (lane < 16 * x + 4), roll(own[x], 16 * x - 32), acc)
             acc = jnp.where((lane >= 16 * x + 4) & (lane < 16 * x + 8), roll(own[x], 16 * x + 4 - 92), acc)
         zs[...] = acc
-
-    def place(m0, c, l, h):
-        a = roll(m0, 32 if h == 0 else 96)
-        e = roll(c, 96 if h == 0 else 32)
-        return jnp.where((l >= 32) & (l < 96), a, e)
 
     s1w, ysw, zsw, yzw = r["S1w"], r["YS1w"], r["ZS1w"], r["YZ1w"]
     s1w[...] = w1
@@ -301,7 +296,6 @@
         ),
     ]
 
-    wait_z = round_of(24, [((0, 0, d), SW3, r["RW3"].at[1 - i]) for i, d in enumerate((-1, 1))], first(r["RW3"]))
     wait_w = [
         round_of(7, [((0, -1, 0), ysw.at[0], RY.at[1]), ((0, 1, 0), ysw.at[1], RY.at[0])], first(RY)),
         round_of(
@@ -321,6 +315,11 @@
         round_of(17, [(o, SWZ, r["RWZ"].at[ZSLOT[neg(o)]]) for o in ZOFFS], first(r["RWZ"])),
         round_of(6, [((-1, 0, 0), s1w.at[pl.ds(0, 2)], RX.at[1]), ((1, 0, 0), s1w.at[pl.ds(6, 2)], RX.at[0])], first(RX)),
         round_of(9, [((dx, 0, dz), zsw, RZ.at[XZ.index((-dx, -dz))]) for dx, dz in XZ], first(RZ)),
+    ]
+    wait_w3 = [
+        round_of(18, [(o, SW3, r["RW3"].at[SLOT[neg(o)]]) for o in OFFS], first(r["RW3"])),
+        round_of(25, [(o, SW3, r["RW3Y"].at[OFF2Y.index(neg(o))]) for o in OFF2Y], first(r["RW3Y"])),
+        round_of(24, [(o, SW3, r["RW3X"].at[OFF2X.index(neg(o))]) for o in OFF2X], first(r["RW3X"])),
     ]
 
     def recv1w(dst):
@@ -365,7 +364,7 @@
                 ],
                 first(rxy),
             ),
-            round_of(25, [(o, zy.at[(o[1] + 1) // 2], rzy.at[ZY.index(neg(o))]) for o in ZY], first(rzy)),
+            round_of(28, [(o, zy.at[(o[1] + 1) // 2], rzy.at[ZY.index(neg(o))]) for o in ZY], first(rzy)),
             round_of(
                 key,
                 [((-1, 0, 0), s1.at[pl.ds(0, 3)], rx.at[1]), ((1, 0, 0), s1.at[pl.ds(5, 3)], rx.at[0])],
@@ -404,19 +403,6 @@
                 at = 8 if dy == 0 else (4 if dy < 0 else 16)
                 dst[x, at : at + (8 if dy == 0 else 4), :] = v
 
-    wait_z()
-    l2, l1 = lane[0:2], lane[0:1]
-    ends3 = jnp.where((l2 // 32) % 2 == 1, keep(r["RW3"][0], 0, 0, -1), keep(r["RW3"][1], 0, 0, 1))
-    own3 = [place(SW3[...], ends3, l2, h) for h in range(2)]
-    XW3 = r["XW3"]
-    XW3[...] = jnp.where(
-        l1 % 4 < 2,
-        jnp.where(l1 % 4 == 0, own3[0][0:1], own3[0][1:2]),
-        jnp.where(l1 % 4 == 2, own3[1][0:1], own3[1][1:2]),
-    )
-    FAR = FLAT + OFF2Y + OFF2X
-    wait_w3 = round_of(18, [(o, XW3, r["RWF"].at[FAR.index(neg(o))]) for o in FAR], first(r["RWF"]))
-
     wi1 = 1.0 / jnp.where(own1, w1, 1.0)
     wi2 = 1.0 / jnp.where(own1[0:4], w2, 1.0)
 
@@ -504,6 +490,11 @@
 
     def spread(m0, lo, hi, l, dx, dy):
         return keep(m0, dx, dy, 0), jnp.where((l // 32) % 2 == 1, keep(lo, dx, dy, -1), keep(hi, dx, dy, 1))
+
+    def place(m0, c, l, h):
+        a = roll(m0, 32 if h == 0 else 96)
+        e = roll(c, 96 if h == 0 else 32)
+        return jnp.where((l >= 32) & (l < 96), a, e)
 
     def piece(buf, own, rows, o):
         return own[rows, :] if o == (0, 0, 0) else buf[SLOT[o], rows, :]
@@ -587,20 +578,19 @@
     C3[...] = jnp.sum(R2[:, 4:20, :].reshape(6, 2, 16, 128), axis=1)
     t = C3[:, pl.ds(0, 6, stride=2), :] + C3[:, pl.ds(1, 6, stride=2), :]
     b3 = pair_z(t, 2) * 0.125
-    wait_w3()
-    W3[5, 12:14, :] = own3[0]
-    W3[6, 12:14, :] = own3[1]
-    ST, SU = r["ST"], r["SU"]
-    for k, o in enumerate(FAR):
-        ST[k : k + 1, :] = keep(r["RWF"][k], *o)
-    for q in range(4):
-        t = roll(jnp.where(lax.broadcasted_iota(jnp.int32, (24, 128), 1) % 4 == q, ST[...], 0.0), -q)
-        t = t + roll(t, 1)
-        SU[q] = t + roll(t, 2)
-    for k, (dx, dy, _) in enumerate(FAR):
-        for q in range(4):
-            at = 12 + 2 * dy + q % 2
-            W3[5 + 2 * dx + q // 2, at : at + 1, :] = SU[q, k : k + 1, :]
+    run(wait_w3)
+
+    def piece3(o):
+        if o == (0, 0, 0):
+            return SW3[...]
+        if abs(o[0]) == 2:
+            return r["RW3X"][OFF2X.index(o)]
+        if abs(o[1]) == 2:
+            return r["RW3Y"][OFF2Y.index(o)]
+        return r["RW3"][SLOT[o]]
+
+    unpack3(piece3, [(a, b) for a in range(-2, 3) for b in range(-2, 3) if abs(a) < 2 or abs(b) < 2], W3)
+
     P3[3:9, 10:16, :] = b3 * inverse(W3[3:9, 10:16, :])
     c, t = nsum(P3, 2, 8, 9, 8, 4)
     Q3[2:10, 9:17, :] = S * (1.2 * c + S * t) * rowmask(9, 8, 12, 14)
@@ -878,8 +868,8 @@
         "QS": (16, 128), "QW": (16, 128), "RQ": (6, 16, 128), "QE": (2, 1, 128), "RQE": (4, 1, 128),
         "YW": (2, 16, 1, 128), "RYW": (2, 16, 1, 128), "RQW": (2, 16, 128),
         "C0": (8, 16, 128), "C1": (4, 8, 128), "C2": (4, 8, 128),
-        "SW2": (4, 128), "SW3": (2, 128), "SWZ": (1, 128), "RW2": (8, 4, 128), "RWZ": (18, 1, 128), "XW3": (1, 128),
-        "RW3": (2, 2, 128), "RWF": (20, 1, 128), "ST": (24, 128), "SU": (4, 24, 128), "C3": (6, 16, 128),
+        "SW2": (4, 128), "SW3": (2, 128), "SWZ": (1, 128), "RW2": (8, 4, 128), "RWZ": (18, 1, 128),
+        "RW3": (26, 2, 128), "RW3X": (18, 2, 128), "RW3Y": (18, 2, 128), "C3": (6, 16, 128),
         "A1": (14, 24, 128), "Q1": (14, 24, 128), "R2": (12, 24, 128), "PT": (12, 24, 128), "QT": (12, 24, 128),
         "G1": (14, 24, 128), "W1": (14, 24, 128), "V1": (14, 24, 128), "U1": (14, 24, 128),
         "G2": (12, 24, 128), "W2": (12, 24, 128), "V2": (12, 24, 128), "U2": (12, 24, 128),
@@ -930,7 +920,7 @@
             out_shape=jax.ShapeDtypeStruct((16, 16, 128), F32),
             in_specs=[pl.BlockSpec(memory_space=pltpu.HBM)] * 3,
             out_specs=vmem,
-            scratch_shapes=[pltpu.VMEM(s, F32) for s in sizes.values()] + [pltpu.SemaphoreType.DMA((28,))] * 2 + [pltpu.SemaphoreType.DMA((3,))],
+            scratch_shapes=[pltpu.VMEM(s, F32) for s in sizes.values()] + [pltpu.SemaphoreType.DMA((29,))] * 2 + [pltpu.SemaphoreType.DMA((3,))],
             compiler_params=pltpu.CompilerParams(collective_id=0, has_side_effects=True, vmem_limit_bytes=24 * 2**20),
             name="vcycle",
         )(*[pltpu.with_memory_space_constraint(a, pltpu.HBM) for a in (sources, stiffness, coarse_inverse)])

time: 53.3 us -> 53.1 us (level); the launches traced: 53.1 us -> 52.3 us
  Pallas kernels: 52.4 us -> 51.6 us
    pallas_call x1, Pallas kernels: 52.4 us -> 51.6 us  [per_device(): pl.pallas_call(body, out_shape=jax.ShapeDtypeStruct((16, 16, 128), F32),...]
where the time goes in v8:
time: 53.1 us; the launch traced here: 52.3 us
  Pallas kernels  51.6 us (97%)
  other arithmetic  0.68 us (1%)
    pallas_call x1, Pallas kernels, per_device(): pl.pallas_call(body, out_shape=jax.ShapeDtypeStruct((16, 16, 128), F32),...  51.6 us

profile of v8, /device:TPU:14, one launch (start us, length us, event | category | flops | bytes accessed | tf_op | source)
XLA Modules:
  0.0 52.3 jit_solution(1791844028075154320)
XLA Ops:
  0.0 0.0 copy-start
  0.0 51.6 %vcycle.1 = f32[16,16,128]{2,1,0:T(8,128)S(1)} custom-call(f32[1,16,16,128]{3,2,1,0:T(8,128)} %args_0_.4, f32[16,16,128]{2,1,0:T(8,128)} %args_1_.4, f32[8,8192]{1,0:T(8,128)} %args_2_.4), custom_call_target="tpu_custom_call" | custom-call | tf_op jit(solution)/shard_map/vcycle/pallas_call | solution.py:918
  51.6 0.0 copy-done
  51.6 0.7 %divide_bitcast_fusion = f32[1,16,16,128]{3,2,1,0:T(8,128)} fusion(f32[16,16,128]{2,1,0:T(8,128)S(1)} %vcycle.1, f32[16,16,128]{2,1,0:T(8,128)S(1)} %copy-done), kind=kLoop, calls=%fused_computation | loop fusion | flops 32768 | bytes 393216 | tf_op jit(solution)/shard_map/broadcast_in_dim | solution.py:927
Async XLA Ops:
  0.0 51.6 %copy-start = (f32[16,16,128]{2,1,0:T(8,128)S(1)}, f32[16,16,128]{2,1,0:T(8,128)}, u32[]{:S(2)}) copy-start(f32[16,16,128]{2,1,0:T(8,128)} %args_1_.4) | copy-start | bytes 393220
